TPU v7x, 32 devices: a whole 2x2x4 slice. The times are simulated.
32 devices in a mesh: parts: 2 (over y), row: 8 (over z, core), col: 2 (over x), sub: 1.
Axes of the slice: x: 2, y: 2, z: 4, core: 2. Of those that a mesh axis runs over, the one named last changes fastest.
Arguments:
- pair: float32 [192, 96, 128], P(('parts', 'row'), ('col', 'sub')), parts along dimension 0, may hold values from -250 to 250, as said below
- residue_mask: int32 [192], P('parts'), parts along dimension 0, may hold values from 0 to 1, as said below
- tri_norm_gain: float32 [128], replicated, may hold values from 0.25 to 1.75
- tri_in_weight: bfloat16 [128, 4, 128], replicated, may hold values from -0.5 to 0.5
- tri_gate_weight: bfloat16 [128, 128], replicated, may hold values from -0.5 to 0.5
- tri_out_norm_gain: float32 [128], replicated, may hold values from 0.25 to 1.75
- tri_out_weight: bfloat16 [128, 128], replicated, may hold values from -0.5 to 0.5
- att_norm_gain: float32 [128], replicated, may hold values from 0.25 to 1.75
- att_proj_weight: bfloat16 [128, 4, 128], replicated, may hold values from -0.5 to 0.5
- att_bias_weight: bfloat16 [128, 4], replicated, may hold values from -15 to 15
- att_out_weight: bfloat16 [128, 128], replicated, may hold values from -0.5 to 0.5
Outputs:
- pair_out: float32 [192, 96, 128], P(('parts', 'row'), ('col', 'sub')), parts along dimension 0
There are 2 independent parts, one for each index of `parts`. A program takes and returns all parts, laid end to end along the dimension named above; an argument that names none is the same for every part. Nothing has to cross between parts.
Inputs may be any that keep to these rules, and one draw needn't show every extreme that they name: The pair entries are finite. `residue_mask`: 0 on every residue at or above a length of at least 48 and less than 96; below it 1, except some unresolved residues that are 0; residue 0 is always 1.
All inputs are finite; a program needn't handle non-finite values.
Results may differ from a plain program's by a relative error of at most 0.0032.
Values may be sent and summed in bfloat16 or wider, within the bound.
No kernel may reach another device: no remote copies, remote signals or barrier semaphores. Data moves between devices by JAX's collectives and lax.ppermute only.
A program may use at most 64 MiB of HBM per device.

v0:
```python
import math

import jax
import jax.numpy as jnp
from jax import lax
from jax.sharding import PartitionSpec as P

epsilon = 1e-05
mask_penalty = 1000000000.0


def norm_last(values_in, gain):
    center = jnp.mean(values_in, axis=-1, keepdims=True)
    centered = values_in - center
    variance = jnp.mean(centered * centered, axis=-1, keepdims=True)
    return centered * lax.rsqrt(variance + epsilon) * gain


def project(normed, weight):
    flat_rows = normed.reshape(-1, normed.shape[-1])
    product = jnp.dot(flat_rows, weight, preferred_element_type=jnp.float32)
    return product.reshape(normed.shape[:-1] + (weight.shape[1],))


def body(
    pair,
    residue_mask,
    tri_norm_gain,
    tri_in_weight,
    tri_gate_weight,
    tri_out_norm_gain,
    tri_out_weight,
    att_norm_gain,
    att_proj_weight,
    att_bias_weight,
    att_out_weight,
):
    rows_here, cols_here, chan_here = pair.shape
    residues = cols_here * lax.axis_size(("col", "sub"))
    row_offset = lax.axis_index("row") * rows_here
    col_offset = lax.axis_index(("col", "sub")) * cols_here
    residue_live = residue_mask.astype(jnp.float32)
    live_rows = lax.dynamic_slice_in_dim(residue_live, row_offset, rows_here)
    live_cols = lax.dynamic_slice_in_dim(residue_live, col_offset, cols_here)
    pair_live = (live_rows[:, None] * live_cols[None, :])[:, :, None]
    tri_normed = norm_last(pair, tri_norm_gain).astype(jnp.bfloat16)
    in_width = tri_in_weight.shape[2]
    projected = project(tri_normed, tri_in_weight.reshape(tri_in_weight.shape[0], -1)).reshape(
        rows_here, cols_here, 4, in_width
    )
    left_factor = (jax.nn.sigmoid(projected[:, :, 0]) * projected[:, :, 1] * pair_live).astype(
        jnp.bfloat16
    )
    right_factor = (jax.nn.sigmoid(projected[:, :, 2]) * projected[:, :, 3] * pair_live).astype(
        jnp.bfloat16
    )
    left_all, right_all = (
        lax.all_gather(left_factor, ("col", "sub"), axis=1, tiled=True),
        lax.all_gather(right_factor, ("col", "sub"), axis=1, tiled=True),
    )
    exchanged = lax.all_to_all(right_all, "row", split_axis=1, concat_axis=0, tiled=True)
    own_rows = lax.dynamic_slice_in_dim(exchanged, col_offset, cols_here, 0)
    tri_sum = jnp.einsum(
        "ikh,jkh->ijh",
        left_all,
        lax.all_gather(own_rows, "row", axis=1, tiled=True),
        preferred_element_type=jnp.float32,
    )
    hidden_normed = norm_last(tri_sum, tri_out_norm_gain).astype(jnp.bfloat16)
    tri_gate = jax.nn.sigmoid(project(tri_normed, tri_gate_weight))
    pair_mid = pair + tri_gate * project(hidden_normed, tri_out_weight)
    att_normed = norm_last(pair_mid, att_norm_gain).astype(jnp.bfloat16)
    head_width = att_proj_weight.shape[2]
    heads_here = att_bias_weight.shape[1]
    head_size = head_width // heads_here
    projected = project(att_normed, att_proj_weight.reshape(att_proj_weight.shape[0], -1)).reshape(
        rows_here, cols_here, 4, head_width
    )
    queries = (projected[:, :, 0] * head_size ** (-0.5)).astype(jnp.bfloat16)
    key_rows = projected[:, :, 1].astype(jnp.bfloat16)
    value_rows = projected[:, :, 2].astype(jnp.bfloat16)
    att_gate = jax.nn.sigmoid(projected[:, :, 3])
    pair_bias = project(att_normed, att_bias_weight).astype(jnp.bfloat16)
    key_all, value_all = (
        lax.all_gather(key_rows, ("col", "sub"), axis=1, tiled=True),
        lax.all_gather(value_rows, ("col", "sub"), axis=1, tiled=True),
    )
    bias_all_rows = lax.all_gather(pair_bias, "row", axis=0, tiled=True)
    bias_panel = lax.all_to_all(
        bias_all_rows, ("col", "sub"), split_axis=0, concat_axis=1, tiled=True
    )
    mask_row = (residue_live - 1.0) * mask_penalty
    head_bias = jnp.transpose(bias_panel.astype(jnp.float32), (2, 0, 1)) + mask_row[None, None, :]
    block_rows = math.gcd(rows_here, max(1, 512 // cols_here))
    blocks = rows_here // block_rows

    def attend(block_items):
        query_block, key_block, value_block = block_items
        scores = (
            jnp.einsum(
                "ijhd,ikhd->ihjk", query_block, key_block, preferred_element_type=jnp.float32
            )
            + head_bias[None]
        )
        row_max = jnp.max(scores, axis=-1, keepdims=True)
        raised = jnp.exp(scores - row_max)
        weights = (raised / jnp.sum(raised, axis=-1, keepdims=True)).astype(jnp.bfloat16)
        return jnp.einsum(
            "ihjk,ikhd->ijhd", weights, value_block, preferred_element_type=jnp.float32
        )

    attended = lax.map(
        attend,
        (
            queries.reshape(blocks, block_rows, cols_here, heads_here, head_size),
            key_all.reshape(blocks, block_rows, residues, heads_here, head_size),
            value_all.reshape(blocks, block_rows, residues, heads_here, head_size),
        ),
    )
    gated = (attended.reshape(rows_here, cols_here, head_width) * att_gate).astype(jnp.bfloat16)
    return pair_mid + project(gated, att_out_weight)


def solution(mesh):
    placed = (
        P(("parts", "row"), ("col", "sub"), None),
        P("parts"),
        P(),
        P(),
        P(),
        P(),
        P(),
        P(),
        P(),
        P(),
        P(),
    )
    return jax.shard_map(
        body,
        mesh=mesh,
        in_specs=placed,
        out_specs=P(("parts", "row"), ("col", "sub"), None),
        check_vma=False,
    )
```

profile of v0, /device:TPU:6, one launch (start us, length us, event | category | flops | bytes accessed | tf_op | source)
XLA Modules:
  0.0 122.8 jit_solution(9761063542724226572)
XLA Ops:
  6.6 0.7 convert_element_type.57
  7.3 0.1 dynamic_slice.21
  7.3 0.1 dynamic_slice.20
  7.4 1.1 reduce_sum.63
  8.5 1.2 %multiply_reduce_fusion.2 = f32[12,48]{1,0:T(8,128)S(1)} fusion(f32[12,48,128]{2,1,0:T(8,128)} %param.13, f32[12,48]{1,0:T(8,128)S(1)} %broadcast_multiply_fusion.3), kind=kLoop, calls=%fused_computation.62 | loop fusion | flops 220608 | bytes 299520 | tf_op jit(solution)/shard_map/reduce_sum | solution.py:15
  9.8 0.9 copy.78
  10.7 0.1 copy.43
  10.8 0.1 broadcast_multiply_fusion
  10.9 0.4 fusion.52
  11.3 0.2 fusion.34
  11.5 6.2 %all_gather.18 = bf16[12,96,128]{2,1,0:T(8,128)(2,1)S(1)} all-gather(bf16[12,48,128]{2,1,0:T(8,128)(2,1)S(1)} %get-tuple-element.57), channel_id=1, replica_groups=mesh['parts'=2,'row'=8,'col'=2,'sub'=1] {'col','sub'}, dimensions={1}, use_global_device_ids=true | all-gather | bytes 442368 | tf_op jit(solution)/shard_map/all_gather | solution.py:59
  17.7 0.1 copy.46
  17.9 17.2 %all_to_all.27 = bf16[12,96,128]{2,0,1:T(8,128)(2,1)S(1)} all-to-all(bf16[12,96,128]{2,0,1:T(8,128)(2,1)S(1)} %copy.46), channel_id=1, replica_groups=mesh['parts'=2,'row'=8,'col'=2,'sub'=1] {'row'}, dimensions={1} | all-to-all | bytes 589824 | tf_op jit(solution)/shard_map/all_to_all | solution.py:61
  35.1 0.1 all_to_all.23
  35.2 0.0 copy-start.12
  35.2 0.7 constant_dynamic-slice_fusion
  35.9 0.0 all-gather.4.cloned.1.call-update
  35.9 6.1 %all_gather.20 = bf16[12,96,128]{2,1,0:T(8,128)(2,1)S(1)} all-gather(bf16[12,48,128]{2,1,0:T(8,128)(2,1)S(1)} %get-tuple-element.56), channel_id=1, replica_groups=mesh['parts'=2,'row'=8,'col'=2,'sub'=1] {'col','sub'}, dimensions={1}, use_global_device_ids=true | all-gather | bytes 442368 | tf_op jit(solution)/shard_map/all_gather | solution.py:58
  42.0 1.2 copy.52
  43.2 0.8 copy.54
  44.0 1.1 fusion.23
  45.1 12.5 %all-gather.4.cloned.1.call-done = bf16[48,96,128]{2,0,1:T(8,128)(2,1)} async-done(((bf16[48,12,128]{2,0,1:T(8,128)(2,1)}), bf16[48,96,128]{2,0,1:T(8,128)(2,1)}) %all-gather.4.cloned.1.call-update) | async-done | bytes 1179664 | tf_op jit(solution)/shard_map/all_gather | solution.py:66
  57.6 5.3 %copy.51 = bf16[48,96,128]{0,1,2:T(8,128)(2,1)S(1)} copy(bf16[48,96,128]{2,0,1:T(8,128)(2,1)} %all-gather.4.cloned.1.call-done) | data formatting | bytes 2359296 | tf_op jit(solution)/shard_map/all_gather | solution.py:66
  62.9 2.0 %fusion.66 = (f32[12,48]{1,0:T(8,128)S(1)}, f32[12,48,128]{1,0,2:T(8,128)S(1)}) fusion(bf16[48,96,128]{0,1,2:T(8,128)(2,1)S(1)} %copy.51, bf16[12,96,128]{1,0,2:T(8,128)(2,1)} %copy.52), kind=kOutput, calls=%fused_computation.89 | convolution fusion | flops 14228928 | bytes 1771776 | tf_op jit(solution)/shard_map/ikh,jkh->ijh/dot_general | solution.py:63
  64.9 0.2 multiply_reduce_fusion
  65.1 0.2 multiply_convert_fusion
  65.4 0.5 copy-done.4
  65.9 0.3 fusion.67
  66.2 0.3 multiply_reduce_fusion.1
  66.6 0.0 copy-done.7
  66.6 0.3 convolution_convert_fusion
  66.9 13.9 %all_gather.23 = bf16[96,48,4]{1,2,0:T(4,128)(2,1)S(1)} all-gather(bf16[12,48,4]{1,2,0:T(4,128)(2,1)S(1)} %convolution_convert_fusion), channel_id=1, replica_groups=mesh['parts'=2,'row'=8,'col'=2,'sub'=1] {'row'}, dimensions={0}, use_global_device_ids=true | all-gather | bytes 41472 | tf_op jit(solution)/shard_map/all_gather | solution.py:88
  80.8 0.8 reshape.162
  81.6 4.4 %all-to-all-start.1 = ((bf16[2,2,4608]{2,1,0:T(2,128)(2,1)}), bf16[2,2,4608]{2,1,0:T(2,128)(2,1)}, u32[]{:S(2)}, u32[]{:S(2)}) async-start(bf16[2,2,4608]{2,1,0:T(2,128)(2,1)} %reshape.162), calls=%async_computation.1 | async-start | bytes 73728 | tf_op jit(solution)/shard_map/all_to_all | solution.py:89
  86.0 0.4 fusion.68
  86.4 6.5 %all-gather = bf16[12,96,1,128]{3,1,2,0:T(8,128)(2,1)S(1)} all-gather(bf16[12,48,1,128]{3,1,2,0:T(8,128)(2,1)S(1)} %get-tuple-element.59), channel_id=2, replica_groups=mesh['parts'=2,'row'=8,'col'=2,'sub'=1] {'col','sub'}, dimensions={1}, use_global_device_ids=true | all-gather | bytes 442368 | tf_op jit(solution)/shard_map/all_gather | solution.py:86
  92.9 5.8 %all-gather.1 = bf16[12,96,1,128]{3,1,2,0:T(8,128)(2,1)S(1)} all-gather(bf16[12,48,1,128]{3,1,2,0:T(8,128)(2,1)S(1)} %get-tuple-element.58), channel_id=3, replica_groups=mesh['parts'=2,'row'=8,'col'=2,'sub'=1] {'col','sub'}, dimensions={1}, use_global_device_ids=true | all-gather | bytes 442368 | tf_op jit(solution)/shard_map/all_gather | solution.py:85
  98.8 0.9 copy.55
  99.7 0.2 copy.57
  99.9 0.2 copy.56
  100.2 0.9 reshape.163
  101.1 0.2 copy.58
  101.3 0.2 reshape.148
  101.5 13.3 %while.10 = (s32[]{:T(128)}, f32[6,2,48,4,32]{2,4,3,1,0:T(8,128)S(1)}, bf16[6,2,96,4,32]{2,4,3,1,0:T(8,128)(2,1)}, bf16[6,2,48,4,32]{2,4,3,1,0:T(8,128)(2,1)S(1)...) while((s32[]{:T(128)}, f32[6,2,48,4,32]{2,4,3,1,0:T(8,128)S(1)}, ...), condition=%wide.region_9.10_spmd, body=%wide.region_6.9_spmd.sunk | while | flops 7336512 | bytes 1204813 | solution.py:112
  101.5 0.2 convolution_add_fusion.3
  101.7 0.4 fusion.88
  102.1 1.6 %fusion.89 = f32[6,2,48,4,32]{2,4,3,1,0:T(8,128)S(1)} fusion(f32[6,2,48,4,32]{2,4,3,1,0:T(8,128)S(1)} %get-tuple-element.111, s32[]{:T(128)} %get-tuple-element.110, f32[2,4,48]{2,1,0:T(4,128)S(1)} %fusion.88, bf16[6,2,96,4,32]{2,4,3,1,0:T(8,128)(2,1)} %get-tuple-element.119, f32[2,4,48,96]{3,2,1,0:T(8,128)S(1)} %convolution_add_fusion.3), kind=kOutput, calls=%fused_computation.5.clone.1 | convolution fusion | flops 2470367 | bytes 594944 | tf_op jit(solution)/shard_map/while/body/eval_jaxpr/ihjk,ikhd->ijhd/dot_general | solution.py:108
  103.7 0.2 convolution_add_fusion.3
  103.9 0.4 fusion.88
  104.3 1.6 %fusion.89 = f32[6,2,48,4,32]{2,4,3,1,0:T(8,128)S(1)} fusion(f32[6,2,48,4,32]{2,4,3,1,0:T(8,128)S(1)} %get-tuple-element.111, s32[]{:T(128)} %get-tuple-element.110, f32[2,4,48]{2,1,0:T(4,128)S(1)} %fusion.88, bf16[6,2,96,4,32]{2,4,3,1,0:T(8,128)(2,1)} %get-tuple-element.119, f32[2,4,48,96]{3,2,1,0:T(8,128)S(1)} %convolution_add_fusion.3), kind=kOutput, calls=%fused_computation.5.clone.1 | convolution fusion | flops 2470367 | bytes 594944 | tf_op jit(solution)/shard_map/while/body/eval_jaxpr/ihjk,ikhd->ijhd/dot_general | solution.py:108
  105.9 0.2 convolution_add_fusion.3
  106.1 0.4 fusion.88
  106.6 1.6 %fusion.89 = f32[6,2,48,4,32]{2,4,3,1,0:T(8,128)S(1)} fusion(f32[6,2,48,4,32]{2,4,3,1,0:T(8,128)S(1)} %get-tuple-element.111, s32[]{:T(128)} %get-tuple-element.110, f32[2,4,48]{2,1,0:T(4,128)S(1)} %fusion.88, bf16[6,2,96,4,32]{2,4,3,1,0:T(8,128)(2,1)} %get-tuple-element.119, f32[2,4,48,96]{3,2,1,0:T(8,128)S(1)} %convolution_add_fusion.3), kind=kOutput, calls=%fused_computation.5.clone.1 | convolution fusion | flops 2470367 | bytes 594944 | tf_op jit(solution)/shard_map/while/body/eval_jaxpr/ihjk,ikhd->ijhd/dot_general | solution.py:108
  108.1 0.2 convolution_add_fusion.3
  108.4 0.4 fusion.88
  108.8 1.6 %fusion.89 = f32[6,2,48,4,32]{2,4,3,1,0:T(8,128)S(1)} fusion(f32[6,2,48,4,32]{2,4,3,1,0:T(8,128)S(1)} %get-tuple-element.111, s32[]{:T(128)} %get-tuple-element.110, f32[2,4,48]{2,1,0:T(4,128)S(1)} %fusion.88, bf16[6,2,96,4,32]{2,4,3,1,0:T(8,128)(2,1)} %get-tuple-element.119, f32[2,4,48,96]{3,2,1,0:T(8,128)S(1)} %convolution_add_fusion.3), kind=kOutput, calls=%fused_computation.5.clone.1 | convolution fusion | flops 2470367 | bytes 594944 | tf_op jit(solution)/shard_map/while/body/eval_jaxpr/ihjk,ikhd->ijhd/dot_general | solution.py:108
  110.3 0.2 convolution_add_fusion.3
  110.6 0.4 fusion.88
  111.0 1.6 %fusion.89 = f32[6,2,48,4,32]{2,4,3,1,0:T(8,128)S(1)} fusion(f32[6,2,48,4,32]{2,4,3,1,0:T(8,128)S(1)} %get-tuple-element.111, s32[]{:T(128)} %get-tuple-element.110, f32[2,4,48]{2,1,0:T(4,128)S(1)} %fusion.88, bf16[6,2,96,4,32]{2,4,3,1,0:T(8,128)(2,1)} %get-tuple-element.119, f32[2,4,48,96]{3,2,1,0:T(8,128)S(1)} %convolution_add_fusion.3), kind=kOutput, calls=%fused_computation.5.clone.1 | convolution fusion | flops 2470367 | bytes 594944 | tf_op jit(solution)/shard_map/while/body/eval_jaxpr/ihjk,ikhd->ijhd/dot_general | solution.py:108
  112.5 0.2 convolution_add_fusion.3
  112.8 0.4 fusion.88
  113.2 1.6 %fusion.89 = f32[6,2,48,4,32]{2,4,3,1,0:T(8,128)S(1)} fusion(f32[6,2,48,4,32]{2,4,3,1,0:T(8,128)S(1)} %get-tuple-element.111, s32[]{:T(128)} %get-tuple-element.110, f32[2,4,48]{2,1,0:T(4,128)S(1)} %fusion.88, bf16[6,2,96,4,32]{2,4,3,1,0:T(8,128)(2,1)} %get-tuple-element.119, f32[2,4,48,96]{3,2,1,0:T(8,128)S(1)} %convolution_add_fusion.3), kind=kOutput, calls=%fused_computation.5.clone.1 | convolution fusion | flops 2470367 | bytes 594944 | tf_op jit(solution)/shard_map/while/body/eval_jaxpr/ihjk,ikhd->ijhd/dot_general | solution.py:108
  114.8 0.2 copy.60
  115.0 0.9 convolution_add_fusion.1
  (39 shorter events, 0.2 us)
Async XLA Ops:
  6.5 58.8 %copy-start = (bf16[128,128]{1,0:T(8,128)(2,1)S(1)}, bf16[128,128]{1,0:T(8,128)(2,1)}, u32[]{:S(2)}) copy-start(bf16[128,128]{1,0:T(8,128)(2,1)} %param.19) | copy-start | bytes 98308
  6.5 4.4 %copy-start.1 = (f32[12,48,128]{2,1,0:T(8,128)S(1)}, f32[12,48,128]{2,1,0:T(8,128)}, u32[]{:S(2)}) copy-start(f32[12,48,128]{2,1,0:T(8,128)} %param.13) | copy-start | bytes 884740
  6.5 4.4 %copy-start.8 = (f32[128]{0:T(128)S(1)}, f32[128]{0:T(128)}, u32[]{:S(2)}) copy-start(f32[128]{0:T(128)} %param.15) | copy-start | bytes 1540
  6.5 51.1 %all-gather.4.cloned.1.call-start = ((), (), s32[]{:S(2)}) async-start(), calls=%async_computation.2 | async-start | bytes 1327104 | tf_op jit(solution)/shard_map/all_gather | solution.py:66
  35.1 8.1 %copy-start.5 = (bf16[128,4,128]{2,1,0:T(4,128)(2,1)S(1)}, bf16[128,4,128]{2,1,0:T(4,128)(2,1)}, u32[]{:S(2)}) copy-start(bf16[128,4,128]{2,1,0:T(4,128)(2,1)} %param.21) | copy-start | bytes 393220
  35.2 8.8 %copy-start.12 = (s32[96]{0:T(128)S(1)}, s32[96]{0:T(128)}, u32[]{:S(2)}) copy-start(s32[96]{0:T(128)} %param.14) | copy-start | bytes 1156
  35.2 8.8 %copy-start.10 = (bf16[128,128]{1,0:T(8,128)(2,1)S(1)}, bf16[128,128]{1,0:T(8,128)(2,1)}, u32[]{:S(2)}) copy-start(bf16[128,128]{1,0:T(8,128)(2,1)} %param.17) | copy-start | bytes 98308
  62.9 2.2 %copy-start.9 = (f32[128]{0:T(128)S(1)}, f32[128]{0:T(128)}, u32[]{:S(2)}) copy-start(f32[128]{0:T(128)} %param.18) | copy-start | bytes 1540
  64.9 1.0 copy-start.4
  65.9 0.7 copy-start.6
  65.9 0.7 copy-start.7
  65.9 20.1 %copy-start.3 = (bf16[512,128]{1,0:T(8,128)(2,1)S(1)}, bf16[512,128]{1,0:T(8,128)(2,1)}, u32[]{:S(2)}) copy-start(bf16[512,128]{1,0:T(8,128)(2,1)} %copy.54) | copy-start | bytes 393220
  81.6 18.6 %all-to-all-start.1 = ((bf16[2,2,4608]{2,1,0:T(2,128)(2,1)}), bf16[2,2,4608]{2,1,0:T(2,128)(2,1)}, u32[]{:S(2)}, u32[]{:S(2)}) async-start(bf16[2,2,4608]{2,1,0:T(2,128)(2,1)} %reshape.162), calls=%async_computation.1 | async-start | bytes 73728 | tf_op jit(solution)/shard_map/all_to_all | solution.py:89
  99.7 1.8 %copy-start.2 = (f32[6,2,48,4,32]{2,4,3,1,0:T(8,128)S(1)}, f32[6,2,48,4,32]{2,4,3,1,0:T(8,128)}, u32[]{:S(2)}) copy-start(f32[6,2,48,4,32]{2,4,3,1,0:T(8,128)} %custom-call) | copy-start | bytes 884740
  101.4 13.6 %copy-start.11 = (bf16[128,128]{1,0:T(8,128)(2,1)S(1)}, bf16[128,128]{1,0:T(8,128)(2,1)}, u32[]{:S(2)}) copy-start(bf16[128,128]{1,0:T(8,128)(2,1)} %param.23) | copy-start | bytes 98308
Sparse Core Ops, SparseCore 0:
  36.1 21.5 all-gather.3
where the time goes:
time: 125 us; the launch traced here: 123 us
  blocking collectives  55.7 us (45%)
  matrix products  18.6 us (15%)
  between operations  13.7 us (11%)
  local copies, waits for them, and re-layouts  13.6 us (11%)
  waiting for transfers between devices  12.6 us (10%)
  starting transfers between devices  4.42 us (4%)
  other arithmetic  4.1 us (3%)
    all_to_all x1, blocking collectives, body(): lax.all_to_all(right_all, 'row', split_axis=1, concat_axis=0, tiled=True)  17.2 us
    all_gather x1, blocking collectives, body(): bias_all_rows = lax.all_gather(pair_bias, 'row', axis=0, tiled=True)  13.9 us
    all_gather x1, waiting for transfers between devices, body(): lax.all_gather(own_rows, 'row', axis=1, tiled=True)  12.5 us
    dot_general x6, matrix products, attend(): jnp.einsum('ihjk,ikhd->ijhd', weights, value_block, preferred_element_typ...  9.36 us
    all_gather x1, blocking collectives, body(): lax.all_gather(value_rows, ('col', 'sub'), axis=1, tiled=True)  6.48 us
    all_gather x1, blocking collectives, body(): lax.all_gather(right_factor, ('col', 'sub'), axis=1, tiled=True)  6.25 us
    all_gather x1, blocking collectives, body(): lax.all_gather(left_factor, ('col', 'sub'), axis=1, tiled=True)  6.06 us
    all_gather x1, blocking collectives, body(): lax.all_gather(key_rows, ('col', 'sub'), axis=1, tiled=True)  5.81 us
  transfers between devices with their start and end apart: 2, of which 1 were waited for; matrix products, arithmetic and copies ran while one was open for 4% of the time, Pallas kernels for 0%

commit v1 on v0

--- a/solution.py
+++ b/solution.py
@@ -1,12 +1,18 @@
+import functools
 import math
 
 import jax
 import jax.numpy as jnp
 from jax import lax
+from jax.experimental import pallas as pl
+from jax.experimental.pallas import tpu as pltpu
 from jax.sharding import PartitionSpec as P
 
 epsilon = 1e-05
 mask_penalty = 1000000000.0
+LANES = 128
+f32 = jnp.float32
+bf16 = jnp.bfloat16
 
 
 def norm_last(values_in, gain):
@@ -16,13 +22,17 @@
     return centered * lax.rsqrt(variance + epsilon) * gain
 
 
+def sigmoid(v):
+    return 0.5 * jnp.tanh(0.5 * v) + 0.5
+
+
 def project(normed, weight):
     flat_rows = normed.reshape(-1, normed.shape[-1])
     product = jnp.dot(flat_rows, weight, preferred_element_type=jnp.float32)
     return product.reshape(normed.shape[:-1] + (weight.shape[1],))
 
 
-def body(
+def body_general(
     pair,
     residue_mask,
     tri_norm_gain,
@@ -121,6 +131,320 @@
     return pair_mid + project(gated, att_out_weight)
 
 
+def dot_nn(a, b):
+    return lax.dot_general(a, b, (((1,), (0,)), ((), ())), preferred_element_type=f32)
+
+
+def dot_nt(a, b):
+    return lax.dot_general(a, b, (((1,), (1,)), ((), ())), preferred_element_type=f32)
+
+
+def split_weight(w_ref, w_scratch):
+    w_scratch[...] = w_ref[...].astype(f32)
+    return [w_scratch[:, p, :] for p in range(w_ref.shape[1])]
+
+
+def factors_kernel(devices, pair_ref, gain_ref, w_ref, lr_ref, normed_ref, w_scratch):
+    cells, chan = pair_ref.shape
+    hidden = w_ref.shape[2]
+    own = hidden // devices
+    normed = norm_last(pair_ref[...], gain_ref[...]).astype(bf16)
+    normed_ref[...] = normed
+    w_t = [jnp.transpose(w).astype(bf16) for w in split_weight(w_ref, w_scratch)]
+    spare = (-cells) % LANES
+    tiles = (cells + spare) // LANES
+    if spare:
+        tail = normed[:spare]
+        rhs_left = jnp.concatenate([normed, tail], axis=0)
+        rhs_right = jnp.concatenate([tail, normed], axis=0)
+    else:
+        rhs_left = rhs_right = normed
+    left = sigmoid(dot_nt(w_t[0], rhs_left)) * dot_nt(w_t[1], rhs_left)
+    right = sigmoid(dot_nt(w_t[2], rhs_right)) * dot_nt(w_t[3], rhs_right)
+    panels = [left[:, t * LANES : (t + 1) * LANES] for t in range(tiles)]
+    right_panels = [right[:, t * LANES : (t + 1) * LANES] for t in range(tiles)]
+    if spare:
+        lane = lax.broadcasted_iota(jnp.int32, (hidden, LANES), 1)
+        panels[-1] = jnp.where(lane < LANES - spare, panels[-1], right_panels[0])
+        panels += right_panels[1:]
+    else:
+        panels += right_panels
+    for t, panel in enumerate(panels):
+        lr_ref[:, t] = panel.reshape(devices, own, LANES).astype(bf16)
+
+
+def segment(panels, start, target):
+    tile, at = divmod(start, LANES)
+    here = panels[tile]
+    if at and tile + 1 < len(panels):
+        lane = lax.broadcasted_iota(jnp.int32, here.shape, 1)
+        here = jnp.where(lane >= at, here, panels[tile + 1])
+    shift = (target - at) % LANES
+    return pltpu.roll(here, shift, 1) if shift else here
+
+
+def triangle_kernel(
+    rows_here, cols_here, live_ref, lr_ref, sum_ref, left_scratch, right_scratch, sum_scratch
+):
+    devices, panels_in, own, _ = lr_ref.shape
+    residues = live_ref.shape[1]
+    cols = residues // cols_here
+    rows = residues // rows_here
+    cells = rows_here * cols_here
+    lane = lax.broadcasted_iota(jnp.int32, (own, LANES), 1)
+    for r in range(rows):
+        parts = [
+            [lr_ref[r * cols + c, t].astype(f32) for t in range(panels_in)] for c in range(cols)
+        ]
+        for side, scratch in ((0, left_scratch), (1, right_scratch)):
+            for i in range(rows_here):
+                start = side * cells + i * cols_here
+                line = segment(parts[0], start, 0)
+                for c in range(1, cols):
+                    moved = segment(parts[c], start, c * cols_here)
+                    line = jnp.where(lane < c * cols_here, line, moved)
+                scratch[r * rows_here + i] = line
+    live = live_ref[...].astype(f32)
+    live_wide = jnp.concatenate([live, jnp.zeros((1, LANES - residues), f32)], axis=1)
+    live_square = jnp.broadcast_to(live_wide, (LANES, LANES))
+    both = live_square * jnp.transpose(live_square)
+    both = both[:residues]
+    keep = live_wide > 0
+    for h in range(own):
+        left = jnp.where(keep, left_scratch[:, h, :], 0.0).astype(bf16)
+        right = jnp.where(keep, right_scratch[:, h, :], 0.0).astype(bf16)
+        right = jnp.concatenate([right, jnp.zeros((LANES - residues, LANES), bf16)], axis=0)
+        sum_scratch[:, h, :] = dot_nt(left, right) * both
+    tiles = sum_ref.shape[1]
+    for r in range(rows):
+        lines = [sum_scratch[r * rows_here + i] for i in range(rows_here)]
+        for c in range(cols):
+            for t in range(tiles):
+                panel = None
+                for i in range(rows_here):
+                    low, high = i * cols_here - t * LANES, (i + 1) * cols_here - t * LANES
+                    if high <= 0 or low >= LANES:
+                        continue
+                    shift = (low - c * cols_here) % LANES
+                    line = pltpu.roll(lines[i], shift, 1) if shift else lines[i]
+                    panel = line if panel is None else jnp.where(lane >= low, line, panel)
+                sum_ref[r * cols + c, t] = panel.astype(bf16)
+
+
+def middle_kernel(
+    pair_ref,
+    normed_ref,
+    sum_ref,
+    out_gain_ref,
+    out_w_ref,
+    gate_w_ref,
+    att_gain_ref,
+    bias_w_ref,
+    mid_ref,
+    att_ref,
+    bias_ref,
+):
+    devices, tiles, own, _ = sum_ref.shape
+    cells, chan = pair_ref.shape
+    hidden = devices * own
+    gain_col = jnp.transpose(jnp.broadcast_to(out_gain_ref[...], (LANES, hidden)))
+    gate = sigmoid(dot_nn(normed_ref[...], gate_w_ref[...]))
+    bias_w = jnp.transpose(bias_w_ref[...].astype(f32)).astype(bf16)
+    for t in range(tiles):
+        total = sum_ref[:, t].astype(f32).reshape(hidden, LANES)
+        center = jnp.mean(total, axis=0, keepdims=True)
+        centered = total - center
+        variance = jnp.mean(centered * centered, axis=0, keepdims=True)
+        hidden_normed = centered * lax.rsqrt(variance + epsilon) * gain_col
+        hidden_rows = jnp.transpose(hidden_normed).astype(bf16)
+        low, high = t * LANES, min((t + 1) * LANES, cells)
+        update = dot_nn(hidden_rows[: high - low], out_w_ref[...])
+        mid = pair_ref[low:high] + gate[low:high] * update
+        mid_ref[low:high] = mid
+        att = norm_last(mid, att_gain_ref[...]).astype(bf16)
+        att_ref[low:high] = att
+        bias_ref[:, low:high] = dot_nt(bias_w, att).astype(bf16)
+
+
+def attention_kernel(
+    rows_here,
+    place_ref,
+    live_ref,
+    bias_a_ref,
+    bias_b_ref,
+    att_ref,
+    att_far_ref,
+    mid_ref,
+    proj_w_ref,
+    out_w_ref,
+    out_ref,
+    w_scratch,
+    bias_scratch,
+):
+    cells, chan = att_ref.shape
+    cols_here = cells // rows_here
+    blocks, heads, _ = bias_a_ref.shape
+    residues = live_ref.shape[1]
+    width = proj_w_ref.shape[2]
+    size = width // heads
+    block_at, col, same = place_ref[0], place_ref[1], place_ref[2]
+    lane_row = lax.broadcasted_iota(jnp.int32, (1, LANES), 1)
+    live = live_ref[...].astype(f32)
+    live_wide = jnp.concatenate([live, jnp.zeros((1, LANES - residues), f32)], axis=1)
+    swapped = jnp.where(
+        lane_row < cols_here,
+        pltpu.roll(live_wide, LANES - cols_here, 1),
+        pltpu.roll(live_wide, cols_here, 1),
+    )
+    live_order = jnp.where(col == 0, live_wide, swapped)
+    penalty = (live_order - 1.0) * mask_penalty
+    lane = lax.broadcasted_iota(jnp.int32, (heads, LANES), 1)
+    pad = (-cells) % LANES
+
+    def panels(v):
+        v = v.astype(f32)
+        v = jnp.concatenate([v, jnp.zeros((heads, pad), f32)], axis=1) if pad else v
+        return [v[:, t * LANES : (t + 1) * LANES] for t in range((cells + pad) // LANES)]
+
+    for m in range(blocks):
+        first, second = bias_a_ref[m].astype(f32), bias_b_ref[m].astype(f32)
+        near = panels(jnp.where(same == 1, first, second))
+        far = panels(jnp.where(same == 1, second, first))
+        base = jnp.bitwise_xor(block_at, m) * rows_here
+        for j in range(rows_here):
+            line = jnp.where(
+                lane < cols_here,
+                segment(near, j * cols_here, 0),
+                segment(far, j * cols_here, cols_here),
+            )
+            bias_scratch[base + j] = line
+    penalty = penalty[:, :residues]
+    head_bias = [bias_scratch[:, h, :][:, :residues] + penalty for h in range(heads)]
+    head_bias = jnp.concatenate(head_bias, axis=0)
+
+    w = [m.astype(bf16) for m in split_weight(proj_w_ref, w_scratch)]
+    att, att_far = att_ref[...], att_far_ref[...]
+    queries = (dot_nn(att, w[0]) * size ** (-0.5)).astype(bf16)
+    keys = dot_nn(att, w[1]).astype(bf16)
+    values = dot_nn(att, w[2]).astype(bf16)
+    keys_far = dot_nn(att_far, w[1]).astype(bf16)
+    values_far = dot_nn(att_far, w[2]).astype(bf16)
+    gate = sigmoid(dot_nn(att, w[3]))
+    head_of = lax.broadcasted_iota(jnp.int32, (cols_here, width), 1) // size
+    for i in range(rows_here):
+        at = slice(i * cols_here, (i + 1) * cols_here)
+        q = queries[at]
+        q_heads = jnp.concatenate(
+            [jnp.where(head_of == h, q, jnp.zeros_like(q)) for h in range(heads)], axis=0
+        )
+        k = jnp.concatenate([keys[at], keys_far[at]], axis=0)
+        v = jnp.concatenate([values[at], values_far[at]], axis=0)
+        scores = dot_nt(q_heads, k) + head_bias
+        raised = jnp.exp(scores - jnp.max(scores, axis=-1, keepdims=True))
+        weights = (raised / jnp.sum(raised, axis=-1, keepdims=True)).astype(bf16)
+        mixed = dot_nn(weights, v)
+        attended = mixed[:cols_here]
+        for h in range(1, heads):
+            attended = jnp.where(head_of == h, mixed[h * cols_here : (h + 1) * cols_here], attended)
+        gated = (attended * gate[at]).astype(bf16)
+        out_ref[at] = mid_ref[at] + dot_nn(gated, out_w_ref[...])
+
+
+def body_channels(
+    pair,
+    residue_mask,
+    tri_norm_gain,
+    tri_in_weight,
+    tri_gate_weight,
+    tri_out_norm_gain,
+    tri_out_weight,
+    att_norm_gain,
+    att_proj_weight,
+    att_bias_weight,
+    att_out_weight,
+):
+    rows_here, cols_here, chan = pair.shape
+    rows, cols = lax.axis_size("row"), lax.axis_size(("col", "sub"))
+    group = ("row", "col", "sub")
+    devices = rows * cols
+    residues = cols_here * cols
+    cells = rows_here * cols_here
+    hidden = tri_in_weight.shape[2]
+    own = hidden // devices
+    heads = att_bias_weight.shape[1]
+    blocks = rows // cols
+    tiles = -(-cells // LANES)
+    lr_panels = -(-2 * cells // LANES) if (-cells) % LANES * 2 == LANES else 2 * tiles
+    flat = pair.reshape(cells, chan)
+    live = residue_mask.reshape(1, residues)
+
+    lr, normed = pl.pallas_call(
+        functools.partial(factors_kernel, devices),
+        out_shape=(
+            jax.ShapeDtypeStruct((devices, lr_panels, own, LANES), bf16),
+            jax.ShapeDtypeStruct((cells, chan), bf16),
+        ),
+        scratch_shapes=[pltpu.VMEM(tri_in_weight.shape, f32)],
+        name="factors",
+    )(flat, tri_norm_gain.reshape(1, chan), tri_in_weight)
+    lr = lax.all_to_all(lr, group, 0, 0, tiled=True)
+    sums = pl.pallas_call(
+        functools.partial(triangle_kernel, rows_here, cols_here),
+        out_shape=jax.ShapeDtypeStruct((devices, tiles, own, LANES), bf16),
+        scratch_shapes=[pltpu.VMEM((residues, own, LANES), f32) for _ in range(3)],
+        name="triangle",
+    )(live, lr)
+    sums = lax.all_to_all(sums, group, 0, 0, tiled=True)
+    mid, att, bias = pl.pallas_call(
+        middle_kernel,
+        out_shape=(
+            jax.ShapeDtypeStruct((cells, chan), f32),
+            jax.ShapeDtypeStruct((cells, chan), bf16),
+            jax.ShapeDtypeStruct((heads, cells), bf16),
+        ),
+        name="middle",
+    )(
+        flat,
+        normed,
+        sums,
+        tri_out_norm_gain.reshape(1, hidden),
+        tri_out_weight,
+        tri_gate_weight,
+        att_norm_gain.reshape(1, chan),
+        att_bias_weight,
+    )
+    att_far = lax.ppermute(att, ("col", "sub"), [(c, c ^ 1) for c in range(cols)])
+    held = bias[None]
+    step = 1
+    while step < blocks:
+        other = lax.ppermute(held, "row", [(r, r ^ step) for r in range(rows)])
+        held = jnp.concatenate([held, other], axis=0)
+        step *= 2
+    spread = []
+    for shift in range(cols):
+        pairs = []
+        for part in range(cols):
+            for q in range(blocks):
+                for c in range(cols):
+                    source = (c * blocks + q) * cols + (part + shift) % cols
+                    pairs.append((source, (part * blocks + q) * cols + c))
+        spread.append(lax.ppermute(held, group, pairs))
+    row, col = lax.axis_index("row"), lax.axis_index(("col", "sub"))
+    place = jnp.stack([row % blocks, col, (row // blocks == col).astype(jnp.int32)])
+    out = pl.pallas_call(
+        functools.partial(attention_kernel, rows_here),
+        out_shape=jax.ShapeDtypeStruct((cells, chan), f32),
+        in_specs=[pl.BlockSpec(memory_space=pltpu.SMEM)]
+        + [pl.BlockSpec(memory_space=pltpu.VMEM)] * 8,
+        scratch_shapes=[
+            pltpu.VMEM(att_proj_weight.shape, f32),
+            pltpu.VMEM((cols_here, heads, LANES), f32),
+        ],
+        name="attention",
+    )(place, live, *spread, att, att_far, mid, att_proj_weight, att_out_weight)
+    return out.reshape(pair.shape)
+
+
 def solution(mesh):
     placed = (
         P(("parts", "row"), ("col", "sub"), None),
@@ -135,6 +459,22 @@
         P(),
         P(),
     )
+
+    def body(pair, residue_mask, tri_norm_gain, tri_in_weight, *others):
+        rows, cols = mesh.shape["row"], mesh.shape["col"] * mesh.shape["sub"]
+        hidden = tri_in_weight.shape[2]
+        fits = (
+            cols == 2
+            and rows % cols == 0
+            and (rows // cols) & (rows // cols - 1) == 0
+            and hidden % (8 * rows * cols) == 0
+            and hidden == pair.shape[2] == LANES
+            and residue_mask.shape[0] <= LANES
+            and pair.shape[0] * cols * pair.shape[1] % 16 == 0
+        )
+        chosen = body_channels if fits else body_general
+        return chosen(pair, residue_mask, tri_norm_gain, tri_in_weight, *others)
+
     return jax.shard_map(
         body,
         mesh=mesh,

time: 125 us -> 58.2 us (0.47); the launches traced: 123 us -> 57.7 us
  blocking collectives: 55.7 us -> 15.7 us
  matrix products: 18.6 us -> 0 us
  Pallas kernels: 0 us -> 14.4 us
  between operations: 13.7 us -> 0.04 us
  local copies, waits for them, and re-layouts: 13.6 us -> 2.06 us
  starting transfers between devices: 4.42 us -> 11.9 us
  other arithmetic: 4.1 us -> 1.38 us
    all_gather x5 -> x0, blocking collectives: 38.5 us -> none  [the longest x1 13.9 us: body(): bias_all_rows = lax.all_gather(pair_bias, 'row', axis=0, tiled=True)]
    dot_general x19 -> x0, matrix products: 16.1 us -> none  [the longest x6 9.36 us: attend(): jnp.einsum('ihjk,ikhd->ijhd', weights, value_block, preferred_element_typ...]
    pallas_call x0 -> x4, Pallas kernels: none -> 14.4 us  [the longest x1 6.34 us: body_channels(): pl.pallas_call(functools.partial(attention_kernel, rows_here), out_shape=...]
    all_gather x1 -> x0, waiting for transfers between devices: 12.5 us -> none  [body(): lax.all_gather(own_rows, 'row', axis=1, tiled=True)]
    all_gather x5 -> x0, local copies, waits for them, and re-layouts: 7.78 us -> none  [the longest x1 5.29 us: body(): lax.all_gather(own_rows, 'row', axis=1, tiled=True)]
    ppermute x0 -> x5, starting transfers between devices: none -> 7.01 us  [the longest x2 4.41 us: body_channels(): spread.append(lax.ppermute(held, group, pairs))]
    ppermute x0 -> x5, waiting for transfers between devices: none -> 6.42 us  [the longest x2 3.9 us: body_channels(): spread.append(lax.ppermute(held, group, pairs))]
    all_to_all x1, waiting for transfers between devices: 0.01 us -> 5.86 us  [body_channels(): sums = lax.all_to_all(sums, group, 0, 0, tiled=True)]
  transfers between devices with their start and end apart: 2 -> 6, of which waited for: 1 -> 4; matrix products, arithmetic and copies ran while one was open for 4% -> 2% of each run, Pallas kernels for 0% -> 0%
where the time goes in v1:
time: 58.2 us; the launch traced here: 57.7 us
  blocking collectives  15.7 us (27%)
  Pallas kernels  14.4 us (25%)
  waiting for transfers between devices  12.3 us (21%)
  starting transfers between devices  11.9 us (20%)
  local copies, waits for them, and re-layouts  2.06 us (4%)
  other arithmetic  1.38 us (2%)
    all_to_all x1, blocking collectives, body_channels(): lr = lax.all_to_all(lr, group, 0, 0, tiled=True)  15.7 us
    pallas_call x1, Pallas kernels, body_channels(): pl.pallas_call(functools.partial(attention_kernel, rows_here), out_shape=...  6.34 us
    all_to_all x1, waiting for transfers between devices, body_channels(): sums = lax.all_to_all(sums, group, 0, 0, tiled=True)  5.86 us
    all_to_all x1, starting transfers between devices, body_channels(): sums = lax.all_to_all(sums, group, 0, 0, tiled=True)  4.9 us
    ppermute x2, starting transfers between devices, body_channels(): spread.append(lax.ppermute(held, group, pairs))  4.41 us
    ppermute x2, waiting for transfers between devices, body_channels(): spread.append(lax.ppermute(held, group, pairs))  3.9 us
    pallas_call x1, Pallas kernels, body_channels(): pl.pallas_call(middle_kernel, out_shape=(jax.ShapeDtypeStruct((cells, cha...  3 us
    pallas_call x1, Pallas kernels, body_channels(): pl.pallas_call(functools.partial(triangle_kernel, rows_here, cols_here),...  2.66 us
  transfers between devices with their start and end apart: 6, of which 4 were waited for; matrix products, arithmetic and copies ran while one was open for 2% of the time, Pallas kernels for 0%

profile of v1, /device:TPU:6, one launch (start us, length us, event | category | flops | bytes accessed | tf_op | source)
XLA Modules:
  0.0 57.7 jit_solution(4850037174015109480)
XLA Ops:
  0.0 2.4 %factors.1 = (bf16[16,9,8,128]{3,2,1,0:T(8,128)(2,1)}, bf16[576,128]{1,0:T(8,128)(2,1)}) custom-call(f32[576,128]{1,0:T(8,128)} %bitcast.10, f32[1,128]{1,0:T(1,128)} %bitcast.17, bf16[128,4,128]{2,1,0:T(4,128)(2,1)} %w_ref.1), custom_call_target="tpu_custom_call" | custom-call | tf_op jit(solution)/shard_map/factors/pallas_call | solution.py:381
  2.4 15.7 %all_to_all.10.lr_ref = bf16[16,9,8,128]{3,2,1,0:T(8,128)(2,1)} all-to-all(bf16[16,9,8,128]{3,2,1,0:T(8,128)(2,1)} %get-tuple-element.11), channel_id=1, replica_groups=mesh['parts'=2,'row'=8,'col'=2,'sub'=1] {'row','col','sub'}, dimensions={0} | all-to-all | bytes 589824 | tf_op jit(solution)/shard_map/all_to_all | solution.py:390
  18.1 2.7 %triangle.1 = bf16[16,5,8,128]{3,2,1,0:T(8,128)(2,1)} custom-call(s32[1,96]{1,0:T(1,128)} %bitcast.15, bf16[16,9,8,128]{3,2,1,0:T(8,128)(2,1)} %all_to_all.10.lr_ref), custom_call_target="tpu_custom_call" | custom-call | tf_op jit(solution)/shard_map/triangle/pallas_call | solution.py:391
  20.7 0.0 copy-start.5
  20.7 4.9 %all-to-all-start.1 = ((bf16[16,5,8,128]{3,2,1,0:T(8,128)(2,1)}), bf16[16,5,8,128]{3,2,1,0:T(8,128)(2,1)S(1)}, u32[]{:S(2)}, u32[]{:S(2)}) async-start(bf16[16,5,8,128]{3,2,1,0:T(8,128)(2,1)} %triangle.1), calls=%async_computation.1 | async-start | bytes 327680 | tf_op jit(solution)/shard_map/all_to_all | solution.py:397
  25.6 0.0 copy-done.5
  25.6 0.7 %copy.12.bias_w_ref = bf16[128,4]{1,0:T(8,128)(2,1)} copy(bf16[128,4]{0,1:T(4,128)(2,1)S(1)} %copy-done.5) | data formatting | bytes 2048 | tf_op args[9]
  26.4 5.9 %all-to-all-done.1.sum_ref = bf16[16,5,8,128]{3,2,1,0:T(8,128)(2,1)S(1)} async-done(((bf16[16,5,8,128]{3,2,1,0:T(8,128)(2,1)}), bf16[16,5,8,128]{3,2,1,0:T(8,128)(2,1)S(1)}, u32[]{:S(2)}, u32[]{:S(2)}) %all-to-all-start.1) | async-done | bytes 163872 | tf_op jit(solution)/shard_map/all_to_all | solution.py:397
  32.2 0.0 copy-start
  32.2 0.7 %copy-done = bf16[16,5,8,128]{3,2,1,0:T(8,128)(2,1)} copy-done((bf16[16,5,8,128]{3,2,1,0:T(8,128)(2,1)}, bf16[16,5,8,128]{3,2,1,0:T(8,128)(2,1)S(1)}, u32[]{:S(2)}) %copy-start) | copy-done | bytes 163864
  32.9 3.0 %middle.1 = (f32[576,128]{1,0:T(8,128)}, bf16[576,128]{1,0:T(8,128)(2,1)}, bf16[4,576]{1,0:T(4,128)(2,1)}) custom-call(f32[576,128]{1,0:T(8,128)} %bitcast.11, bf16[576,128]{1,0:T(8,128)(2,1)} %get-tuple-element.10.normed_ref, bf16[16,5,8,128]{3,2,1,0:T(8,128)(2,1)} %copy-done, f32[1,128]{1,0:T(1,128)} %bitcast.18, bf16[128,128]{1,0:T(8,128)(2,1)} %out_w_ref.2, ...), custom_call_target="tpu_custom_call" | custom-call | tf_op jit(solution)/shard_map/middle/pallas_call | solution.py:398
  35.9 0.1 collective-permute-start
  36.0 1.3 %collective-permute-done = bf16[1,4,576]{2,1,0:T(4,128)(2,1)S(1)} collective-permute-done((bf16[1,4,576]{2,1,0:T(4,128)(2,1)}, bf16[1,4,576]{2,1,0:T(4,128)(2,1)S(1)}, u32[]{:S(2)}, u32[]{:S(2)}) %collective-permute-start) | collective-permute-done | bytes 4640 | tf_op jit(solution)/shard_map/ppermute | solution.py:420
  37.3 0.7 %pad_maximum_fusion.1 = bf16[2,4,576]{2,1,0:T(4,128)(2,1)S(1)} fusion(bf16[1,4,576]{2,1,0:T(4,128)(2,1)S(1)} %collective-permute-done, bf16[1,4,576]{2,1,0:T(4,128)(2,1)} %bitcast.13), kind=kLoop, calls=%fused_computation.1 | loop fusion | flops 4608 | bytes 18432 | tf_op jit(solution)/shard_map/concatenate | solution.py:421
  38.0 1.0 %collective-permute-start.1 = (bf16[2,4,576]{2,1,0:T(4,128)(2,1)S(1)}, bf16[2,4,576]{2,1,0:T(4,128)(2,1)S(1)}, u32[]{:S(2)}, u32[]{:S(2)}) collective-permute-start(bf16[2,4,576]{2,1,0:T(4,128)(2,1)S(1)} %pad_maximum_fusion.1), channel_id=1, source_target_pairs={{0,4},{2,6},{4,0},{6,2},{8,12},{10,14},{12,8},{14,10},{1,5},{3,7},... | collective-permute-start | bytes 27656 | tf_op jit(solution)/shard_map/ppermute | solution.py:420
  39.0 0.0 copy-start.2
  39.0 1.5 %collective-permute-start.4 = (bf16[576,128]{1,0:T(8,128)(2,1)}, bf16[576,128]{1,0:T(8,128)(2,1)S(1)}, u32[]{:S(2)}, u32[]{:S(2)}) collective-permute-start(bf16[576,128]{1,0:T(8,128)(2,1)} %get-tuple-element.13.att_ref), channel_id=1, source_target_pairs={{0,1},{1,0},{2,3},{3,2},{4,5},{5,4},{6,7},{7,6},{8,9},{9,8},{10,11... | collective-permute-start | bytes 442376 | tf_op jit(solution)/shard_map/ppermute | solution.py:416
  40.5 1.2 %collective-permute-done.1 = bf16[2,4,576]{2,1,0:T(4,128)(2,1)S(1)} collective-permute-done((bf16[2,4,576]{2,1,0:T(4,128)(2,1)S(1)}, bf16[2,4,576]{2,1,0:T(4,128)(2,1)S(1)}, u32[]{:S(2)}, u32[]{:S(2)}) %collective-permute-start.1) | collective-permute-done | bytes 9248 | tf_op jit(solution)/shard_map/ppermute | solution.py:420
  41.7 0.0 copy-done.2
  41.7 1.5 %collective-permute-start.3 = (bf16[4,4,576]{2,1,0:T(4,128)(2,1)S(1)}, bf16[4,4,576]{2,1,0:T(4,128)(2,1)S(1)}, u32[]{:S(2)}, u32[]{:S(2)}) collective-permute-start(bf16[4,4,576]{2,1,0:T(4,128)(2,1)S(1)} %pad_maximum_fusion), channel_id=1, source_target_pairs={{1,0},{9,1},{3,2},{11,3},{5,4},{13,5},{7,6},{15,7},{0,8},{8,9},{2,... | collective-permute-start | bytes 55304 | tf_op jit(solution)/shard_map/ppermute | solution.py:431
  43.3 2.9 %collective-permute-start.2 = (bf16[4,4,576]{2,1,0:T(4,128)(2,1)S(1)}, bf16[4,4,576]{2,1,0:T(4,128)(2,1)S(1)}, u32[]{:S(2)}, u32[]{:S(2)}) collective-permute-start(bf16[4,4,576]{2,1,0:T(4,128)(2,1)S(1)} %pad_maximum_fusion), channel_id=1, source_target_pairs={{0,0},{8,1},{2,2},{10,3},{4,4},{12,5},{6,6},{14,7},{1,8},{9,9},{3,... | collective-permute-start | bytes 55304 | tf_op jit(solution)/shard_map/ppermute | solution.py:431
  46.2 0.7 %pad_add_fusion.place_ref = s32[3]{0:T(128)} fusion(s32[1]{0:T(128)} %bitcast.2, s32[1]{0:T(128)} %bitcast.1, s32[1]{0:T(128)} %bitcast), kind=kLoop, calls=%fused_computation.2 | loop fusion | flops 6 | bytes 24 | tf_op jit(solution)/shard_map/stack | solution.py:433
  46.8 0.0 collective-permute-done.3.bias_b_ref
  46.8 0.0 copy-start.3
  46.8 3.9 %collective-permute-done.2.bias_a_ref = bf16[4,4,576]{2,1,0:T(4,128)(2,1)S(1)} collective-permute-done((bf16[4,4,576]{2,1,0:T(4,128)(2,1)S(1)}, bf16[4,4,576]{2,1,0:T(4,128)(2,1)S(1)}, u32[]{:S(2)}, u32[]{:S(2)}) %collective-permute-start.2) | collective-permute-done | bytes 18464 | tf_op jit(solution)/shard_map/ppermute | solution.py:431
  50.7 0.0 copy-start.4
  50.7 0.0 collective-permute-done.4.att_far_ref
  50.7 0.0 copy-start.1
  50.7 0.0 copy-done.3
  50.7 0.6 %copy-done.4 = bf16[4,4,576]{2,1,0:T(4,128)(2,1)} copy-done((bf16[4,4,576]{2,1,0:T(4,128)(2,1)}, bf16[4,4,576]{2,1,0:T(4,128)(2,1)S(1)}, u32[]{:S(2)}) %copy-start.4) | copy-done | bytes 18456
  51.3 0.1 copy-done.1
  51.4 6.3 %attention.1 = f32[576,128]{1,0:T(8,128)} custom-call(s32[3]{0:T(128)} %pad_add_fusion.place_ref, s32[1,96]{1,0:T(1,128)} %bitcast.16, bf16[4,4,576]{2,1,0:T(4,128)(2,1)} %copy-done.4, bf16[4,4,576]{2,1,0:T(4,128)(2,1)} %copy-done.3, bf16[576,128]{1,0:T(8,128)(2,1)} %get-tuple-element.13.att_ref, bf16[576,128]{1,0:T(8,128)(2,1)} %copy-done.1, ...), custom_call_target="tpu_custom_call" | custom-call | tf_op jit(solution)/shard_map/attention/pallas_call | solution.py:434
  (1 shorter events, 0.0 us)
Async XLA Ops:
  20.7 4.9 %copy-start.5 = (bf16[128,4]{0,1:T(4,128)(2,1)S(1)}, bf16[128,4]{0,1:T(4,128)(2,1)}, u32[]{:S(2)}) copy-start(bf16[128,4]{0,1:T(4,128)(2,1)} %param.20) | copy-start | bytes 3076
  20.7 11.5 %all-to-all-start.1 = ((bf16[16,5,8,128]{3,2,1,0:T(8,128)(2,1)}), bf16[16,5,8,128]{3,2,1,0:T(8,128)(2,1)S(1)}, u32[]{:S(2)}, u32[]{:S(2)}) async-start(bf16[16,5,8,128]{3,2,1,0:T(8,128)(2,1)} %triangle.1), calls=%async_computation.1 | async-start | bytes 327680 | tf_op jit(solution)/shard_map/all_to_all | solution.py:397
  32.2 0.7 %copy-start = (bf16[16,5,8,128]{3,2,1,0:T(8,128)(2,1)}, bf16[16,5,8,128]{3,2,1,0:T(8,128)(2,1)S(1)}, u32[]{:S(2)}) copy-start(bf16[16,5,8,128]{3,2,1,0:T(8,128)(2,1)S(1)} %all-to-all-done.1.sum_ref) | copy-start | bytes 491524
  35.9 1.4 %collective-permute-start = (bf16[1,4,576]{2,1,0:T(4,128)(2,1)}, bf16[1,4,576]{2,1,0:T(4,128)(2,1)S(1)}, u32[]{:S(2)}, u32[]{:S(2)}) collective-permute-start(bf16[1,4,576]{2,1,0:T(4,128)(2,1)} %bitcast.12), channel_id=1, source_target_pairs={{0,2},{2,0},{4,6},{6,4},{8,10},{10,8},{12,14},{14,12},{1,3},{3,1},... | collective-permute-start | bytes 13832 | tf_op jit(solution)/shard_map/ppermute | solution.py:420
  38.0 3.7 %collective-permute-start.1 = (bf16[2,4,576]{2,1,0:T(4,128)(2,1)S(1)}, bf16[2,4,576]{2,1,0:T(4,128)(2,1)S(1)}, u32[]{:S(2)}, u32[]{:S(2)}) collective-permute-start(bf16[2,4,576]{2,1,0:T(4,128)(2,1)S(1)} %pad_maximum_fusion.1), channel_id=1, source_target_pairs={{0,4},{2,6},{4,0},{6,2},{8,12},{10,14},{12,8},{14,10},{1,5},{3,7},... | collective-permute-start | bytes 27656 | tf_op jit(solution)/shard_map/ppermute | solution.py:420
  39.0 2.7 %copy-start.2 = (bf16[4,576]{1,0:T(4,128)(2,1)S(1)}, bf16[4,576]{1,0:T(4,128)(2,1)}, u32[]{:S(2)}) copy-start(bf16[4,576]{1,0:T(4,128)(2,1)} %get-tuple-element.12) | copy-start | bytes 13828
  39.0 11.7 %collective-permute-start.4 = (bf16[576,128]{1,0:T(8,128)(2,1)}, bf16[576,128]{1,0:T(8,128)(2,1)S(1)}, u32[]{:S(2)}, u32[]{:S(2)}) collective-permute-start(bf16[576,128]{1,0:T(8,128)(2,1)} %get-tuple-element.13.att_ref), channel_id=1, source_target_pairs={{0,1},{1,0},{2,3},{3,2},{4,5},{5,4},{6,7},{7,6},{8,9},{9,8},{10,11... | collective-permute-start | bytes 442376 | tf_op jit(solution)/shard_map/ppermute | solution.py:416
  41.7 5.1 %collective-permute-start.3 = (bf16[4,4,576]{2,1,0:T(4,128)(2,1)S(1)}, bf16[4,4,576]{2,1,0:T(4,128)(2,1)S(1)}, u32[]{:S(2)}, u32[]{:S(2)}) collective-permute-start(bf16[4,4,576]{2,1,0:T(4,128)(2,1)S(1)} %pad_maximum_fusion), channel_id=1, source_target_pairs={{1,0},{9,1},{3,2},{11,3},{5,4},{13,5},{7,6},{15,7},{0,8},{8,9},{2,... | collective-permute-start | bytes 55304 | tf_op jit(solution)/shard_map/ppermute | solution.py:431
  43.3 7.5 %collective-permute-start.2 = (bf16[4,4,576]{2,1,0:T(4,128)(2,1)S(1)}, bf16[4,4,576]{2,1,0:T(4,128)(2,1)S(1)}, u32[]{:S(2)}, u32[]{:S(2)}) collective-permute-start(bf16[4,4,576]{2,1,0:T(4,128)(2,1)S(1)} %pad_maximum_fusion), channel_id=1, source_target_pairs={{0,0},{8,1},{2,2},{10,3},{4,4},{12,5},{6,6},{14,7},{1,8},{9,9},{3,... | collective-permute-start | bytes 55304 | tf_op jit(solution)/shard_map/ppermute | solution.py:431
  46.8 3.9 %copy-start.3 = (bf16[4,4,576]{2,1,0:T(4,128)(2,1)}, bf16[4,4,576]{2,1,0:T(4,128)(2,1)S(1)}, u32[]{:S(2)}) copy-start(bf16[4,4,576]{2,1,0:T(4,128)(2,1)S(1)} %collective-permute-done.3.bias_b_ref) | copy-start | bytes 55300
  50.7 0.6 %copy-start.4 = (bf16[4,4,576]{2,1,0:T(4,128)(2,1)}, bf16[4,4,576]{2,1,0:T(4,128)(2,1)S(1)}, u32[]{:S(2)}) copy-start(bf16[4,4,576]{2,1,0:T(4,128)(2,1)S(1)} %collective-permute-done.2.bias_a_ref) | copy-start | bytes 55300
  50.7 0.7 %copy-start.1 = (bf16[576,128]{1,0:T(8,128)(2,1)}, bf16[576,128]{1,0:T(8,128)(2,1)S(1)}, u32[]{:S(2)}) copy-start(bf16[576,128]{1,0:T(8,128)(2,1)S(1)} %collective-permute-done.4.att_far_ref) | copy-start | bytes 442372

commit v2 on v1

--- a/solution.py
+++ b/solution.py
@@ -139,13 +139,33 @@
     return lax.dot_general(a, b, (((1,), (1,)), ((), ())), preferred_element_type=f32)
 
 
+def near(v):
+    return pltpu.with_memory_space_constraint(v, pltpu.VMEM)
+
+
 def split_weight(w_ref, w_scratch):
     w_scratch[...] = w_ref[...].astype(f32)
     return [w_scratch[:, p, :] for p in range(w_ref.shape[1])]
 
 
-def factors_kernel(devices, pair_ref, gain_ref, w_ref, lr_ref, normed_ref, w_scratch):
+def factors_kernel(
+    devices,
+    pair_ref,
+    gain_ref,
+    w_ref,
+    live_ref,
+    out_gain_ref,
+    att_gain_ref,
+    lr_ref,
+    normed_ref,
+    rows_ref,
+    w_scratch,
+):
     cells, chan = pair_ref.shape
+    live = live_ref[...].astype(f32)
+    rows_ref[0:1] = jnp.concatenate([live, jnp.zeros((1, LANES - live.shape[1]), f32)], axis=1)
+    rows_ref[1:2] = out_gain_ref[...]
+    rows_ref[2:3] = att_gain_ref[...]
     hidden = w_ref.shape[2]
     own = hidden // devices
     normed = norm_last(pair_ref[...], gain_ref[...]).astype(bf16)
@@ -184,10 +204,10 @@
 
 
 def triangle_kernel(
-    rows_here, cols_here, live_ref, lr_ref, sum_ref, left_scratch, right_scratch, sum_scratch
+    rows_here, cols_here, vectors_ref, lr_ref, sum_ref, left_scratch, right_scratch, sum_scratch
 ):
     devices, panels_in, own, _ = lr_ref.shape
-    residues = live_ref.shape[1]
+    residues = left_scratch.shape[0]
     cols = residues // cols_here
     rows = residues // rows_here
     cells = rows_here * cols_here
@@ -204,8 +224,7 @@
                     moved = segment(parts[c], start, c * cols_here)
                     line = jnp.where(lane < c * cols_here, line, moved)
                 scratch[r * rows_here + i] = line
-    live = live_ref[...].astype(f32)
-    live_wide = jnp.concatenate([live, jnp.zeros((1, LANES - residues), f32)], axis=1)
+    live_wide = vectors_ref[0:1]
     live_square = jnp.broadcast_to(live_wide, (LANES, LANES))
     both = live_square * jnp.transpose(live_square)
     both = both[:residues]
@@ -235,10 +254,9 @@
     pair_ref,
     normed_ref,
     sum_ref,
-    out_gain_ref,
+    vectors_ref,
     out_w_ref,
     gate_w_ref,
-    att_gain_ref,
     bias_w_ref,
     mid_ref,
     att_ref,
@@ -247,7 +265,7 @@
     devices, tiles, own, _ = sum_ref.shape
     cells, chan = pair_ref.shape
     hidden = devices * own
-    gain_col = jnp.transpose(jnp.broadcast_to(out_gain_ref[...], (LANES, hidden)))
+    gain_col = jnp.transpose(jnp.broadcast_to(vectors_ref[1:2], (LANES, hidden)))
     gate = sigmoid(dot_nn(normed_ref[...], gate_w_ref[...]))
     bias_w = jnp.transpose(bias_w_ref[...].astype(f32)).astype(bf16)
     for t in range(tiles):
@@ -261,15 +279,14 @@
         update = dot_nn(hidden_rows[: high - low], out_w_ref[...])
         mid = pair_ref[low:high] + gate[low:high] * update
         mid_ref[low:high] = mid
-        att = norm_last(mid, att_gain_ref[...]).astype(bf16)
+        att = norm_last(mid, vectors_ref[2:3]).astype(bf16)
         att_ref[low:high] = att
         bias_ref[:, low:high] = dot_nt(bias_w, att).astype(bf16)
 
 
 def attention_kernel(
     rows_here,
-    place_ref,
-    live_ref,
+    vectors_ref,
     bias_a_ref,
     bias_b_ref,
     att_ref,
@@ -284,13 +301,14 @@
     cells, chan = att_ref.shape
     cols_here = cells // rows_here
     blocks, heads, _ = bias_a_ref.shape
-    residues = live_ref.shape[1]
+    residues = 2 * cols_here
     width = proj_w_ref.shape[2]
     size = width // heads
-    block_at, col, same = place_ref[0], place_ref[1], place_ref[2]
+    row, col = lax.axis_index("row"), lax.axis_index(("col", "sub"))
+    block_at = lax.rem(row, blocks)
+    same = (lax.div(row, blocks) == col).astype(jnp.int32)
     lane_row = lax.broadcasted_iota(jnp.int32, (1, LANES), 1)
-    live = live_ref[...].astype(f32)
-    live_wide = jnp.concatenate([live, jnp.zeros((1, LANES - residues), f32)], axis=1)
+    live_wide = vectors_ref[0:1]
     swapped = jnp.where(
         lane_row < cols_here,
         pltpu.roll(live_wide, LANES - cols_here, 1),
@@ -308,13 +326,13 @@
 
     for m in range(blocks):
         first, second = bias_a_ref[m].astype(f32), bias_b_ref[m].astype(f32)
-        near = panels(jnp.where(same == 1, first, second))
+        mine = panels(jnp.where(same == 1, first, second))
         far = panels(jnp.where(same == 1, second, first))
         base = jnp.bitwise_xor(block_at, m) * rows_here
         for j in range(rows_here):
             line = jnp.where(
                 lane < cols_here,
-                segment(near, j * cols_here, 0),
+                segment(mine, j * cols_here, 0),
                 segment(far, j * cols_here, cols_here),
             )
             bias_scratch[base + j] = line
@@ -378,40 +396,52 @@
     flat = pair.reshape(cells, chan)
     live = residue_mask.reshape(1, residues)
 
-    lr, normed = pl.pallas_call(
+    lr, normed, vectors = pl.pallas_call(
         functools.partial(factors_kernel, devices),
         out_shape=(
-            jax.ShapeDtypeStruct((devices, lr_panels, own, LANES), bf16),
-            jax.ShapeDtypeStruct((cells, chan), bf16),
+            pltpu.VMEM((devices, lr_panels, own, LANES), bf16),
+            pltpu.VMEM((cells, chan), bf16),
+            pltpu.VMEM((8, LANES), f32),
         ),
         scratch_shapes=[pltpu.VMEM(tri_in_weight.shape, f32)],
         name="factors",
-    )(flat, tri_norm_gain.reshape(1, chan), tri_in_weight)
+    )(
+        flat,
+        tri_norm_gain.reshape(1, chan),
+        tri_in_weight,
+        live,
+        tri_out_norm_gain.reshape(1, hidden),
+        att_norm_gain.reshape(1, chan),
+    )
     lr = lax.all_to_all(lr, group, 0, 0, tiled=True)
     sums = pl.pallas_call(
         functools.partial(triangle_kernel, rows_here, cols_here),
-        out_shape=jax.ShapeDtypeStruct((devices, tiles, own, LANES), bf16),
+        out_shape=pltpu.VMEM((devices, tiles, own, LANES), bf16),
         scratch_shapes=[pltpu.VMEM((residues, own, LANES), f32) for _ in range(3)],
         name="triangle",
-    )(live, lr)
+    )(near(vectors), near(lr))
     sums = lax.all_to_all(sums, group, 0, 0, tiled=True)
     mid, att, bias = pl.pallas_call(
         middle_kernel,
         out_shape=(
-            jax.ShapeDtypeStruct((cells, chan), f32),
-            jax.ShapeDtypeStruct((cells, chan), bf16),
-            jax.ShapeDtypeStruct((heads, cells), bf16),
+            pltpu.VMEM((cells, chan), f32),
+            pltpu.VMEM((cells, chan), bf16),
+            pltpu.VMEM((heads, cells), bf16),
         ),
         name="middle",
     )(
-        flat,
-        normed,
-        sums,
-        tri_out_norm_gain.reshape(1, hidden),
-        tri_out_weight,
-        tri_gate_weight,
-        att_norm_gain.reshape(1, chan),
-        att_bias_weight,
+        *map(
+            near,
+            (
+                flat,
+                normed,
+                sums,
+                vectors,
+                tri_out_weight,
+                tri_gate_weight,
+                att_bias_weight,
+            ),
+        )
     )
     att_far = lax.ppermute(att, ("col", "sub"), [(c, c ^ 1) for c in range(cols)])
     held = bias[None]
@@ -429,19 +459,15 @@
                     source = (c * blocks + q) * cols + (part + shift) % cols
                     pairs.append((source, (part * blocks + q) * cols + c))
         spread.append(lax.ppermute(held, group, pairs))
-    row, col = lax.axis_index("row"), lax.axis_index(("col", "sub"))
-    place = jnp.stack([row % blocks, col, (row // blocks == col).astype(jnp.int32)])
     out = pl.pallas_call(
         functools.partial(attention_kernel, rows_here),
         out_shape=jax.ShapeDtypeStruct((cells, chan), f32),
-        in_specs=[pl.BlockSpec(memory_space=pltpu.SMEM)]
-        + [pl.BlockSpec(memory_space=pltpu.VMEM)] * 8,
         scratch_shapes=[
             pltpu.VMEM(att_proj_weight.shape, f32),
             pltpu.VMEM((cols_here, heads, LANES), f32),
         ],
         name="attention",
-    )(place, live, *spread, att, att_far, mid, att_proj_weight, att_out_weight)
+    )(*map(near, (vectors, *spread, att, att_far, mid, att_proj_weight, att_out_weight)))
     return out.reshape(pair.shape)
 
 

time: 58.2 us -> 50.9 us (0.87)
  Pallas kernels: 14.4 us -> 9.8 us
  local copies, waits for them, and re-layouts: 2.06 us -> 0.16 us
  other arithmetic: 1.38 us -> 0.03 us
  waiting for transfers between devices: 12.3 us -> 13.3 us
    pallas_call x2, Pallas kernels: 5.38 us -> 2.98 us  [the longest x1 1.68 us: body_channels(): pl.pallas_call(functools.partial(factors_kernel, devices), out_shape=(plt...]
    unnamed x13, local copies, waits for them, and re-layouts: 2.06 us -> 0.16 us
    pallas_call x1, Pallas kernels: 6.34 us -> 5.14 us  [body_channels(): pl.pallas_call(functools.partial(attention_kernel, rows_here), out_shape=...]
    pallas_call x1, Pallas kernels: 2.66 us -> 1.68 us  [body_channels(): pl.pallas_call(functools.partial(triangle_kernel, rows_here, cols_here),...]
    concatenate x2, other arithmetic: 0.72 us -> 0.03 us  [body_channels(): held = jnp.concatenate([held, other], axis=0)]
    another operation x1 -> x0, other arithmetic: 0.66 us -> none  [body_channels(): jnp.stack([row % blocks, col, (row // blocks == col).astype(jnp.int32)])]
    all_to_all x1, waiting for transfers between devices: 5.86 us -> 6.45 us  [body_channels(): sums = lax.all_to_all(sums, group, 0, 0, tiled=True)]
  transfers between devices with their start and end apart: 6 -> 6, of which waited for: 4 -> 4; matrix products, arithmetic and copies ran while one was open for 2% -> 0% of each run, Pallas kernels for 0% -> 0%
where the time goes in v2:
time: 50.9 us; the launch traced here: 50.7 us
  blocking collectives  15.4 us (30%)
  waiting for transfers between devices  13.3 us (26%)
  starting transfers between devices  11.9 us (23%)
  Pallas kernels  9.8 us (19%)
    all_to_all x1, blocking collectives, body_channels(): lr = lax.all_to_all(lr, group, 0, 0, tiled=True)  15.4 us
    all_to_all x1, waiting for transfers between devices, body_channels(): sums = lax.all_to_all(sums, group, 0, 0, tiled=True)  6.45 us
    pallas_call x1, Pallas kernels, body_channels(): pl.pallas_call(functools.partial(attention_kernel, rows_here), out_shape=...  5.14 us
    all_to_all x1, starting transfers between devices, body_channels(): sums = lax.all_to_all(sums, group, 0, 0, tiled=True)  4.9 us
    ppermute x2, starting transfers between devices, body_channels(): spread.append(lax.ppermute(held, group, pairs))  4.41 us
    ppermute x2, waiting for transfers between devices, body_channels(): spread.append(lax.ppermute(held, group, pairs))  4.14 us
    ppermute x2, waiting for transfers between devices, body_channels(): other = lax.ppermute(held, 'row', [(r, r ^ step) for r in range(rows)])  2.72 us
    pallas_call x1, Pallas kernels, body_channels(): pl.pallas_call(functools.partial(triangle_kernel, rows_here, cols_here),...  1.68 us
  transfers between devices with their start and end apart: 6, of which 4 were waited for; matrix products, arithmetic and copies ran while one was open for 0% of the time, Pallas kernels for 0%

profile of v2, /device:TPU:6, one launch (start us, length us, event | category | flops | bytes accessed | tf_op | source)
XLA Modules:
  0.0 50.7 jit_solution(12642665176077173819)
XLA Ops:
  0.0 1.7 %factors.1 = (bf16[16,9,8,128]{3,2,1,0:T(8,128)(2,1)S(1)}, bf16[576,128]{1,0:T(8,128)(2,1)S(1)}, f32[8,128]{1,0:T(8,128)S(1)}) custom-call(f32[576,128]{1,0:T(8,128)} %bitcast.7, f32[1,128]{1,0:T(1,128)} %bitcast.12, bf16[128,4,128]{2,1,0:T(4,128)(2,1)} %w_ref.1, s32[1,96]{1,0:T(1,128)} %bitcast.13, f32[1,128]{1,0:T(1,128)} %bitcast.14, f32[1,128]{1,0:T(1,128)} %bitcast.15), custom_call_target="tpu_custom_call" | custom-call | tf_op jit(solution)/shard_map/factors/pallas_call | solution.py:399
  1.7 15.4 %all_to_all.10.lr_ref = bf16[16,9,8,128]{3,2,1,0:T(8,128)(2,1)S(1)} all-to-all(bf16[16,9,8,128]{3,2,1,0:T(8,128)(2,1)S(1)} %get-tuple-element.13), channel_id=1, replica_groups=mesh['parts'=2,'row'=8,'col'=2,'sub'=1] {'row','col','sub'}, dimensions={0} | all-to-all | bytes 589824 | tf_op jit(solution)/shard_map/all_to_all | solution.py:416
  17.1 0.0 copy-start.5
  17.1 1.7 %triangle.1 = bf16[16,5,8,128]{3,2,1,0:T(8,128)(2,1)} custom-call(f32[8,128]{1,0:T(8,128)S(1)} %get-tuple-element.11.vectors_ref, bf16[16,9,8,128]{3,2,1,0:T(8,128)(2,1)S(1)} %all_to_all.10.lr_ref), custom_call_target="tpu_custom_call" | custom-call | tf_op jit(solution)/shard_map/triangle/pallas_call | solution.py:417
  18.8 0.0 copy-start
  18.8 0.0 copy-start.3
  18.8 4.9 %all-to-all-start.1 = ((bf16[16,5,8,128]{3,2,1,0:T(8,128)(2,1)}), bf16[16,5,8,128]{3,2,1,0:T(8,128)(2,1)S(1)}, u32[]{:S(2)}, u32[]{:S(2)}) async-start(bf16[16,5,8,128]{3,2,1,0:T(8,128)(2,1)} %triangle.1), calls=%async_computation.1 | async-start | bytes 327680 | tf_op jit(solution)/shard_map/all_to_all | solution.py:423
  23.7 0.0 copy-done.5
  23.7 0.0 copy-start.2
  23.7 0.1 copy.12.bias_w_ref
  23.8 6.4 %all-to-all-done.1.sum_ref = bf16[16,5,8,128]{3,2,1,0:T(8,128)(2,1)S(1)} async-done(((bf16[16,5,8,128]{3,2,1,0:T(8,128)(2,1)}), bf16[16,5,8,128]{3,2,1,0:T(8,128)(2,1)S(1)}, u32[]{:S(2)}, u32[]{:S(2)}) %all-to-all-start.1) | async-done | bytes 163872 | tf_op jit(solution)/shard_map/all_to_all | solution.py:423
  30.3 0.0 copy-done
  30.3 0.0 copy-done.3
  30.3 0.0 copy-done.2
  30.3 0.0 copy-start.1
  30.3 1.3 %middle.1 = (f32[576,128]{1,0:T(8,128)S(1)}, bf16[576,128]{1,0:T(8,128)(2,1)S(1)}, bf16[4,576]{1,0:T(4,128)(2,1)S(1)}) custom-call(f32[576,128]{1,0:T(8,128)S(1)} %bitcast.8, bf16[576,128]{1,0:T(8,128)(2,1)S(1)} %get-tuple-element.12.normed_ref, bf16[16,5,8,128]{3,2,1,0:T(8,128)(2,1)S(1)} %all-to-all-done.1.sum_ref, ...), custom_call_target="tpu_custom_call" | custom-call | tf_op jit(solution)/shard_map/middle/pallas_call | solution.py:424
  31.6 0.0 copy-start.4
  31.6 0.1 collective-permute-start
  31.7 1.5 %collective-permute-start.4 = (bf16[576,128]{1,0:T(8,128)(2,1)S(1)}, bf16[576,128]{1,0:T(8,128)(2,1)S(1)}, u32[]{:S(2)}, u32[]{:S(2)}) collective-permute-start(bf16[576,128]{1,0:T(8,128)(2,1)S(1)} %get-tuple-element.15.att_ref), channel_id=1, source_target_pairs={{0,1},{1,0},{2,3},{3,2},{4,5},{5,4},{6,7},{7,6},{8,9},{9,8},{10,11... | collective-permute-start | bytes 442376 | tf_op jit(solution)/shard_map/ppermute | solution.py:446
  33.2 0.0 collective-permute-done
  33.2 1.0 %collective-permute-start.1 = (bf16[2,4,576]{2,1,0:T(4,128)(2,1)S(1)}, bf16[2,4,576]{2,1,0:T(4,128)(2,1)S(1)}, u32[]{:S(2)}, u32[]{:S(2)}) collective-permute-start(bf16[2,4,576]{2,1,0:T(4,128)(2,1)S(1)} %pad_maximum_fusion.1), channel_id=1, source_target_pairs={{0,4},{2,6},{4,0},{6,2},{8,12},{10,14},{12,8},{14,10},{1,5},{3,7},... | collective-permute-start | bytes 27656 | tf_op jit(solution)/shard_map/ppermute | solution.py:450
  34.2 2.7 %collective-permute-done.1 = bf16[2,4,576]{2,1,0:T(4,128)(2,1)S(1)} collective-permute-done((bf16[2,4,576]{2,1,0:T(4,128)(2,1)S(1)}, bf16[2,4,576]{2,1,0:T(4,128)(2,1)S(1)}, u32[]{:S(2)}, u32[]{:S(2)}) %collective-permute-start.1) | collective-permute-done | bytes 9248 | tf_op jit(solution)/shard_map/ppermute | solution.py:450
  37.0 1.1 %collective-permute-start.3 = (bf16[4,4,576]{2,1,0:T(4,128)(2,1)S(1)}, bf16[4,4,576]{2,1,0:T(4,128)(2,1)S(1)}, u32[]{:S(2)}, u32[]{:S(2)}) collective-permute-start(bf16[4,4,576]{2,1,0:T(4,128)(2,1)S(1)} %pad_maximum_fusion), channel_id=1, source_target_pairs={{1,0},{9,1},{3,2},{11,3},{5,4},{13,5},{7,6},{15,7},{0,8},{8,9},{2,... | collective-permute-start | bytes 55304 | tf_op jit(solution)/shard_map/ppermute | solution.py:461
  38.1 3.3 %collective-permute-start.2 = (bf16[4,4,576]{2,1,0:T(4,128)(2,1)S(1)}, bf16[4,4,576]{2,1,0:T(4,128)(2,1)S(1)}, u32[]{:S(2)}, u32[]{:S(2)}) collective-permute-start(bf16[4,4,576]{2,1,0:T(4,128)(2,1)S(1)} %pad_maximum_fusion), channel_id=1, source_target_pairs={{0,0},{8,1},{2,2},{10,3},{4,4},{12,5},{6,6},{14,7},{1,8},{9,9},{3,... | collective-permute-start | bytes 55304 | tf_op jit(solution)/shard_map/ppermute | solution.py:461
  41.4 0.3 collective-permute-done.3.bias_b_ref
  41.7 3.8 %collective-permute-done.2.bias_a_ref = bf16[4,4,576]{2,1,0:T(4,128)(2,1)S(1)} collective-permute-done((bf16[4,4,576]{2,1,0:T(4,128)(2,1)S(1)}, bf16[4,4,576]{2,1,0:T(4,128)(2,1)S(1)}, u32[]{:S(2)}, u32[]{:S(2)}) %collective-permute-start.2) | collective-permute-done | bytes 18464 | tf_op jit(solution)/shard_map/ppermute | solution.py:461
  45.5 0.0 collective-permute-done.4.att_far_ref
  45.5 0.0 copy-done.1
  45.5 0.0 copy-done.4
  45.5 5.1 %attention.1 = f32[576,128]{1,0:T(8,128)} custom-call(f32[8,128]{1,0:T(8,128)S(1)} %get-tuple-element.11.vectors_ref, bf16[4,4,576]{2,1,0:T(4,128)(2,1)S(1)} %collective-permute-done.2.bias_a_ref, bf16[4,4,576]{2,1,0:T(4,128)(2,1)S(1)} %collective-permute-done.3.bias_b_ref, bf16[576,128]{1,0:T(8,128)(2,1)S(1)} %get-tuple-element.15.att_ref, ...), custom_call_target="tpu_custom_call" | custom-call | tf_op jit(solution)/shard_map/attention/pallas_call | solution.py:462
  (2 shorter events, 0.0 us)
Async XLA Ops:
  17.1 6.6 %copy-start.5 = (bf16[128,4]{0,1:T(4,128)(2,1)S(1)}, bf16[128,4]{0,1:T(4,128)(2,1)}, u32[]{:S(2)}) copy-start(bf16[128,4]{0,1:T(4,128)(2,1)} %param.20) | copy-start | bytes 3076
  18.8 11.5 %copy-start = (f32[12,48,128]{2,1,0:T(8,128)S(1)}, f32[12,48,128]{2,1,0:T(8,128)}, u32[]{:S(2)}) copy-start(f32[12,48,128]{2,1,0:T(8,128)} %param.11) | copy-start | bytes 884740
  18.8 11.5 %copy-start.3 = (bf16[128,128]{1,0:T(8,128)(2,1)S(1)}, bf16[128,128]{1,0:T(8,128)(2,1)}, u32[]{:S(2)}) copy-start(bf16[128,128]{1,0:T(8,128)(2,1)} %gate_w_ref.1) | copy-start | bytes 98308
  18.8 11.5 %all-to-all-start.1 = ((bf16[16,5,8,128]{3,2,1,0:T(8,128)(2,1)}), bf16[16,5,8,128]{3,2,1,0:T(8,128)(2,1)S(1)}, u32[]{:S(2)}, u32[]{:S(2)}) async-start(bf16[16,5,8,128]{3,2,1,0:T(8,128)(2,1)} %triangle.1), calls=%async_computation.1 | async-start | bytes 327680 | tf_op jit(solution)/shard_map/all_to_all | solution.py:423
  23.7 6.6 %copy-start.2 = (bf16[128,128]{1,0:T(8,128)(2,1)S(1)}, bf16[128,128]{1,0:T(8,128)(2,1)}, u32[]{:S(2)}) copy-start(bf16[128,128]{1,0:T(8,128)(2,1)} %out_w_ref.2) | copy-start | bytes 98308
  30.3 15.3 %copy-start.1 = (bf16[128,4,128]{2,1,0:T(4,128)(2,1)S(1)}, bf16[128,4,128]{2,1,0:T(4,128)(2,1)}, u32[]{:S(2)}) copy-start(bf16[128,4,128]{2,1,0:T(4,128)(2,1)} %proj_w_ref.1) | copy-start | bytes 393220
  31.6 13.9 %copy-start.4 = (bf16[128,128]{1,0:T(8,128)(2,1)S(1)}, bf16[128,128]{1,0:T(8,128)(2,1)}, u32[]{:S(2)}) copy-start(bf16[128,128]{1,0:T(8,128)(2,1)} %out_w_ref.3) | copy-start | bytes 98308
  31.6 1.6 %collective-permute-start = (bf16[1,4,576]{2,1,0:T(4,128)(2,1)S(1)}, bf16[1,4,576]{2,1,0:T(4,128)(2,1)S(1)}, u32[]{:S(2)}, u32[]{:S(2)}) collective-permute-start(bf16[1,4,576]{2,1,0:T(4,128)(2,1)S(1)} %bitcast.9), channel_id=1, source_target_pairs={{0,2},{2,0},{4,6},{6,4},{8,10},{10,8},{12,14},{14,12},{1,3},{3,1},... | collective-permute-start | bytes 13832 | tf_op jit(solution)/shard_map/ppermute | solution.py:450
  31.7 13.8 %collective-permute-start.4 = (bf16[576,128]{1,0:T(8,128)(2,1)S(1)}, bf16[576,128]{1,0:T(8,128)(2,1)S(1)}, u32[]{:S(2)}, u32[]{:S(2)}) collective-permute-start(bf16[576,128]{1,0:T(8,128)(2,1)S(1)} %get-tuple-element.15.att_ref), channel_id=1, source_target_pairs={{0,1},{1,0},{2,3},{3,2},{4,5},{5,4},{6,7},{7,6},{8,9},{9,8},{10,11... | collective-permute-start | bytes 442376 | tf_op jit(solution)/shard_map/ppermute | solution.py:446
  33.2 3.7 %collective-permute-start.1 = (bf16[2,4,576]{2,1,0:T(4,128)(2,1)S(1)}, bf16[2,4,576]{2,1,0:T(4,128)(2,1)S(1)}, u32[]{:S(2)}, u32[]{:S(2)}) collective-permute-start(bf16[2,4,576]{2,1,0:T(4,128)(2,1)S(1)} %pad_maximum_fusion.1), channel_id=1, source_target_pairs={{0,4},{2,6},{4,0},{6,2},{8,12},{10,14},{12,8},{14,10},{1,5},{3,7},... | collective-permute-start | bytes 27656 | tf_op jit(solution)/shard_map/ppermute | solution.py:450
  37.0 4.7 %collective-permute-start.3 = (bf16[4,4,576]{2,1,0:T(4,128)(2,1)S(1)}, bf16[4,4,576]{2,1,0:T(4,128)(2,1)S(1)}, u32[]{:S(2)}, u32[]{:S(2)}) collective-permute-start(bf16[4,4,576]{2,1,0:T(4,128)(2,1)S(1)} %pad_maximum_fusion), channel_id=1, source_target_pairs={{1,0},{9,1},{3,2},{11,3},{5,4},{13,5},{7,6},{15,7},{0,8},{8,9},{2,... | collective-permute-start | bytes 55304 | tf_op jit(solution)/shard_map/ppermute | solution.py:461
  38.1 7.5 %collective-permute-start.2 = (bf16[4,4,576]{2,1,0:T(4,128)(2,1)S(1)}, bf16[4,4,576]{2,1,0:T(4,128)(2,1)S(1)}, u32[]{:S(2)}, u32[]{:S(2)}) collective-permute-start(bf16[4,4,576]{2,1,0:T(4,128)(2,1)S(1)} %pad_maximum_fusion), channel_id=1, source_target_pairs={{0,0},{8,1},{2,2},{10,3},{4,4},{12,5},{6,6},{14,7},{1,8},{9,9},{3,... | collective-permute-start | bytes 55304 | tf_op jit(solution)/shard_map/ppermute | solution.py:461

commit v3 on v2

--- a/solution.py
+++ b/solution.py
@@ -7,6 +7,7 @@
 from jax.experimental import pallas as pl
 from jax.experimental.pallas import tpu as pltpu
 from jax.sharding import PartitionSpec as P
+
 
 epsilon = 1e-05
 mask_penalty = 1000000000.0
@@ -45,7 +46,7 @@
     att_bias_weight,
     att_out_weight,
 ):
-    rows_here, cols_here, chan_here = pair.shape
+    rows_here, cols_here, _ = pair.shape
     residues = cols_here * lax.axis_size(("col", "sub"))
     row_offset = lax.axis_index("row") * rows_here
     col_offset = lax.axis_index(("col", "sub")) * cols_here
@@ -139,8 +140,15 @@
     return lax.dot_general(a, b, (((1,), (1,)), ((), ())), preferred_element_type=f32)
 
 
+kernel_params = pltpu.CompilerParams(vmem_limit_bytes=16 << 20)
+
+
 def near(v):
     return pltpu.with_memory_space_constraint(v, pltpu.VMEM)
+
+
+def afar(v):
+    return pltpu.with_memory_space_constraint(v, pltpu.HBM)
 
 
 def split_weight(w_ref, w_scratch):
@@ -161,7 +169,7 @@
     rows_ref,
     w_scratch,
 ):
-    cells, chan = pair_ref.shape
+    cells, _ = pair_ref.shape
     live = live_ref[...].astype(f32)
     rows_ref[0:1] = jnp.concatenate([live, jnp.zeros((1, LANES - live.shape[1]), f32)], axis=1)
     rows_ref[1:2] = out_gain_ref[...]
@@ -206,7 +214,7 @@
 def triangle_kernel(
     rows_here, cols_here, vectors_ref, lr_ref, sum_ref, left_scratch, right_scratch, sum_scratch
 ):
-    devices, panels_in, own, _ = lr_ref.shape
+    _, panels_in, own, _ = lr_ref.shape
     residues = left_scratch.shape[0]
     cols = residues // cols_here
     rows = residues // rows_here
@@ -263,11 +271,11 @@
     bias_ref,
 ):
     devices, tiles, own, _ = sum_ref.shape
-    cells, chan = pair_ref.shape
+    cells, _ = pair_ref.shape
     hidden = devices * own
     gain_col = jnp.transpose(jnp.broadcast_to(vectors_ref[1:2], (LANES, hidden)))
     gate = sigmoid(dot_nn(normed_ref[...], gate_w_ref[...]))
-    bias_w = jnp.transpose(bias_w_ref[...].astype(f32)).astype(bf16)
+    bias_w = bias_w_ref[...]
     for t in range(tiles):
         total = sum_ref[:, t].astype(f32).reshape(hidden, LANES)
         center = jnp.mean(total, axis=0, keepdims=True)
@@ -281,91 +289,98 @@
         mid_ref[low:high] = mid
         att = norm_last(mid, vectors_ref[2:3]).astype(bf16)
         att_ref[low:high] = att
-        bias_ref[:, low:high] = dot_nt(bias_w, att).astype(bf16)
+        bias_ref[0, :, low:high] = dot_nt(bias_w, att).astype(bf16)
+
+
+def own_kernel(heads, att_ref, w_ref, q_ref, k_ref, v_ref, gate_ref, kv_w_ref, w_scratch):
+    rows_here, cols_here, chan = att_ref.shape
+    width = w_ref.shape[2]
+    shape = (rows_here, cols_here, width)
+    att = att_ref[...].reshape(rows_here * cols_here, chan)
+    w = [m.astype(bf16) for m in split_weight(w_ref, w_scratch)]
+    kv_w_ref[0], kv_w_ref[1] = w[1], w[2]
+    q_ref[...] = (dot_nn(att, w[0]) * (width // heads) ** (-0.5)).astype(bf16).reshape(shape)
+    k_ref[...] = dot_nn(att, w[1]).astype(bf16).reshape(shape)
+    v_ref[...] = dot_nn(att, w[2]).astype(bf16).reshape(shape)
+    gate_ref[...] = sigmoid(dot_nn(att, w[3])).reshape(shape)
+
+
+def scores_kernel(heads, q_ref, k_ref, far_ref, kv_w_ref, scores_ref, v_far_ref):
+    rows_here, cols_here, width = q_ref.shape
+    far = far_ref[...].reshape(rows_here * cols_here, width)
+    k_far = dot_nn(far, kv_w_ref[0]).astype(bf16).reshape(q_ref.shape)
+    v_far_ref[...] = dot_nn(far, kv_w_ref[1]).astype(bf16).reshape(q_ref.shape)
+    head_of = lax.broadcasted_iota(jnp.int32, (cols_here, width), 1) // (width // heads)
+    for i in range(rows_here):
+        q = q_ref[i]
+        q_heads = jnp.concatenate(
+            [jnp.where(head_of == h, q, jnp.zeros_like(q)) for h in range(heads)], axis=0
+        )
+        scores_ref[i] = dot_nt(q_heads, jnp.concatenate([k_ref[i], k_far[i]], axis=0))
 
 
 def attention_kernel(
-    rows_here,
     vectors_ref,
-    bias_a_ref,
-    bias_b_ref,
-    att_ref,
-    att_far_ref,
+    fetched_ref,
+    swapped_ref,
+    scores_ref,
+    v_ref,
+    v_far_ref,
+    gate_ref,
     mid_ref,
-    proj_w_ref,
     out_w_ref,
     out_ref,
-    w_scratch,
     bias_scratch,
 ):
-    cells, chan = att_ref.shape
-    cols_here = cells // rows_here
-    blocks, heads, _ = bias_a_ref.shape
+    rows_here, cols_here, width = v_ref.shape
+    blocks, heads, cells = fetched_ref.shape
     residues = 2 * cols_here
-    width = proj_w_ref.shape[2]
-    size = width // heads
     row, col = lax.axis_index("row"), lax.axis_index(("col", "sub"))
-    block_at = lax.rem(row, blocks)
-    same = (lax.div(row, blocks) == col).astype(jnp.int32)
+    same = jnp.bitwise_and(row, 1) == col
+    chip = lax.div(row, 2)
     lane_row = lax.broadcasted_iota(jnp.int32, (1, LANES), 1)
-    live_wide = vectors_ref[0:1]
+    live = vectors_ref[0:1]
     swapped = jnp.where(
         lane_row < cols_here,
-        pltpu.roll(live_wide, LANES - cols_here, 1),
-        pltpu.roll(live_wide, cols_here, 1),
-    )
-    live_order = jnp.where(col == 0, live_wide, swapped)
-    penalty = (live_order - 1.0) * mask_penalty
+        pltpu.roll(live, LANES - cols_here, 1),
+        pltpu.roll(live, cols_here, 1),
+    )
+    penalty = (jnp.where(col == 0, live, swapped) - 1.0) * mask_penalty
     lane = lax.broadcasted_iota(jnp.int32, (heads, LANES), 1)
     pad = (-cells) % LANES
 
     def panels(v):
-        v = v.astype(f32)
         v = jnp.concatenate([v, jnp.zeros((heads, pad), f32)], axis=1) if pad else v
         return [v[:, t * LANES : (t + 1) * LANES] for t in range((cells + pad) // LANES)]
 
     for m in range(blocks):
-        first, second = bias_a_ref[m].astype(f32), bias_b_ref[m].astype(f32)
-        mine = panels(jnp.where(same == 1, first, second))
-        far = panels(jnp.where(same == 1, second, first))
-        base = jnp.bitwise_xor(block_at, m) * rows_here
+        p, n = m // 2, m % 2
+        block = 2 * jnp.bitwise_xor(jnp.bitwise_and(chip, 1), p)
+        block = block + jnp.bitwise_xor(n, lax.div(chip, 2))
+        first, second = fetched_ref[m].astype(f32), swapped_ref[m].astype(f32)
+        mine = panels(jnp.where(same, first, second))
+        other = panels(jnp.where(same, second, first))
         for j in range(rows_here):
-            line = jnp.where(
+            bias_scratch[block * rows_here + j] = jnp.where(
                 lane < cols_here,
                 segment(mine, j * cols_here, 0),
-                segment(far, j * cols_here, cols_here),
+                segment(other, j * cols_here, cols_here),
             )
-            bias_scratch[base + j] = line
     penalty = penalty[:, :residues]
     head_bias = [bias_scratch[:, h, :][:, :residues] + penalty for h in range(heads)]
     head_bias = jnp.concatenate(head_bias, axis=0)
-
-    w = [m.astype(bf16) for m in split_weight(proj_w_ref, w_scratch)]
-    att, att_far = att_ref[...], att_far_ref[...]
-    queries = (dot_nn(att, w[0]) * size ** (-0.5)).astype(bf16)
-    keys = dot_nn(att, w[1]).astype(bf16)
-    values = dot_nn(att, w[2]).astype(bf16)
-    keys_far = dot_nn(att_far, w[1]).astype(bf16)
-    values_far = dot_nn(att_far, w[2]).astype(bf16)
-    gate = sigmoid(dot_nn(att, w[3]))
-    head_of = lax.broadcasted_iota(jnp.int32, (cols_here, width), 1) // size
+    head_of = lax.broadcasted_iota(jnp.int32, (cols_here, width), 1) // (width // heads)
     for i in range(rows_here):
-        at = slice(i * cols_here, (i + 1) * cols_here)
-        q = queries[at]
-        q_heads = jnp.concatenate(
-            [jnp.where(head_of == h, q, jnp.zeros_like(q)) for h in range(heads)], axis=0
-        )
-        k = jnp.concatenate([keys[at], keys_far[at]], axis=0)
-        v = jnp.concatenate([values[at], values_far[at]], axis=0)
-        scores = dot_nt(q_heads, k) + head_bias
+        v = jnp.concatenate([v_ref[i], v_far_ref[i]], axis=0)
+        scores = scores_ref[i] + head_bias
         raised = jnp.exp(scores - jnp.max(scores, axis=-1, keepdims=True))
         weights = (raised / jnp.sum(raised, axis=-1, keepdims=True)).astype(bf16)
         mixed = dot_nn(weights, v)
         attended = mixed[:cols_here]
         for h in range(1, heads):
             attended = jnp.where(head_of == h, mixed[h * cols_here : (h + 1) * cols_here], attended)
-        gated = (attended * gate[at]).astype(bf16)
-        out_ref[at] = mid_ref[at] + dot_nn(gated, out_w_ref[...])
+        gated = (attended * gate_ref[i]).astype(bf16)
+        out_ref[i] = mid_ref[i] + dot_nn(gated, out_w_ref[...])
 
 
 def body_channels(
@@ -390,7 +405,6 @@
     hidden = tri_in_weight.shape[2]
     own = hidden // devices
     heads = att_bias_weight.shape[1]
-    blocks = rows // cols
     tiles = -(-cells // LANES)
     lr_panels = -(-2 * cells // LANES) if (-cells) % LANES * 2 == LANES else 2 * tiles
     flat = pair.reshape(cells, chan)
@@ -404,30 +418,39 @@
             pltpu.VMEM((8, LANES), f32),
         ),
         scratch_shapes=[pltpu.VMEM(tri_in_weight.shape, f32)],
+        compiler_params=kernel_params,
         name="factors",
     )(
-        flat,
-        tri_norm_gain.reshape(1, chan),
-        tri_in_weight,
-        live,
-        tri_out_norm_gain.reshape(1, hidden),
-        att_norm_gain.reshape(1, chan),
+        *map(
+            afar,
+            (
+                flat,
+                tri_norm_gain.reshape(1, chan),
+                tri_in_weight,
+                live,
+                tri_out_norm_gain.reshape(1, hidden),
+                att_norm_gain.reshape(1, chan),
+            ),
+        )
     )
     lr = lax.all_to_all(lr, group, 0, 0, tiled=True)
     sums = pl.pallas_call(
         functools.partial(triangle_kernel, rows_here, cols_here),
         out_shape=pltpu.VMEM((devices, tiles, own, LANES), bf16),
         scratch_shapes=[pltpu.VMEM((residues, own, LANES), f32) for _ in range(3)],
+        compiler_params=kernel_params,
         name="triangle",
     )(near(vectors), near(lr))
     sums = lax.all_to_all(sums, group, 0, 0, tiled=True)
+    shape = (rows_here, cols_here, chan)
     mid, att, bias = pl.pallas_call(
         middle_kernel,
         out_shape=(
             pltpu.VMEM((cells, chan), f32),
             pltpu.VMEM((cells, chan), bf16),
-            pltpu.VMEM((heads, cells), bf16),
+            pltpu.VMEM((1, heads, cells), bf16),
         ),
+        compiler_params=kernel_params,
         name="middle",
     )(
         *map(
@@ -439,36 +462,58 @@
                 vectors,
                 tri_out_weight,
                 tri_gate_weight,
-                att_bias_weight,
+                att_bias_weight.T,
             ),
         )
     )
-    att_far = lax.ppermute(att, ("col", "sub"), [(c, c ^ 1) for c in range(cols)])
-    held = bias[None]
-    step = 1
-    while step < blocks:
-        other = lax.ppermute(held, "row", [(r, r ^ step) for r in range(rows)])
-        held = jnp.concatenate([held, other], axis=0)
-        step *= 2
-    spread = []
-    for shift in range(cols):
+    att, mid = att.reshape(shape), mid.reshape(shape)
+
+    def swap(v):
+        return lax.ppermute(v, "row", [(r, r ^ 1) for r in range(rows)])
+
+    joined = swap(bias)
+    bias = jnp.concatenate([bias, joined], axis=0)
+    fetched = []
+    for p in range(2):
         pairs = []
-        for part in range(cols):
-            for q in range(blocks):
-                for c in range(cols):
-                    source = (c * blocks + q) * cols + (part + shift) % cols
-                    pairs.append((source, (part * blocks + q) * cols + c))
-        spread.append(lax.ppermute(held, group, pairs))
-    out = pl.pallas_call(
-        functools.partial(attention_kernel, rows_here),
-        out_shape=jax.ShapeDtypeStruct((cells, chan), f32),
-        scratch_shapes=[
-            pltpu.VMEM(att_proj_weight.shape, f32),
-            pltpu.VMEM((cols_here, heads, LANES), f32),
-        ],
+        for z in range(rows // 2):
+            for s in range(2):
+                for x in range(cols):
+                    target = (2 * s + ((z & 1) ^ p)) * 2 + x
+                    pairs.append(((2 * z + s) * cols + x, target * cols + (z >> 1)))
+        fetched.append(lax.ppermute(bias, group, pairs))
+    far = lax.ppermute(att, ("col", "sub"), [(c, c ^ 1) for c in range(cols)])
+    queries, keys, values, gate, kv_weight = pl.pallas_call(
+        functools.partial(own_kernel, heads),
+        out_shape=(
+            pltpu.VMEM(shape, bf16),
+            pltpu.VMEM(shape, bf16),
+            pltpu.VMEM(shape, bf16),
+            pltpu.VMEM(shape, f32),
+            pltpu.VMEM((2, chan, chan), bf16),
+        ),
+        scratch_shapes=[pltpu.VMEM(att_proj_weight.shape, f32)],
+        compiler_params=kernel_params,
+        name="own",
+    )(near(att), near(att_proj_weight))
+    fetched = jnp.concatenate(fetched, axis=0)
+    swapped = swap(fetched)
+    scores, values_far = pl.pallas_call(
+        functools.partial(scores_kernel, heads),
+        out_shape=(
+            pltpu.VMEM((rows_here, heads * cols_here, residues), f32),
+            pltpu.VMEM(shape, bf16),
+        ),
+        compiler_params=kernel_params,
+        name="scores",
+    )(*map(near, (queries, keys, far, kv_weight)))
+    return pl.pallas_call(
+        attention_kernel,
+        out_shape=jax.ShapeDtypeStruct(shape, f32),
+        scratch_shapes=[pltpu.VMEM((cols_here, heads, LANES), f32)],
+        compiler_params=kernel_params,
         name="attention",
-    )(*map(near, (vectors, *spread, att, att_far, mid, att_proj_weight, att_out_weight)))
-    return out.reshape(pair.shape)
+    )(*map(near, (vectors, fetched, swapped, scores, values, values_far, gate, mid, att_out_weight)))
 
 
 def solution(mesh):
@@ -491,8 +536,7 @@
         hidden = tri_in_weight.shape[2]
         fits = (
             cols == 2
-            and rows % cols == 0
-            and (rows // cols) & (rows // cols - 1) == 0
+            and rows == 8
             and hidden % (8 * rows * cols) == 0
             and hidden == pair.shape[2] == LANES
             and residue_mask.shape[0] <= LANES

time: 50.9 us -> 46.4 us (0.912); the launches traced: 50.7 us -> 45.6 us
  blocking collectives: 15.4 us -> 26.3 us
  waiting for transfers between devices: 13.3 us -> 4.94 us
  starting transfers between devices: 11.9 us -> 6.15 us
  Pallas kernels: 9.8 us -> 7.99 us
    all_to_all x0 -> x1, blocking collectives: none -> 10.9 us  [body_channels(): sums = lax.all_to_all(sums, group, 0, 0, tiled=True)]
    all_to_all x1 -> x0, waiting for transfers between devices: 6.45 us -> none  [body_channels(): sums = lax.all_to_all(sums, group, 0, 0, tiled=True)]
    all_to_all x1 -> x0, starting transfers between devices: 4.9 us -> none  [body_channels(): sums = lax.all_to_all(sums, group, 0, 0, tiled=True)]
    ppermute x5, waiting for transfers between devices: 6.87 us -> 4.94 us  [the longest x2 3.74 us: body_channels(): fetched.append(lax.ppermute(bias, group, pairs))]
    pallas_call x1 -> x3, Pallas kernels: 5.14 us -> 3.96 us  [the longest x1 2.96 us: body_channels(): pl.pallas_call(attention_kernel, out_shape=jax.ShapeDtypeStruct(shape, f3...]
    ppermute x5, starting transfers between devices: 7.02 us -> 6.15 us  [the longest x2 5.89 us: body_channels(): fetched.append(lax.ppermute(bias, group, pairs))]
    pallas_call x1, Pallas kernels: 1.68 us -> 1.02 us  [body_channels(): pl.pallas_call(functools.partial(triangle_kernel, rows_here, cols_here),...]
  transfers between devices with their start and end apart: 6 -> 5, of which waited for: 4 -> 4; matrix products, arithmetic and copies ran while one was open for 0% -> 0% of each run, Pallas kernels for 0% -> 2%
where the time goes in v3:
time: 46.4 us; the launch traced here: 45.6 us
  blocking collectives  26.3 us (57%)
  Pallas kernels  7.99 us (17%)
  starting transfers between devices  6.15 us (13%)
  waiting for transfers between devices  4.94 us (11%)
    all_to_all x1, blocking collectives, body_channels(): lr = lax.all_to_all(lr, group, 0, 0, tiled=True)  15.4 us
    all_to_all x1, blocking collectives, body_channels(): sums = lax.all_to_all(sums, group, 0, 0, tiled=True)  10.9 us
    ppermute x2, starting transfers between devices, body_channels(): fetched.append(lax.ppermute(bias, group, pairs))  5.89 us
    ppermute x2, waiting for transfers between devices, body_channels(): fetched.append(lax.ppermute(bias, group, pairs))  3.74 us
    pallas_call x1, Pallas kernels, body_channels(): pl.pallas_call(attention_kernel, out_shape=jax.ShapeDtypeStruct(shape, f3...  2.96 us
    pallas_call x1, Pallas kernels, body_channels(): pl.pallas_call(functools.partial(factors_kernel, devices), out_shape=(plt...  1.72 us
    pallas_call x1, Pallas kernels, body_channels(): pl.pallas_call(middle_kernel, out_shape=(pltpu.VMEM((cells, chan), f32),...  1.29 us
    ppermute x2, waiting for transfers between devices, swap(): return lax.ppermute(v, 'row', [(r, r ^ 1) for r in range(rows)])  1.2 us
  transfers between devices with their start and end apart: 5, of which 4 were waited for; matrix products, arithmetic and copies ran while one was open for 0% of the time, Pallas kernels for 2%

profile of v3, /device:TPU:6, one launch (start us, length us, event | category | flops | bytes accessed | tf_op | source)
XLA Modules:
  0.0 45.6 jit_solution(5558447588116650453)
XLA Ops:
  0.0 0.0 copy-start
  0.0 0.0 copy-start.5
  0.0 0.0 copy-start.4
  0.0 0.0 copy-start.3
  0.0 0.0 copy-start.1
  0.0 1.7 %factors.1 = (bf16[16,9,8,128]{3,2,1,0:T(8,128)(2,1)S(1)}, bf16[576,128]{1,0:T(8,128)(2,1)S(1)}, f32[8,128]{1,0:T(8,128)S(1)}) custom-call(f32[576,128]{1,0:T(8,128)} %bitcast.8, f32[1,128]{1,0:T(1,128)} %bitcast.14, bf16[128,4,128]{2,1,0:T(4,128)(2,1)} %w_ref.2, s32[1,96]{1,0:T(1,128)} %bitcast.15, f32[1,128]{1,0:T(1,128)} %bitcast.16, f32[1,128]{1,0:T(1,128)} %bitcast.17), custom_call_target="tpu_custom_call" | custom-call | tf_op jit(solution)/shard_map/factors/pallas_call | solution.py:413
  1.8 15.4 %all_to_all.10.lr_ref = bf16[16,9,8,128]{3,2,1,0:T(8,128)(2,1)S(1)} all-to-all(bf16[16,9,8,128]{3,2,1,0:T(8,128)(2,1)S(1)} %get-tuple-element.20), channel_id=1, replica_groups=mesh['parts'=2,'row'=8,'col'=2,'sub'=1] {'row','col','sub'}, dimensions={0} | all-to-all | bytes 589824 | tf_op jit(solution)/shard_map/all_to_all | solution.py:436
  17.1 0.0 copy-start.2
  17.1 1.0 %triangle.1 = bf16[16,5,8,128]{3,2,1,0:T(8,128)(2,1)S(1)} custom-call(f32[8,128]{1,0:T(8,128)S(1)} %get-tuple-element.18.vectors_ref, bf16[16,9,8,128]{3,2,1,0:T(8,128)(2,1)S(1)} %all_to_all.10.lr_ref), custom_call_target="tpu_custom_call" | custom-call | tf_op jit(solution)/shard_map/triangle/pallas_call | solution.py:437
  18.2 10.9 %all_to_all.11.sum_ref = bf16[16,5,8,128]{3,2,1,0:T(8,128)(2,1)S(1)} all-to-all(bf16[16,5,8,128]{3,2,1,0:T(8,128)(2,1)S(1)} %triangle.1), channel_id=1, replica_groups=mesh['parts'=2,'row'=8,'col'=2,'sub'=1] {'row','col','sub'}, dimensions={0} | all-to-all | bytes 327680 | tf_op jit(solution)/shard_map/all_to_all | solution.py:444
  29.1 0.0 copy-done
  29.1 0.0 copy-done.5
  29.1 0.0 copy-done.4
  29.1 0.0 copy-done.3
  29.1 1.3 %middle.1 = (f32[576,128]{1,0:T(8,128)S(1)}, bf16[576,128]{1,0:T(8,128)(2,1)S(1)}, bf16[1,4,576]{2,1,0:T(4,128)(2,1)S(1)}) custom-call(f32[576,128]{1,0:T(8,128)S(1)} %bitcast.9, bf16[576,128]{1,0:T(8,128)(2,1)S(1)} %get-tuple-element.19.normed_ref, bf16[16,5,8,128]{3,2,1,0:T(8,128)(2,1)S(1)} %all_to_all.11.sum_ref, ...), custom_call_target="tpu_custom_call" | custom-call | tf_op jit(solution)/shard_map/middle/pallas_call | solution.py:446
  30.4 0.1 collective-permute-start
  30.6 1.1 %collective-permute-done = bf16[1,4,576]{2,1,0:T(4,128)(2,1)S(1)} collective-permute-done((bf16[1,4,576]{2,1,0:T(4,128)(2,1)S(1)}, bf16[1,4,576]{2,1,0:T(4,128)(2,1)S(1)}, u32[]{:S(2)}, u32[]{:S(2)}) %collective-permute-start) | collective-permute-done | bytes 4640 | tf_op jit(solution)/shard_map/ppermute | solution.py:472
  31.6 3.1 %collective-permute-start.1 = (bf16[2,4,576]{2,1,0:T(4,128)(2,1)S(1)}, bf16[2,4,576]{2,1,0:T(4,128)(2,1)S(1)}, u32[]{:S(2)}, u32[]{:S(2)}) collective-permute-start(bf16[2,4,576]{2,1,0:T(4,128)(2,1)S(1)} %constant_dynamic-update-slice_fusion), channel_id=1, source_target_pairs={{0,0},{1,2},{2,8},{3,10},{4,4},{5,6},{6,12},{7,14},{8,1},{9,3},{10... | collective-permute-start | bytes 27656 | tf_op jit(solution)/shard_map/ppermute | solution.py:484
  34.8 0.1 collective-permute-start.4
  34.8 2.8 %collective-permute-start.2 = (bf16[2,4,576]{2,1,0:T(4,128)(2,1)S(1)}, bf16[2,4,576]{2,1,0:T(4,128)(2,1)S(1)}, u32[]{:S(2)}, u32[]{:S(2)}) collective-permute-start(bf16[2,4,576]{2,1,0:T(4,128)(2,1)S(1)} %constant_dynamic-update-slice_fusion), channel_id=1, source_target_pairs={{0,4},{1,6},{2,12},{3,14},{4,0},{5,2},{6,8},{7,10},{8,5},{9,7},{10... | collective-permute-start | bytes 27656 | tf_op jit(solution)/shard_map/ppermute | solution.py:484
  37.6 1.5 %collective-permute-done.1 = bf16[2,4,576]{2,1,0:T(4,128)(2,1)S(1)} collective-permute-done((bf16[2,4,576]{2,1,0:T(4,128)(2,1)S(1)}, bf16[2,4,576]{2,1,0:T(4,128)(2,1)S(1)}, u32[]{:S(2)}, u32[]{:S(2)}) %collective-permute-start.1) | collective-permute-done | bytes 9248 | tf_op jit(solution)/shard_map/ppermute | solution.py:484
  39.1 2.3 %collective-permute-done.2 = bf16[2,4,576]{2,1,0:T(4,128)(2,1)S(1)} collective-permute-done((bf16[2,4,576]{2,1,0:T(4,128)(2,1)S(1)}, bf16[2,4,576]{2,1,0:T(4,128)(2,1)S(1)}, u32[]{:S(2)}, u32[]{:S(2)}) %collective-permute-start.2) | collective-permute-done | bytes 9248 | tf_op jit(solution)/shard_map/ppermute | solution.py:484
  41.4 0.1 collective-permute-start.3
  41.4 0.0 copy-done.1
  41.4 0.5 %own.1 = (bf16[12,48,128]{2,1,0:T(8,128)(2,1)S(1)}, bf16[12,48,128]{2,1,0:T(8,128)(2,1)S(1)}, bf16[12,48,128]{2,1,0:T(8,128)(2,1)S(1)}, f32[12,48,128]{2,1,0:T(8,128)S(1)}, bf16[2,128,128]{2,1,0:T(8,128)(2,1)S(1)}) custom-call(bf16[12,48,128]{2,1,0:T(8,128)(2,1)S(1)} %bitcast.12, bf16[128,4,128]{2,1,0:T(4,128)(2,1)S(1)} %copy-done.1), custom_call_target="tpu_custom_call" | custom-call | tf_op jit(solution)/shard_map/own/pallas_call | solution.py:486
  42.0 0.0 collective-permute-done.4.far_ref
  42.0 0.5 %scores.1 = (f32[12,192,96]{2,1,0:T(8,128)S(1)}, bf16[12,48,128]{2,1,0:T(8,128)(2,1)S(1)}) custom-call(bf16[12,48,128]{2,1,0:T(8,128)(2,1)S(1)} %get-tuple-element.23.q_ref, bf16[12,48,128]{2,1,0:T(8,128)(2,1)S(1)} %get-tuple-element.24.k_ref, bf16[12,48,128]{2,1,0:T(8,128)(2,1)S(1)} %collective-permute-done.4.far_ref, ...), custom_call_target="tpu_custom_call" | custom-call | tf_op jit(solution)/shard_map/scores/pallas_call | solution.py:501
  42.5 0.1 collective-permute-done.3.swapped_ref
  42.6 0.0 copy-done.2
  42.6 3.0 %attention.1 = f32[12,48,128]{2,1,0:T(8,128)} custom-call(f32[8,128]{1,0:T(8,128)S(1)} %get-tuple-element.18.vectors_ref, bf16[4,4,576]{2,1,0:T(4,128)(2,1)S(1)} %constant_dynamic-update-slice_fusion.2.fetched_ref, bf16[4,4,576]{2,1,0:T(4,128)(2,1)S(1)} %collective-permute-done.3.swapped_ref, f32[12,192,96]{2,1,0:T(8,128)S(1)} %get-tuple-element.26.scores_ref, ...), custom_call_target="tpu_custom_call" | custom-call | tf_op jit(solution)/shard_map/attention/pallas_call | solution.py:510
  (4 shorter events, 0.0 us)
Async XLA Ops:
  0.0 29.1 %copy-start = (f32[12,48,128]{2,1,0:T(8,128)S(1)}, f32[12,48,128]{2,1,0:T(8,128)}, u32[]{:S(2)}) copy-start(f32[12,48,128]{2,1,0:T(8,128)} %param.11) | copy-start | bytes 884740
  0.0 29.1 %copy-start.5 = (bf16[128,4]{0,1:T(4,128)(2,1)S(1)}, bf16[128,4]{0,1:T(4,128)(2,1)}, u32[]{:S(2)}) copy-start(bf16[128,4]{0,1:T(4,128)(2,1)} %param.20) | copy-start | bytes 3076
  0.0 29.1 %copy-start.4 = (bf16[128,128]{1,0:T(8,128)(2,1)S(1)}, bf16[128,128]{1,0:T(8,128)(2,1)}, u32[]{:S(2)}) copy-start(bf16[128,128]{1,0:T(8,128)(2,1)} %gate_w_ref.1) | copy-start | bytes 98308
  0.0 29.1 %copy-start.3 = (bf16[128,128]{1,0:T(8,128)(2,1)S(1)}, bf16[128,128]{1,0:T(8,128)(2,1)}, u32[]{:S(2)}) copy-start(bf16[128,128]{1,0:T(8,128)(2,1)} %out_w_ref.2) | copy-start | bytes 98308
  0.0 41.4 %copy-start.1 = (bf16[128,4,128]{2,1,0:T(4,128)(2,1)S(1)}, bf16[128,4,128]{2,1,0:T(4,128)(2,1)}, u32[]{:S(2)}) copy-start(bf16[128,4,128]{2,1,0:T(4,128)(2,1)} %w_ref.3) | copy-start | bytes 393220
  17.1 25.5 %copy-start.2 = (bf16[128,128]{1,0:T(8,128)(2,1)S(1)}, bf16[128,128]{1,0:T(8,128)(2,1)}, u32[]{:S(2)}) copy-start(bf16[128,128]{1,0:T(8,128)(2,1)} %out_w_ref.3) | copy-start | bytes 98308
  30.4 1.2 %collective-permute-start = (bf16[1,4,576]{2,1,0:T(4,128)(2,1)S(1)}, bf16[1,4,576]{2,1,0:T(4,128)(2,1)S(1)}, u32[]{:S(2)}, u32[]{:S(2)}) collective-permute-start(bf16[1,4,576]{2,1,0:T(4,128)(2,1)S(1)} %get-tuple-element.21), channel_id=1, source_target_pairs={{0,2},{2,0},{4,6},{6,4},{8,10},{10,8},{12,14},{14,12},{1,3},{3,1},... | collective-permute-start | bytes 13832 | tf_op jit(solution)/shard_map/ppermute | solution.py:472
  31.6 7.5 %collective-permute-start.1 = (bf16[2,4,576]{2,1,0:T(4,128)(2,1)S(1)}, bf16[2,4,576]{2,1,0:T(4,128)(2,1)S(1)}, u32[]{:S(2)}, u32[]{:S(2)}) collective-permute-start(bf16[2,4,576]{2,1,0:T(4,128)(2,1)S(1)} %constant_dynamic-update-slice_fusion), channel_id=1, source_target_pairs={{0,0},{1,2},{2,8},{3,10},{4,4},{5,6},{6,12},{7,14},{8,1},{9,3},{10... | collective-permute-start | bytes 27656 | tf_op jit(solution)/shard_map/ppermute | solution.py:484
  34.8 7.2 %collective-permute-start.4 = (bf16[12,48,128]{2,1,0:T(8,128)(2,1)S(1)}, bf16[12,48,128]{2,1,0:T(8,128)(2,1)S(1)}, u32[]{:S(2)}, u32[]{:S(2)}) collective-permute-start(bf16[12,48,128]{2,1,0:T(8,128)(2,1)S(1)} %bitcast.11), channel_id=1, source_target_pairs={{0,1},{1,0},{2,3},{3,2},{4,5},{5,4},{6,7},{7,6},{8,9},{9,8},{10,11... | collective-permute-start | bytes 442376 | tf_op jit(solution)/shard_map/ppermute | solution.py:485
  34.8 6.5 %collective-permute-start.2 = (bf16[2,4,576]{2,1,0:T(4,128)(2,1)S(1)}, bf16[2,4,576]{2,1,0:T(4,128)(2,1)S(1)}, u32[]{:S(2)}, u32[]{:S(2)}) collective-permute-start(bf16[2,4,576]{2,1,0:T(4,128)(2,1)S(1)} %constant_dynamic-update-slice_fusion), channel_id=1, source_target_pairs={{0,4},{1,6},{2,12},{3,14},{4,0},{5,2},{6,8},{7,10},{8,5},{9,7},{10... | collective-permute-start | bytes 27656 | tf_op jit(solution)/shard_map/ppermute | solution.py:484
  41.4 1.3 %collective-permute-start.3 = (bf16[4,4,576]{2,1,0:T(4,128)(2,1)S(1)}, bf16[4,4,576]{2,1,0:T(4,128)(2,1)S(1)}, u32[]{:S(2)}, u32[]{:S(2)}) collective-permute-start(bf16[4,4,576]{2,1,0:T(4,128)(2,1)S(1)} %constant_dynamic-update-slice_fusion.2.fetched_ref), channel_id=1, source_target_pairs={{0,2},{2,0},{4,6},{6,4},{8,10},{10,8},{12,14},{14,12},{1,3},{3,1},... | collective-permute-start | bytes 55304 | tf_op jit(solution)/shard_map/ppermute | solution.py:472

commit v4 on v3

--- a/solution.py
+++ b/solution.py
@@ -276,20 +276,20 @@
     gain_col = jnp.transpose(jnp.broadcast_to(vectors_ref[1:2], (LANES, hidden)))
     gate = sigmoid(dot_nn(normed_ref[...], gate_w_ref[...]))
     bias_w = bias_w_ref[...]
+    hidden_rows = []
     for t in range(tiles):
         total = sum_ref[:, t].astype(f32).reshape(hidden, LANES)
         center = jnp.mean(total, axis=0, keepdims=True)
         centered = total - center
         variance = jnp.mean(centered * centered, axis=0, keepdims=True)
         hidden_normed = centered * lax.rsqrt(variance + epsilon) * gain_col
-        hidden_rows = jnp.transpose(hidden_normed).astype(bf16)
-        low, high = t * LANES, min((t + 1) * LANES, cells)
-        update = dot_nn(hidden_rows[: high - low], out_w_ref[...])
-        mid = pair_ref[low:high] + gate[low:high] * update
-        mid_ref[low:high] = mid
-        att = norm_last(mid, vectors_ref[2:3]).astype(bf16)
-        att_ref[low:high] = att
-        bias_ref[0, :, low:high] = dot_nt(bias_w, att).astype(bf16)
+        hidden_rows.append(jnp.transpose(hidden_normed).astype(bf16))
+    hidden_rows = jnp.concatenate(hidden_rows, axis=0)[:cells]
+    mid = pair_ref[...] + gate * dot_nn(hidden_rows, out_w_ref[...])
+    mid_ref[...] = mid
+    att = norm_last(mid, vectors_ref[2:3]).astype(bf16)
+    att_ref[...] = att
+    bias_ref[0] = dot_nt(bias_w, att).astype(bf16)
 
 
 def own_kernel(heads, att_ref, w_ref, q_ref, k_ref, v_ref, gate_ref, kv_w_ref, w_scratch):
@@ -331,8 +331,11 @@
     out_w_ref,
     out_ref,
     bias_scratch,
+    result,
+    done,
 ):
     rows_here, cols_here, width = v_ref.shape
+    chunks = done.shape[0]
     blocks, heads, cells = fetched_ref.shape
     residues = 2 * cols_here
     row, col = lax.axis_index("row"), lax.axis_index(("col", "sub"))
@@ -355,8 +358,8 @@
 
     for m in range(blocks):
         p, n = m // 2, m % 2
-        block = 2 * jnp.bitwise_xor(jnp.bitwise_and(chip, 1), p)
-        block = block + jnp.bitwise_xor(n, lax.div(chip, 2))
+        block = 2 * jnp.bitwise_xor(lax.div(chip, 2), 1 - p)
+        block = block + jnp.bitwise_xor(n, jnp.bitwise_and(chip, 1))
         first, second = fetched_ref[m].astype(f32), swapped_ref[m].astype(f32)
         mine = panels(jnp.where(same, first, second))
         other = panels(jnp.where(same, second, first))
@@ -370,17 +373,29 @@
     head_bias = [bias_scratch[:, h, :][:, :residues] + penalty for h in range(heads)]
     head_bias = jnp.concatenate(head_bias, axis=0)
     head_of = lax.broadcasted_iota(jnp.int32, (cols_here, width), 1) // (width // heads)
-    for i in range(rows_here):
-        v = jnp.concatenate([v_ref[i], v_far_ref[i]], axis=0)
-        scores = scores_ref[i] + head_bias
-        raised = jnp.exp(scores - jnp.max(scores, axis=-1, keepdims=True))
-        weights = (raised / jnp.sum(raised, axis=-1, keepdims=True)).astype(bf16)
-        mixed = dot_nn(weights, v)
-        attended = mixed[:cols_here]
-        for h in range(1, heads):
-            attended = jnp.where(head_of == h, mixed[h * cols_here : (h + 1) * cols_here], attended)
-        gated = (attended * gate_ref[i]).astype(bf16)
-        out_ref[i] = mid_ref[i] + dot_nn(gated, out_w_ref[...])
+    ones = jnp.ones((residues, width), bf16)
+    chunk = rows_here // chunks
+    copies = []
+    for c in range(chunks):
+        gated = []
+        for i in range(c * chunk, (c + 1) * chunk):
+            v = jnp.concatenate([v_ref[i], v_far_ref[i]], axis=0)
+            scores = scores_ref[i] + head_bias
+            raised = jnp.exp(scores - jnp.max(scores, axis=-1, keepdims=True)).astype(bf16)
+            mixed = dot_nn(raised, jnp.concatenate([v, ones], axis=1))
+            attended = mixed[:cols_here]
+            for h in range(1, heads):
+                part = mixed[h * cols_here : (h + 1) * cols_here]
+                attended = jnp.where(jnp.tile(head_of, (1, 2)) == h, part, attended)
+            attended = attended[:, :width] / attended[:, width:]
+            gated.append((attended * gate_ref[i]).astype(bf16))
+        update = dot_nn(jnp.concatenate(gated, axis=0), out_w_ref[...])
+        at = slice(c * chunk, (c + 1) * chunk)
+        result[at] = mid_ref[at] + update.reshape(chunk, cols_here, width)
+        copies.append(pltpu.make_async_copy(result.at[at], out_ref.at[at], done.at[c]))
+        copies[-1].start()
+    for copy in copies:
+        copy.wait()
 
 
 def body_channels(
@@ -443,6 +458,7 @@
     )(near(vectors), near(lr))
     sums = lax.all_to_all(sums, group, 0, 0, tiled=True)
     shape = (rows_here, cols_here, chan)
+    chunks = math.gcd(rows_here, 3)
     mid, att, bias = pl.pallas_call(
         middle_kernel,
         out_shape=(
@@ -479,7 +495,7 @@
         for z in range(rows // 2):
             for s in range(2):
                 for x in range(cols):
-                    target = (2 * s + ((z & 1) ^ p)) * 2 + x
+                    target = (2 * ((z & 1) ^ 1 ^ p) + s) * 2 + x
                     pairs.append(((2 * z + s) * cols + x, target * cols + (z >> 1)))
         fetched.append(lax.ppermute(bias, group, pairs))
     far = lax.ppermute(att, ("col", "sub"), [(c, c ^ 1) for c in range(cols)])
@@ -510,7 +526,12 @@
     return pl.pallas_call(
         attention_kernel,
         out_shape=jax.ShapeDtypeStruct(shape, f32),
-        scratch_shapes=[pltpu.VMEM((cols_here, heads, LANES), f32)],
+        out_specs=pl.BlockSpec(memory_space=pltpu.HBM),
+        scratch_shapes=[
+            pltpu.VMEM((cols_here, heads, LANES), f32),
+            pltpu.VMEM(shape, f32),
+            pltpu.SemaphoreType.DMA((chunks,)),
+        ],
         compiler_params=kernel_params,
         name="attention",
     )(*map(near, (vectors, fetched, swapped, scores, values, values_far, gate, mid, att_out_weight)))

time: 46.4 us -> 44.6 us (0.961)
  Pallas kernels: 7.99 us -> 6.09 us
    pallas_call x1, Pallas kernels: 2.96 us -> 1.72 us  [body_channels(): pl.pallas_call(attention_kernel, out_shape=jax.ShapeDtypeStruct(shape, f3...]
    ppermute x2, starting transfers between devices: 5.89 us -> 5.11 us  [body_channels(): fetched.append(lax.ppermute(bias, group, pairs))]
    ppermute x1, starting transfers between devices: 0.07 us -> 0.82 us  [body_channels(): far = lax.ppermute(att, ('col', 'sub'), [(c, c ^ 1) for c in range(cols)])]
    pallas_call x1, Pallas kernels: 1.29 us -> 0.64 us  [body_channels(): pl.pallas_call(middle_kernel, out_shape=(pltpu.VMEM((cells, chan), f32),...]
where the time goes in v4:
time: 44.6 us; the launch traced here: 43.8 us
  blocking collectives  26.3 us (59%)
  starting transfers between devices  6.12 us (14%)
  Pallas kernels  6.09 us (14%)
  waiting for transfers between devices  5.13 us (12%)
    all_to_all x1, blocking collectives, body_channels(): lr = lax.all_to_all(lr, group, 0, 0, tiled=True)  15.4 us
    all_to_all x1, blocking collectives, body_channels(): sums = lax.all_to_all(sums, group, 0, 0, tiled=True)  10.9 us
    ppermute x2, starting transfers between devices, body_channels(): fetched.append(lax.ppermute(bias, group, pairs))  5.11 us
    ppermute x2, waiting for transfers between devices, body_channels(): fetched.append(lax.ppermute(bias, group, pairs))  3.92 us
    pallas_call x1, Pallas kernels, body_channels(): pl.pallas_call(functools.partial(factors_kernel, devices), out_shape=(plt...  1.72 us
    pallas_call x1, Pallas kernels, body_channels(): pl.pallas_call(attention_kernel, out_shape=jax.ShapeDtypeStruct(shape, f3...  1.72 us
    ppermute x2, waiting for transfers between devices, swap(): return lax.ppermute(v, 'row', [(r, r ^ 1) for r in range(rows)])  1.21 us
    pallas_call x1, Pallas kernels, body_channels(): pl.pallas_call(functools.partial(triangle_kernel, rows_here, cols_here),...  1.02 us
  transfers between devices with their start and end apart: 5, of which 4 were waited for; matrix products, arithmetic and copies ran while one was open for 0% of the time, Pallas kernels for 2%

profile of v4, /device:TPU:6, one launch (start us, length us, event | category | flops | bytes accessed | tf_op | source)
XLA Modules:
  0.0 43.8 jit_solution(5673820093917485672)
XLA Ops:
  0.0 0.0 copy-start
  0.0 0.0 copy-start.5
  0.0 0.0 copy-start.4
  0.0 0.0 copy-start.3
  0.0 0.0 copy-start.1
  0.0 1.7 %factors.1 = (bf16[16,9,8,128]{3,2,1,0:T(8,128)(2,1)S(1)}, bf16[576,128]{1,0:T(8,128)(2,1)S(1)}, f32[8,128]{1,0:T(8,128)S(1)}) custom-call(f32[576,128]{1,0:T(8,128)} %bitcast.8, f32[1,128]{1,0:T(1,128)} %bitcast.14, bf16[128,4,128]{2,1,0:T(4,128)(2,1)} %w_ref.2, s32[1,96]{1,0:T(1,128)} %bitcast.15, f32[1,128]{1,0:T(1,128)} %bitcast.16, f32[1,128]{1,0:T(1,128)} %bitcast.17), custom_call_target="tpu_custom_call" | custom-call | tf_op jit(solution)/shard_map/factors/pallas_call | solution.py:428
  1.8 15.4 %all_to_all.10.lr_ref = bf16[16,9,8,128]{3,2,1,0:T(8,128)(2,1)S(1)} all-to-all(bf16[16,9,8,128]{3,2,1,0:T(8,128)(2,1)S(1)} %get-tuple-element.20), channel_id=1, replica_groups=mesh['parts'=2,'row'=8,'col'=2,'sub'=1] {'row','col','sub'}, dimensions={0} | all-to-all | bytes 589824 | tf_op jit(solution)/shard_map/all_to_all | solution.py:451
  17.1 0.0 copy-start.2
  17.1 1.0 %triangle.1 = bf16[16,5,8,128]{3,2,1,0:T(8,128)(2,1)S(1)} custom-call(f32[8,128]{1,0:T(8,128)S(1)} %get-tuple-element.18.vectors_ref, bf16[16,9,8,128]{3,2,1,0:T(8,128)(2,1)S(1)} %all_to_all.10.lr_ref), custom_call_target="tpu_custom_call" | custom-call | tf_op jit(solution)/shard_map/triangle/pallas_call | solution.py:452
  18.2 10.9 %all_to_all.11.sum_ref = bf16[16,5,8,128]{3,2,1,0:T(8,128)(2,1)S(1)} all-to-all(bf16[16,5,8,128]{3,2,1,0:T(8,128)(2,1)S(1)} %triangle.1), channel_id=1, replica_groups=mesh['parts'=2,'row'=8,'col'=2,'sub'=1] {'row','col','sub'}, dimensions={0} | all-to-all | bytes 327680 | tf_op jit(solution)/shard_map/all_to_all | solution.py:459
  29.1 0.0 copy-done
  29.1 0.0 copy-done.5
  29.1 0.0 copy-done.4
  29.1 0.0 copy-done.3
  29.1 0.6 %middle.1 = (f32[576,128]{1,0:T(8,128)S(1)}, bf16[576,128]{1,0:T(8,128)(2,1)S(1)}, bf16[1,4,576]{2,1,0:T(4,128)(2,1)S(1)}) custom-call(f32[576,128]{1,0:T(8,128)S(1)} %bitcast.9, bf16[576,128]{1,0:T(8,128)(2,1)S(1)} %get-tuple-element.19.normed_ref, bf16[16,5,8,128]{3,2,1,0:T(8,128)(2,1)S(1)} %all_to_all.11.sum_ref, ...), custom_call_target="tpu_custom_call" | custom-call | tf_op jit(solution)/shard_map/middle/pallas_call | solution.py:462
  29.8 0.1 collective-permute-start
  29.9 1.1 %collective-permute-done = bf16[1,4,576]{2,1,0:T(4,128)(2,1)S(1)} collective-permute-done((bf16[1,4,576]{2,1,0:T(4,128)(2,1)S(1)}, bf16[1,4,576]{2,1,0:T(4,128)(2,1)S(1)}, u32[]{:S(2)}, u32[]{:S(2)}) %collective-permute-start) | collective-permute-done | bytes 4640 | tf_op jit(solution)/shard_map/ppermute | solution.py:488
  31.0 1.7 %collective-permute-start.1 = (bf16[2,4,576]{2,1,0:T(4,128)(2,1)S(1)}, bf16[2,4,576]{2,1,0:T(4,128)(2,1)S(1)}, u32[]{:S(2)}, u32[]{:S(2)}) collective-permute-start(bf16[2,4,576]{2,1,0:T(4,128)(2,1)S(1)} %constant_dynamic-update-slice_fusion), channel_id=1, source_target_pairs={{0,8},{1,10},{2,12},{3,14},{4,0},{5,2},{6,4},{7,6},{8,9},{9,11},{1... | collective-permute-start | bytes 27656 | tf_op jit(solution)/shard_map/ppermute | solution.py:500
  32.7 0.8 %collective-permute-start.4 = (bf16[12,48,128]{2,1,0:T(8,128)(2,1)S(1)}, bf16[12,48,128]{2,1,0:T(8,128)(2,1)S(1)}, u32[]{:S(2)}, u32[]{:S(2)}) collective-permute-start(bf16[12,48,128]{2,1,0:T(8,128)(2,1)S(1)} %bitcast.11), channel_id=1, source_target_pairs={{0,1},{1,0},{2,3},{3,2},{4,5},{5,4},{6,7},{7,6},{8,9},{9,8},{10,11... | collective-permute-start | bytes 442376 | tf_op jit(solution)/shard_map/ppermute | solution.py:501
  33.5 3.4 %collective-permute-start.2 = (bf16[2,4,576]{2,1,0:T(4,128)(2,1)S(1)}, bf16[2,4,576]{2,1,0:T(4,128)(2,1)S(1)}, u32[]{:S(2)}, u32[]{:S(2)}) collective-permute-start(bf16[2,4,576]{2,1,0:T(4,128)(2,1)S(1)} %constant_dynamic-update-slice_fusion), channel_id=1, source_target_pairs={{0,0},{1,2},{2,4},{3,6},{4,8},{5,10},{6,12},{7,14},{8,1},{9,3},{10... | collective-permute-start | bytes 27656 | tf_op jit(solution)/shard_map/ppermute | solution.py:500
  36.9 0.6 %collective-permute-done.1 = bf16[2,4,576]{2,1,0:T(4,128)(2,1)S(1)} collective-permute-done((bf16[2,4,576]{2,1,0:T(4,128)(2,1)S(1)}, bf16[2,4,576]{2,1,0:T(4,128)(2,1)S(1)}, u32[]{:S(2)}, u32[]{:S(2)}) %collective-permute-start.1) | collective-permute-done | bytes 9248 | tf_op jit(solution)/shard_map/ppermute | solution.py:500
  37.5 3.3 %collective-permute-done.2 = bf16[2,4,576]{2,1,0:T(4,128)(2,1)S(1)} collective-permute-done((bf16[2,4,576]{2,1,0:T(4,128)(2,1)S(1)}, bf16[2,4,576]{2,1,0:T(4,128)(2,1)S(1)}, u32[]{:S(2)}, u32[]{:S(2)}) %collective-permute-start.2) | collective-permute-done | bytes 9248 | tf_op jit(solution)/shard_map/ppermute | solution.py:500
  40.8 0.1 collective-permute-start.3
  40.9 0.0 copy-done.1
  40.9 0.5 %own.1 = (bf16[12,48,128]{2,1,0:T(8,128)(2,1)S(1)}, bf16[12,48,128]{2,1,0:T(8,128)(2,1)S(1)}, bf16[12,48,128]{2,1,0:T(8,128)(2,1)S(1)}, f32[12,48,128]{2,1,0:T(8,128)S(1)}, bf16[2,128,128]{2,1,0:T(8,128)(2,1)S(1)}) custom-call(bf16[12,48,128]{2,1,0:T(8,128)(2,1)S(1)} %bitcast.12, bf16[128,4,128]{2,1,0:T(4,128)(2,1)S(1)} %copy-done.1), custom_call_target="tpu_custom_call" | custom-call | tf_op jit(solution)/shard_map/own/pallas_call | solution.py:502
  41.5 0.0 collective-permute-done.4.far_ref
  41.5 0.5 %scores.1 = (f32[12,192,96]{2,1,0:T(8,128)S(1)}, bf16[12,48,128]{2,1,0:T(8,128)(2,1)S(1)}) custom-call(bf16[12,48,128]{2,1,0:T(8,128)(2,1)S(1)} %get-tuple-element.23.q_ref, bf16[12,48,128]{2,1,0:T(8,128)(2,1)S(1)} %get-tuple-element.24.k_ref, bf16[12,48,128]{2,1,0:T(8,128)(2,1)S(1)} %collective-permute-done.4.far_ref, ...), custom_call_target="tpu_custom_call" | custom-call | tf_op jit(solution)/shard_map/scores/pallas_call | solution.py:517
  41.9 0.2 collective-permute-done.3.swapped_ref
  42.1 0.0 copy-done.2
  42.1 1.7 %attention.1 = f32[12,48,128]{2,1,0:T(8,128)} custom-call(f32[8,128]{1,0:T(8,128)S(1)} %get-tuple-element.18.vectors_ref, bf16[4,4,576]{2,1,0:T(4,128)(2,1)S(1)} %constant_dynamic-update-slice_fusion.2.fetched_ref, bf16[4,4,576]{2,1,0:T(4,128)(2,1)S(1)} %collective-permute-done.3.swapped_ref, f32[12,192,96]{2,1,0:T(8,128)S(1)} %get-tuple-element.26.scores_ref, ...), custom_call_target="tpu_custom_call" | custom-call | tf_op jit(solution)/shard_map/attention/pallas_call | solution.py:526
  (4 shorter events, 0.0 us)
Async XLA Ops:
  0.0 29.1 %copy-start = (f32[12,48,128]{2,1,0:T(8,128)S(1)}, f32[12,48,128]{2,1,0:T(8,128)}, u32[]{:S(2)}) copy-start(f32[12,48,128]{2,1,0:T(8,128)} %param.11) | copy-start | bytes 884740
  0.0 29.1 %copy-start.5 = (bf16[128,4]{0,1:T(4,128)(2,1)S(1)}, bf16[128,4]{0,1:T(4,128)(2,1)}, u32[]{:S(2)}) copy-start(bf16[128,4]{0,1:T(4,128)(2,1)} %param.20) | copy-start | bytes 3076
  0.0 29.1 %copy-start.4 = (bf16[128,128]{1,0:T(8,128)(2,1)S(1)}, bf16[128,128]{1,0:T(8,128)(2,1)}, u32[]{:S(2)}) copy-start(bf16[128,128]{1,0:T(8,128)(2,1)} %gate_w_ref.1) | copy-start | bytes 98308
  0.0 29.1 %copy-start.3 = (bf16[128,128]{1,0:T(8,128)(2,1)S(1)}, bf16[128,128]{1,0:T(8,128)(2,1)}, u32[]{:S(2)}) copy-start(bf16[128,128]{1,0:T(8,128)(2,1)} %out_w_ref.2) | copy-start | bytes 98308
  0.0 40.9 %copy-start.1 = (bf16[128,4,128]{2,1,0:T(4,128)(2,1)S(1)}, bf16[128,4,128]{2,1,0:T(4,128)(2,1)}, u32[]{:S(2)}) copy-start(bf16[128,4,128]{2,1,0:T(4,128)(2,1)} %w_ref.3) | copy-start | bytes 393220
  17.1 25.0 %copy-start.2 = (bf16[128,128]{1,0:T(8,128)(2,1)S(1)}, bf16[128,128]{1,0:T(8,128)(2,1)}, u32[]{:S(2)}) copy-start(bf16[128,128]{1,0:T(8,128)(2,1)} %out_w_ref.3) | copy-start | bytes 98308
  29.8 1.2 %collective-permute-start = (bf16[1,4,576]{2,1,0:T(4,128)(2,1)S(1)}, bf16[1,4,576]{2,1,0:T(4,128)(2,1)S(1)}, u32[]{:S(2)}, u32[]{:S(2)}) collective-permute-start(bf16[1,4,576]{2,1,0:T(4,128)(2,1)S(1)} %get-tuple-element.21), channel_id=1, source_target_pairs={{0,2},{2,0},{4,6},{6,4},{8,10},{10,8},{12,14},{14,12},{1,3},{3,1},... | collective-permute-start | bytes 13832 | tf_op jit(solution)/shard_map/ppermute | solution.py:488
  31.0 6.5 %collective-permute-start.1 = (bf16[2,4,576]{2,1,0:T(4,128)(2,1)S(1)}, bf16[2,4,576]{2,1,0:T(4,128)(2,1)S(1)}, u32[]{:S(2)}, u32[]{:S(2)}) collective-permute-start(bf16[2,4,576]{2,1,0:T(4,128)(2,1)S(1)} %constant_dynamic-update-slice_fusion), channel_id=1, source_target_pairs={{0,8},{1,10},{2,12},{3,14},{4,0},{5,2},{6,4},{7,6},{8,9},{9,11},{1... | collective-permute-start | bytes 27656 | tf_op jit(solution)/shard_map/ppermute | solution.py:500
  32.7 8.8 %collective-permute-start.4 = (bf16[12,48,128]{2,1,0:T(8,128)(2,1)S(1)}, bf16[12,48,128]{2,1,0:T(8,128)(2,1)S(1)}, u32[]{:S(2)}, u32[]{:S(2)}) collective-permute-start(bf16[12,48,128]{2,1,0:T(8,128)(2,1)S(1)} %bitcast.11), channel_id=1, source_target_pairs={{0,1},{1,0},{2,3},{3,2},{4,5},{5,4},{6,7},{7,6},{8,9},{9,8},{10,11... | collective-permute-start | bytes 442376 | tf_op jit(solution)/shard_map/ppermute | solution.py:501
  33.5 7.4 %collective-permute-start.2 = (bf16[2,4,576]{2,1,0:T(4,128)(2,1)S(1)}, bf16[2,4,576]{2,1,0:T(4,128)(2,1)S(1)}, u32[]{:S(2)}, u32[]{:S(2)}) collective-permute-start(bf16[2,4,576]{2,1,0:T(4,128)(2,1)S(1)} %constant_dynamic-update-slice_fusion), channel_id=1, source_target_pairs={{0,0},{1,2},{2,4},{3,6},{4,8},{5,10},{6,12},{7,14},{8,1},{9,3},{10... | collective-permute-start | bytes 27656 | tf_op jit(solution)/shard_map/ppermute | solution.py:500
  40.8 1.3 %collective-permute-start.3 = (bf16[4,4,576]{2,1,0:T(4,128)(2,1)S(1)}, bf16[4,4,576]{2,1,0:T(4,128)(2,1)S(1)}, u32[]{:S(2)}, u32[]{:S(2)}) collective-permute-start(bf16[4,4,576]{2,1,0:T(4,128)(2,1)S(1)} %constant_dynamic-update-slice_fusion.2.fetched_ref), channel_id=1, source_target_pairs={{0,2},{2,0},{4,6},{6,4},{8,10},{10,8},{12,14},{14,12},{1,3},{3,1},... | collective-permute-start | bytes 55304 | tf_op jit(solution)/shard_map/ppermute | solution.py:488

commit v5 on v4

--- a/solution.py
+++ b/solution.py
@@ -152,8 +152,9 @@
 
 
 def split_weight(w_ref, w_scratch):
-    w_scratch[...] = w_ref[...].astype(f32)
-    return [w_scratch[:, p, :] for p in range(w_ref.shape[1])]
+    rows, mats, out = w_ref.shape
+    w_scratch[...] = w_ref[...].astype(f32).reshape(rows * mats, out)
+    return [w_scratch[pl.ds(p, rows, stride=mats), :] for p in range(mats)]
 
 
 def factors_kernel(
@@ -215,7 +216,7 @@
     rows_here, cols_here, vectors_ref, lr_ref, sum_ref, left_scratch, right_scratch, sum_scratch
 ):
     _, panels_in, own, _ = lr_ref.shape
-    residues = left_scratch.shape[0]
+    residues = left_scratch.shape[0] // own
     cols = residues // cols_here
     rows = residues // rows_here
     cells = rows_here * cols_here
@@ -231,20 +232,22 @@
                 for c in range(1, cols):
                     moved = segment(parts[c], start, c * cols_here)
                     line = jnp.where(lane < c * cols_here, line, moved)
-                scratch[r * rows_here + i] = line
+                scratch[pl.ds((r * rows_here + i) * own, own), :] = line
     live_wide = vectors_ref[0:1]
     live_square = jnp.broadcast_to(live_wide, (LANES, LANES))
     both = live_square * jnp.transpose(live_square)
     both = both[:residues]
     keep = live_wide > 0
     for h in range(own):
-        left = jnp.where(keep, left_scratch[:, h, :], 0.0).astype(bf16)
-        right = jnp.where(keep, right_scratch[:, h, :], 0.0).astype(bf16)
+        left = jnp.where(keep, left_scratch[pl.ds(h, residues, stride=own), :], 0.0).astype(bf16)
+        right = jnp.where(keep, right_scratch[pl.ds(h, residues, stride=own), :], 0.0).astype(bf16)
         right = jnp.concatenate([right, jnp.zeros((LANES - residues, LANES), bf16)], axis=0)
-        sum_scratch[:, h, :] = dot_nt(left, right) * both
+        sum_scratch[pl.ds(h, residues, stride=own), :] = dot_nt(left, right) * both
     tiles = sum_ref.shape[1]
     for r in range(rows):
-        lines = [sum_scratch[r * rows_here + i] for i in range(rows_here)]
+        lines = [
+            sum_scratch[pl.ds((r * rows_here + i) * own, own), :] for i in range(rows_here)
+        ]
         for c in range(cols):
             for t in range(tiles):
                 panel = None
@@ -339,7 +342,7 @@
     blocks, heads, cells = fetched_ref.shape
     residues = 2 * cols_here
     row, col = lax.axis_index("row"), lax.axis_index(("col", "sub"))
-    same = jnp.bitwise_and(row, 1) == col
+    same = jnp.bitwise_and(row, 1) == 0
     chip = lax.div(row, 2)
     lane_row = lax.broadcasted_iota(jnp.int32, (1, LANES), 1)
     live = vectors_ref[0:1]
@@ -359,18 +362,21 @@
     for m in range(blocks):
         p, n = m // 2, m % 2
         block = 2 * jnp.bitwise_xor(lax.div(chip, 2), 1 - p)
-        block = block + jnp.bitwise_xor(n, jnp.bitwise_and(chip, 1))
+        block = block + jnp.bitwise_xor(n, jnp.bitwise_xor(jnp.bitwise_and(chip, 1), col))
         first, second = fetched_ref[m].astype(f32), swapped_ref[m].astype(f32)
         mine = panels(jnp.where(same, first, second))
         other = panels(jnp.where(same, second, first))
         for j in range(rows_here):
-            bias_scratch[block * rows_here + j] = jnp.where(
+            bias_scratch[pl.ds((block * rows_here + j) * heads, heads), :] = jnp.where(
                 lane < cols_here,
                 segment(mine, j * cols_here, 0),
                 segment(other, j * cols_here, cols_here),
             )
     penalty = penalty[:, :residues]
-    head_bias = [bias_scratch[:, h, :][:, :residues] + penalty for h in range(heads)]
+    head_bias = [
+        bias_scratch[pl.ds(h, cols_here, stride=heads), :][:, :residues] + penalty
+        for h in range(heads)
+    ]
     head_bias = jnp.concatenate(head_bias, axis=0)
     head_of = lax.broadcasted_iota(jnp.int32, (cols_here, width), 1) // (width // heads)
     ones = jnp.ones((residues, width), bf16)
@@ -432,7 +438,7 @@
             pltpu.VMEM((cells, chan), bf16),
             pltpu.VMEM((8, LANES), f32),
         ),
-        scratch_shapes=[pltpu.VMEM(tri_in_weight.shape, f32)],
+        scratch_shapes=[pltpu.VMEM((chan * tri_in_weight.shape[1], hidden), f32)],
         compiler_params=kernel_params,
         name="factors",
     )(
@@ -452,7 +458,7 @@
     sums = pl.pallas_call(
         functools.partial(triangle_kernel, rows_here, cols_here),
         out_shape=pltpu.VMEM((devices, tiles, own, LANES), bf16),
-        scratch_shapes=[pltpu.VMEM((residues, own, LANES), f32) for _ in range(3)],
+        scratch_shapes=[pltpu.VMEM((residues * own, LANES), f32) for _ in range(3)],
         compiler_params=kernel_params,
         name="triangle",
     )(near(vectors), near(lr))
@@ -495,8 +501,9 @@
         for z in range(rows // 2):
             for s in range(2):
                 for x in range(cols):
-                    target = (2 * ((z & 1) ^ 1 ^ p) + s) * 2 + x
-                    pairs.append(((2 * z + s) * cols + x, target * cols + (z >> 1)))
+                    half = z >> 1
+                    target = (2 * ((z & 1) ^ 1 ^ p) + (s ^ half)) * 2 + (x ^ half)
+                    pairs.append(((2 * z + s) * cols + x, target * cols + half))
         fetched.append(lax.ppermute(bias, group, pairs))
     far = lax.ppermute(att, ("col", "sub"), [(c, c ^ 1) for c in range(cols)])
     queries, keys, values, gate, kv_weight = pl.pallas_call(
@@ -508,7 +515,7 @@
             pltpu.VMEM(shape, f32),
             pltpu.VMEM((2, chan, chan), bf16),
         ),
-        scratch_shapes=[pltpu.VMEM(att_proj_weight.shape, f32)],
+        scratch_shapes=[pltpu.VMEM((chan * att_proj_weight.shape[1], chan), f32)],
         compiler_params=kernel_params,
         name="own",
     )(near(att), near(att_proj_weight))
@@ -528,7 +535,7 @@
         out_shape=jax.ShapeDtypeStruct(shape, f32),
         out_specs=pl.BlockSpec(memory_space=pltpu.HBM),
         scratch_shapes=[
-            pltpu.VMEM((cols_here, heads, LANES), f32),
+            pltpu.VMEM((cols_here * heads, LANES), f32),
             pltpu.VMEM(shape, f32),
             pltpu.SemaphoreType.DMA((chunks,)),
         ],

time: 44.6 us -> 43.8 us (0.982)
  the two profiles are of different devices: /device:TPU:6 before, /device:TPU:0 now
where the time goes in v5:
time: 43.8 us; the launch traced here: 43.6 us
  blocking collectives  28.7 us (66%)
  starting transfers between devices  7.29 us (17%)
  Pallas kernels  5.53 us (13%)
  waiting for transfers between devices  1.89 us (4%)
    all_to_all x1, blocking collectives, body_channels(): lr = lax.all_to_all(lr, group, 0, 0, tiled=True)  17.8 us
    all_to_all x1, blocking collectives, body_channels(): sums = lax.all_to_all(sums, group, 0, 0, tiled=True)  10.9 us
    ppermute x2, starting transfers between devices, swap(): return lax.ppermute(v, 'row', [(r, r ^ 1) for r in range(rows)])  4.39 us
    pallas_call x1, Pallas kernels, body_channels(): pl.pallas_call(attention_kernel, out_shape=jax.ShapeDtypeStruct(shape, f3...  1.73 us
    ppermute x2, starting transfers between devices, body_channels(): fetched.append(lax.ppermute(bias, group, pairs))  1.7 us
    pallas_call x1, Pallas kernels, body_channels(): pl.pallas_call(functools.partial(factors_kernel, devices), out_shape=(plt...  1.69 us
    ppermute x1, starting transfers between devices, body_channels(): far = lax.ppermute(att, ('col', 'sub'), [(c, c ^ 1) for c in range(cols)])  1.21 us
    ppermute x2, waiting for transfers between devices, swap(): return lax.ppermute(v, 'row', [(r, r ^ 1) for r in range(rows)])  1.07 us
  transfers between devices with their start and end apart: 5, of which 2 were waited for; matrix products, arithmetic and copies ran while one was open for 0% of the time, Pallas kernels for 2%

profile of v5, /device:TPU:0, one launch (start us, length us, event | category | flops | bytes accessed | tf_op | source)
XLA Modules:
  0.0 43.6 jit_solution(4008340365034780875)
XLA Ops:
  0.0 0.0 copy-start
  0.0 0.0 copy-start.5
  0.0 0.0 copy-start.4
  0.0 0.0 copy-start.3
  0.0 0.0 copy-start.1
  0.0 1.7 %factors.1 = (bf16[16,9,8,128]{3,2,1,0:T(8,128)(2,1)S(1)}, bf16[576,128]{1,0:T(8,128)(2,1)S(1)}, f32[8,128]{1,0:T(8,128)S(1)}) custom-call(f32[576,128]{1,0:T(8,128)} %bitcast.8, f32[1,128]{1,0:T(1,128)} %bitcast.14, bf16[128,4,128]{2,1,0:T(4,128)(2,1)} %w_ref.2, s32[1,96]{1,0:T(1,128)} %bitcast.15, f32[1,128]{1,0:T(1,128)} %bitcast.16, f32[1,128]{1,0:T(1,128)} %bitcast.17), custom_call_target="tpu_custom_call" | custom-call | tf_op jit(solution)/shard_map/factors/pallas_call | solution.py:434
  1.7 17.8 %all_to_all.10.lr_ref = bf16[16,9,8,128]{3,2,1,0:T(8,128)(2,1)S(1)} all-to-all(bf16[16,9,8,128]{3,2,1,0:T(8,128)(2,1)S(1)} %get-tuple-element.20), channel_id=1, replica_groups=mesh['parts'=2,'row'=8,'col'=2,'sub'=1] {'row','col','sub'}, dimensions={0} | all-to-all | bytes 589824 | tf_op jit(solution)/shard_map/all_to_all | solution.py:457
  19.5 0.0 copy-start.2
  19.5 0.7 %triangle.1 = bf16[16,5,8,128]{3,2,1,0:T(8,128)(2,1)S(1)} custom-call(f32[8,128]{1,0:T(8,128)S(1)} %get-tuple-element.18.vectors_ref, bf16[16,9,8,128]{3,2,1,0:T(8,128)(2,1)S(1)} %all_to_all.10.lr_ref), custom_call_target="tpu_custom_call" | custom-call | tf_op jit(solution)/shard_map/triangle/pallas_call | solution.py:458
  20.2 10.9 %all_to_all.11.sum_ref = bf16[16,5,8,128]{3,2,1,0:T(8,128)(2,1)S(1)} all-to-all(bf16[16,5,8,128]{3,2,1,0:T(8,128)(2,1)S(1)} %triangle.1), channel_id=1, replica_groups=mesh['parts'=2,'row'=8,'col'=2,'sub'=1] {'row','col','sub'}, dimensions={0} | all-to-all | bytes 327680 | tf_op jit(solution)/shard_map/all_to_all | solution.py:465
  31.1 0.0 copy-done
  31.1 0.0 copy-done.5
  31.1 0.0 copy-done.4
  31.1 0.0 copy-done.3
  31.2 0.6 %middle.1 = (f32[576,128]{1,0:T(8,128)S(1)}, bf16[576,128]{1,0:T(8,128)(2,1)S(1)}, bf16[1,4,576]{2,1,0:T(4,128)(2,1)S(1)}) custom-call(f32[576,128]{1,0:T(8,128)S(1)} %bitcast.9, bf16[576,128]{1,0:T(8,128)(2,1)S(1)} %get-tuple-element.19.normed_ref, bf16[16,5,8,128]{3,2,1,0:T(8,128)(2,1)S(1)} %all_to_all.11.sum_ref, ...), custom_call_target="tpu_custom_call" | custom-call | tf_op jit(solution)/shard_map/middle/pallas_call | solution.py:468
  31.8 0.1 collective-permute-start
  31.9 1.1 %collective-permute-done = bf16[1,4,576]{2,1,0:T(4,128)(2,1)S(1)} collective-permute-done((bf16[1,4,576]{2,1,0:T(4,128)(2,1)S(1)}, bf16[1,4,576]{2,1,0:T(4,128)(2,1)S(1)}, u32[]{:S(2)}, u32[]{:S(2)}) %collective-permute-start) | collective-permute-done | bytes 4640 | tf_op jit(solution)/shard_map/ppermute | solution.py:494
  33.0 1.0 %collective-permute-start.1 = (bf16[2,4,576]{2,1,0:T(4,128)(2,1)S(1)}, bf16[2,4,576]{2,1,0:T(4,128)(2,1)S(1)}, u32[]{:S(2)}, u32[]{:S(2)}) collective-permute-start(bf16[2,4,576]{2,1,0:T(4,128)(2,1)S(1)} %constant_dynamic-update-slice_fusion), channel_id=1, source_target_pairs={{0,8},{1,10},{2,12},{3,14},{4,0},{5,2},{6,4},{7,6},{8,15},{9,13},{... | collective-permute-start | bytes 27656 | tf_op jit(solution)/shard_map/ppermute | solution.py:507
  34.0 1.2 %collective-permute-start.4 = (bf16[12,48,128]{2,1,0:T(8,128)(2,1)S(1)}, bf16[12,48,128]{2,1,0:T(8,128)(2,1)S(1)}, u32[]{:S(2)}, u32[]{:S(2)}) collective-permute-start(bf16[12,48,128]{2,1,0:T(8,128)(2,1)S(1)} %bitcast.11), channel_id=1, source_target_pairs={{0,1},{1,0},{2,3},{3,2},{4,5},{5,4},{6,7},{7,6},{8,9},{9,8},{10,11... | collective-permute-start | bytes 442376 | tf_op jit(solution)/shard_map/ppermute | solution.py:508
  35.2 0.7 %collective-permute-start.2 = (bf16[2,4,576]{2,1,0:T(4,128)(2,1)S(1)}, bf16[2,4,576]{2,1,0:T(4,128)(2,1)S(1)}, u32[]{:S(2)}, u32[]{:S(2)}) collective-permute-start(bf16[2,4,576]{2,1,0:T(4,128)(2,1)S(1)} %constant_dynamic-update-slice_fusion), channel_id=1, source_target_pairs={{0,0},{1,2},{2,4},{3,6},{4,8},{5,10},{6,12},{7,14},{8,7},{9,5},{10... | collective-permute-start | bytes 27656 | tf_op jit(solution)/shard_map/ppermute | solution.py:507
  35.9 0.8 %collective-permute-done.1 = bf16[2,4,576]{2,1,0:T(4,128)(2,1)S(1)} collective-permute-done((bf16[2,4,576]{2,1,0:T(4,128)(2,1)S(1)}, bf16[2,4,576]{2,1,0:T(4,128)(2,1)S(1)}, u32[]{:S(2)}, u32[]{:S(2)}) %collective-permute-start.1) | collective-permute-done | bytes 9248 | tf_op jit(solution)/shard_map/ppermute | solution.py:507
  36.7 0.0 collective-permute-done.2
  36.7 4.3 %collective-permute-start.3 = (bf16[4,4,576]{2,1,0:T(4,128)(2,1)S(1)}, bf16[4,4,576]{2,1,0:T(4,128)(2,1)S(1)}, u32[]{:S(2)}, u32[]{:S(2)}) collective-permute-start(bf16[4,4,576]{2,1,0:T(4,128)(2,1)S(1)} %constant_dynamic-update-slice_fusion.2.fetched_ref), channel_id=1, source_target_pairs={{0,2},{2,0},{4,6},{6,4},{8,10},{10,8},{12,14},{14,12},{1,3},{3,1},... | collective-permute-start | bytes 55304 | tf_op jit(solution)/shard_map/ppermute | solution.py:494
  41.0 0.0 copy-done.1
  41.0 0.3 own.1
  41.4 0.0 collective-permute-done.4.far_ref
  41.4 0.5 %scores.1 = (f32[12,192,96]{2,1,0:T(8,128)S(1)}, bf16[12,48,128]{2,1,0:T(8,128)(2,1)S(1)}) custom-call(bf16[12,48,128]{2,1,0:T(8,128)(2,1)S(1)} %get-tuple-element.23.q_ref, bf16[12,48,128]{2,1,0:T(8,128)(2,1)S(1)} %get-tuple-element.24.k_ref, bf16[12,48,128]{2,1,0:T(8,128)(2,1)S(1)} %collective-permute-done.4.far_ref, ...), custom_call_target="tpu_custom_call" | custom-call | tf_op jit(solution)/shard_map/scores/pallas_call | solution.py:524
  41.8 0.0 collective-permute-done.3.swapped_ref
  41.9 0.0 copy-done.2
  41.9 1.7 %attention.1 = f32[12,48,128]{2,1,0:T(8,128)} custom-call(f32[8,128]{1,0:T(8,128)S(1)} %get-tuple-element.18.vectors_ref, bf16[4,4,576]{2,1,0:T(4,128)(2,1)S(1)} %constant_dynamic-update-slice_fusion.2.fetched_ref, bf16[4,4,576]{2,1,0:T(4,128)(2,1)S(1)} %collective-permute-done.3.swapped_ref, f32[12,192,96]{2,1,0:T(8,128)S(1)} %get-tuple-element.26.scores_ref, ...), custom_call_target="tpu_custom_call" | custom-call | tf_op jit(solution)/shard_map/attention/pallas_call | solution.py:533
  (4 shorter events, 0.0 us)
Async XLA Ops:
  0.0 31.1 %copy-start = (f32[12,48,128]{2,1,0:T(8,128)S(1)}, f32[12,48,128]{2,1,0:T(8,128)}, u32[]{:S(2)}) copy-start(f32[12,48,128]{2,1,0:T(8,128)} %param.11) | copy-start | bytes 884740
  0.0 31.1 %copy-start.5 = (bf16[128,4]{0,1:T(4,128)(2,1)S(1)}, bf16[128,4]{0,1:T(4,128)(2,1)}, u32[]{:S(2)}) copy-start(bf16[128,4]{0,1:T(4,128)(2,1)} %param.20) | copy-start | bytes 3076
  0.0 31.1 %copy-start.4 = (bf16[128,128]{1,0:T(8,128)(2,1)S(1)}, bf16[128,128]{1,0:T(8,128)(2,1)}, u32[]{:S(2)}) copy-start(bf16[128,128]{1,0:T(8,128)(2,1)} %gate_w_ref.1) | copy-start | bytes 98308
  0.0 31.1 %copy-start.3 = (bf16[128,128]{1,0:T(8,128)(2,1)S(1)}, bf16[128,128]{1,0:T(8,128)(2,1)}, u32[]{:S(2)}) copy-start(bf16[128,128]{1,0:T(8,128)(2,1)} %out_w_ref.2) | copy-start | bytes 98308
  0.0 41.0 %copy-start.1 = (bf16[128,4,128]{2,1,0:T(4,128)(2,1)S(1)}, bf16[128,4,128]{2,1,0:T(4,128)(2,1)}, u32[]{:S(2)}) copy-start(bf16[128,4,128]{2,1,0:T(4,128)(2,1)} %w_ref.3) | copy-start | bytes 393220
  19.5 22.4 %copy-start.2 = (bf16[128,128]{1,0:T(8,128)(2,1)S(1)}, bf16[128,128]{1,0:T(8,128)(2,1)}, u32[]{:S(2)}) copy-start(bf16[128,128]{1,0:T(8,128)(2,1)} %out_w_ref.3) | copy-start | bytes 98308
  31.8 1.2 %collective-permute-start = (bf16[1,4,576]{2,1,0:T(4,128)(2,1)S(1)}, bf16[1,4,576]{2,1,0:T(4,128)(2,1)S(1)}, u32[]{:S(2)}, u32[]{:S(2)}) collective-permute-start(bf16[1,4,576]{2,1,0:T(4,128)(2,1)S(1)} %get-tuple-element.21), channel_id=1, source_target_pairs={{0,2},{2,0},{4,6},{6,4},{8,10},{10,8},{12,14},{14,12},{1,3},{3,1},... | collective-permute-start | bytes 13832 | tf_op jit(solution)/shard_map/ppermute | solution.py:494
  33.0 3.7 %collective-permute-start.1 = (bf16[2,4,576]{2,1,0:T(4,128)(2,1)S(1)}, bf16[2,4,576]{2,1,0:T(4,128)(2,1)S(1)}, u32[]{:S(2)}, u32[]{:S(2)}) collective-permute-start(bf16[2,4,576]{2,1,0:T(4,128)(2,1)S(1)} %constant_dynamic-update-slice_fusion), channel_id=1, source_target_pairs={{0,8},{1,10},{2,12},{3,14},{4,0},{5,2},{6,4},{7,6},{8,15},{9,13},{... | collective-permute-start | bytes 27656 | tf_op jit(solution)/shard_map/ppermute | solution.py:507
  34.0 7.3 %collective-permute-start.4 = (bf16[12,48,128]{2,1,0:T(8,128)(2,1)S(1)}, bf16[12,48,128]{2,1,0:T(8,128)(2,1)S(1)}, u32[]{:S(2)}, u32[]{:S(2)}) collective-permute-start(bf16[12,48,128]{2,1,0:T(8,128)(2,1)S(1)} %bitcast.11), channel_id=1, source_target_pairs={{0,1},{1,0},{2,3},{3,2},{4,5},{5,4},{6,7},{7,6},{8,9},{9,8},{10,11... | collective-permute-start | bytes 442376 | tf_op jit(solution)/shard_map/ppermute | solution.py:508
  35.2 1.5 %collective-permute-start.2 = (bf16[2,4,576]{2,1,0:T(4,128)(2,1)S(1)}, bf16[2,4,576]{2,1,0:T(4,128)(2,1)S(1)}, u32[]{:S(2)}, u32[]{:S(2)}) collective-permute-start(bf16[2,4,576]{2,1,0:T(4,128)(2,1)S(1)} %constant_dynamic-update-slice_fusion), channel_id=1, source_target_pairs={{0,0},{1,2},{2,4},{3,6},{4,8},{5,10},{6,12},{7,14},{8,7},{9,5},{10... | collective-permute-start | bytes 27656 | tf_op jit(solution)/shard_map/ppermute | solution.py:507
  36.7 5.1 %collective-permute-start.3 = (bf16[4,4,576]{2,1,0:T(4,128)(2,1)S(1)}, bf16[4,4,576]{2,1,0:T(4,128)(2,1)S(1)}, u32[]{:S(2)}, u32[]{:S(2)}) collective-permute-start(bf16[4,4,576]{2,1,0:T(4,128)(2,1)S(1)} %constant_dynamic-update-slice_fusion.2.fetched_ref), channel_id=1, source_target_pairs={{0,2},{2,0},{4,6},{6,4},{8,10},{10,8},{12,14},{14,12},{1,3},{3,1},... | collective-permute-start | bytes 55304 | tf_op jit(solution)/shard_map/ppermute | solution.py:494

commit v6 on v5

--- a/solution.py
+++ b/solution.py
@@ -308,27 +308,110 @@
     gate_ref[...] = sigmoid(dot_nn(att, w[3])).reshape(shape)
 
 
-def scores_kernel(heads, q_ref, k_ref, far_ref, kv_w_ref, scores_ref, v_far_ref):
+def fetch_plan():
+    trips, codes = ([], []), [0] * 16
+    for h in range(2):
+        for x in range(2):
+            for p in range(2):
+                for b in range(2):
+                    chips = [t for t in range(4) if (t in FIRST[h][x]) == (b == p)]
+                    for n, target in enumerate(chips):
+                        source_core = n ^ TURNED[2 * h + b][x][p]
+                        core = x ^ (target in SWAPPED[h])
+                        source = ((2 * h + b) * 2 + source_core) * 2 + x
+                        device = (target * 2 + core) * 2 + h
+                        trips[p].append((source, device))
+                        codes[device] |= (b if p == 0 else 0) | source_core << (1 + p)
+                        codes[device] |= (x == h) << 3
+    return trips, codes
+
+
+FIRST = (((1, 3), (2, 3)), ((2, 3), (2, 3)))
+SWAPPED = ((), (0, 1, 3))
+TURNED = (((1, 0), (1, 1)), ((1, 0), (1, 0)), ((0, 1), (0, 1)), ((0, 0), (0, 1)))
+
+
+def fetch_code(codes, row, col):
+    index = row * 2 + col
+    code = jnp.int32(0)
+    for device, entry in enumerate(codes):
+        code = jnp.where(index == device, jnp.int32(entry), code)
+    return [jnp.bitwise_and(lax.shift_right_logical(code, jnp.int32(n)), 1) for n in range(4)]
+
+
+def head_bias_half(ref, scratch, rows_here, cols_here, code, target):
+    blocks, heads, cells = ref.shape
+    first, *cores, _ = code
+    pad = (-cells) % LANES
+    for m in range(blocks):
+        p, n = m // 2, m % 2
+        block = 2 * jnp.bitwise_xor(first, p) + jnp.bitwise_xor(n, cores[p])
+        v = ref[m].astype(f32)
+        v = jnp.concatenate([v, jnp.zeros((heads, pad), f32)], axis=1) if pad else v
+        panels = [v[:, t * LANES : (t + 1) * LANES] for t in range((cells + pad) // LANES)]
+        for j in range(rows_here):
+            line = segment(panels, j * cols_here, target)
+            scratch[pl.ds((block * rows_here + j) * heads, heads), :] = line
+    return jnp.concatenate(
+        [scratch[pl.ds(h, cols_here, stride=heads), :] for h in range(heads)], axis=0
+    )
+
+
+def scores_kernel(
+    codes,
+    vectors_ref,
+    fetched_ref,
+    q_ref,
+    k_ref,
+    far_ref,
+    v_ref,
+    kv_w_ref,
+    scores_ref,
+    v_all_ref,
+    bias_ref,
+    bias_scratch,
+):
     rows_here, cols_here, width = q_ref.shape
+    heads = fetched_ref.shape[1]
     far = far_ref[...].reshape(rows_here * cols_here, width)
     k_far = dot_nn(far, kv_w_ref[0]).astype(bf16).reshape(q_ref.shape)
-    v_far_ref[...] = dot_nn(far, kv_w_ref[1]).astype(bf16).reshape(q_ref.shape)
+    v_far = dot_nn(far, kv_w_ref[1]).astype(bf16).reshape(q_ref.shape)
+    row, col = lax.axis_index("row"), lax.axis_index(("col", "sub"))
+    code = fetch_code(codes, row, col)
+    own_first = code[3] == 1
+
+    def in_order(own, other):
+        return jnp.concatenate(
+            [jnp.where(own_first, own, other), jnp.where(own_first, other, own)], axis=0
+        )
+
     head_of = lax.broadcasted_iota(jnp.int32, (cols_here, width), 1) // (width // heads)
     for i in range(rows_here):
         q = q_ref[i]
         q_heads = jnp.concatenate(
             [jnp.where(head_of == h, q, jnp.zeros_like(q)) for h in range(heads)], axis=0
         )
-        scores_ref[i] = dot_nt(q_heads, jnp.concatenate([k_ref[i], k_far[i]], axis=0))
+        scores_ref[i] = dot_nt(q_heads, in_order(k_ref[i], k_far[i]))
+        v_all_ref[i] = in_order(v_ref[i], v_far[i])
+    lane_row = lax.broadcasted_iota(jnp.int32, (1, LANES), 1)
+    live = vectors_ref[0:1]
+    swapped = jnp.where(
+        lane_row < cols_here,
+        pltpu.roll(live, LANES - cols_here, 1),
+        pltpu.roll(live, cols_here, 1),
+    )
+    natural = (col == 0) == own_first
+    penalty = (jnp.where(natural, live, swapped) - 1.0) * mask_penalty
+    half = head_bias_half(fetched_ref, bias_scratch, rows_here, cols_here, code, 0)
+    bias_ref[...] = jnp.where(lane_row < cols_here, half, 0.0) + penalty
 
 
 def attention_kernel(
-    vectors_ref,
-    fetched_ref,
+    codes,
+    bias_ref,
     swapped_ref,
     scores_ref,
-    v_ref,
-    v_far_ref,
+    v_all_ref,
     gate_ref,
     mid_ref,
     out_w_ref,
@@ -337,47 +420,15 @@
     result,
     done,
 ):
-    rows_here, cols_here, width = v_ref.shape
+    rows_here, cols_here, width = gate_ref.shape
     chunks = done.shape[0]
-    blocks, heads, cells = fetched_ref.shape
+    heads = swapped_ref.shape[1]
     residues = 2 * cols_here
     row, col = lax.axis_index("row"), lax.axis_index(("col", "sub"))
-    same = jnp.bitwise_and(row, 1) == 0
-    chip = lax.div(row, 2)
+    code = fetch_code(codes, jnp.bitwise_xor(row, 1), col)
+    half = head_bias_half(swapped_ref, bias_scratch, rows_here, cols_here, code, cols_here)
     lane_row = lax.broadcasted_iota(jnp.int32, (1, LANES), 1)
-    live = vectors_ref[0:1]
-    swapped = jnp.where(
-        lane_row < cols_here,
-        pltpu.roll(live, LANES - cols_here, 1),
-        pltpu.roll(live, cols_here, 1),
-    )
-    penalty = (jnp.where(col == 0, live, swapped) - 1.0) * mask_penalty
-    lane = lax.broadcasted_iota(jnp.int32, (heads, LANES), 1)
-    pad = (-cells) % LANES
-
-    def panels(v):
-        v = jnp.concatenate([v, jnp.zeros((heads, pad), f32)], axis=1) if pad else v
-        return [v[:, t * LANES : (t + 1) * LANES] for t in range((cells + pad) // LANES)]
-
-    for m in range(blocks):
-        p, n = m // 2, m % 2
-        block = 2 * jnp.bitwise_xor(lax.div(chip, 2), 1 - p)
-        block = block + jnp.bitwise_xor(n, jnp.bitwise_xor(jnp.bitwise_and(chip, 1), col))
-        first, second = fetched_ref[m].astype(f32), swapped_ref[m].astype(f32)
-        mine = panels(jnp.where(same, first, second))
-        other = panels(jnp.where(same, second, first))
-        for j in range(rows_here):
-            bias_scratch[pl.ds((block * rows_here + j) * heads, heads), :] = jnp.where(
-                lane < cols_here,
-                segment(mine, j * cols_here, 0),
-                segment(other, j * cols_here, cols_here),
-            )
-    penalty = penalty[:, :residues]
-    head_bias = [
-        bias_scratch[pl.ds(h, cols_here, stride=heads), :][:, :residues] + penalty
-        for h in range(heads)
-    ]
-    head_bias = jnp.concatenate(head_bias, axis=0)
+    head_bias = (bias_ref[...] + jnp.where(lane_row < cols_here, 0.0, half))[:, :residues]
     head_of = lax.broadcasted_iota(jnp.int32, (cols_here, width), 1) // (width // heads)
     ones = jnp.ones((residues, width), bf16)
     chunk = rows_here // chunks
@@ -385,10 +436,9 @@
     for c in range(chunks):
         gated = []
         for i in range(c * chunk, (c + 1) * chunk):
-            v = jnp.concatenate([v_ref[i], v_far_ref[i]], axis=0)
             scores = scores_ref[i] + head_bias
             raised = jnp.exp(scores - jnp.max(scores, axis=-1, keepdims=True)).astype(bf16)
-            mixed = dot_nn(raised, jnp.concatenate([v, ones], axis=1))
+            mixed = dot_nn(raised, jnp.concatenate([v_all_ref[i], ones], axis=1))
             attended = mixed[:cols_here]
             for h in range(1, heads):
                 part = mixed[h * cols_here : (h + 1) * cols_here]
@@ -493,18 +543,12 @@
     def swap(v):
         return lax.ppermute(v, "row", [(r, r ^ 1) for r in range(rows)])
 
+    trips, codes = fetch_plan()
     joined = swap(bias)
     bias = jnp.concatenate([bias, joined], axis=0)
     fetched = []
     for p in range(2):
-        pairs = []
-        for z in range(rows // 2):
-            for s in range(2):
-                for x in range(cols):
-                    half = z >> 1
-                    target = (2 * ((z & 1) ^ 1 ^ p) + (s ^ half)) * 2 + (x ^ half)
-                    pairs.append(((2 * z + s) * cols + x, target * cols + half))
-        fetched.append(lax.ppermute(bias, group, pairs))
+        fetched.append(lax.ppermute(bias, group, trips[p]))
     far = lax.ppermute(att, ("col", "sub"), [(c, c ^ 1) for c in range(cols)])
     queries, keys, values, gate, kv_weight = pl.pallas_call(
         functools.partial(own_kernel, heads),
@@ -521,17 +565,19 @@
     )(near(att), near(att_proj_weight))
     fetched = jnp.concatenate(fetched, axis=0)
     swapped = swap(fetched)
-    scores, values_far = pl.pallas_call(
-        functools.partial(scores_kernel, heads),
+    scores, values, bias = pl.pallas_call(
+        functools.partial(scores_kernel, codes),
         out_shape=(
             pltpu.VMEM((rows_here, heads * cols_here, residues), f32),
-            pltpu.VMEM(shape, bf16),
+            pltpu.VMEM((rows_here, residues, chan), bf16),
+            pltpu.VMEM((heads * cols_here, LANES), f32),
         ),
+        scratch_shapes=[pltpu.VMEM((cols_here * heads, LANES), f32)],
         compiler_params=kernel_params,
         name="scores",
-    )(*map(near, (queries, keys, far, kv_weight)))
+    )(*map(near, (vectors, fetched, queries, keys, far, values, kv_weight)))
     return pl.pallas_call(
-        attention_kernel,
+        functools.partial(attention_kernel, codes),
         out_shape=jax.ShapeDtypeStruct(shape, f32),
         out_specs=pl.BlockSpec(memory_space=pltpu.HBM),
         scratch_shapes=[
@@ -541,7 +587,7 @@
         ],
         compiler_params=kernel_params,
         name="attention",
-    )(*map(near, (vectors, fetched, swapped, scores, values, values_far, gate, mid, att_out_weight)))
+    )(*map(near, (bias, swapped, scores, values, gate, mid, att_out_weight)))
 
 
 def solution(mesh):

time: 43.8 us -> 43.4 us (level)
  the two profiles are of different devices: /device:TPU:0 before, /device:TPU:6 now
where the time goes in v6:
time: 43.4 us; the launch traced here: 42.8 us
  blocking collectives  26.3 us (61%)
  starting transfers between devices  5.71 us (13%)
  Pallas kernels  5.51 us (13%)
  waiting for transfers between devices  5.1 us (12%)
    all_to_all x1, blocking collectives, body_channels(): lr = lax.all_to_all(lr, group, 0, 0, tiled=True)  15.4 us
    all_to_all x1, blocking collectives, body_channels(): sums = lax.all_to_all(sums, group, 0, 0, tiled=True)  10.9 us
    ppermute x2, starting transfers between devices, body_channels(): fetched.append(lax.ppermute(bias, group, trips[p]))  4.7 us
    ppermute x2, waiting for transfers between devices, body_channels(): fetched.append(lax.ppermute(bias, group, trips[p]))  3.71 us
    pallas_call x1, Pallas kernels, body_channels(): pl.pallas_call(functools.partial(attention_kernel, codes), out_shape=jax....  1.69 us
    pallas_call x1, Pallas kernels, body_channels(): pl.pallas_call(functools.partial(factors_kernel, devices), out_shape=(plt...  1.69 us
    ppermute x2, waiting for transfers between devices, swap(): return lax.ppermute(v, 'row', [(r, r ^ 1) for r in range(rows)])  1.38 us
  transfers between devices with their start and end apart: 5, of which 3 were waited for; matrix products, arithmetic and copies ran while one was open for 0% of the time, Pallas kernels for 2%

profile of v6, /device:TPU:6, one launch (start us, length us, event | category | flops | bytes accessed | tf_op | source)
XLA Modules:
  0.0 42.8 jit_solution(11248400809024035646)
XLA Ops:
  0.0 0.0 copy-start
  0.0 0.0 copy-start.5
  0.0 0.0 copy-start.4
  0.0 0.0 copy-start.3
  0.0 0.0 copy-start.1
  0.0 1.7 %factors.1 = (bf16[16,9,8,128]{3,2,1,0:T(8,128)(2,1)S(1)}, bf16[576,128]{1,0:T(8,128)(2,1)S(1)}, f32[8,128]{1,0:T(8,128)S(1)}) custom-call(f32[576,128]{1,0:T(8,128)} %bitcast.8, f32[1,128]{1,0:T(1,128)} %bitcast.14, bf16[128,4,128]{2,1,0:T(4,128)(2,1)} %w_ref.2, s32[1,96]{1,0:T(1,128)} %bitcast.15, f32[1,128]{1,0:T(1,128)} %bitcast.16, f32[1,128]{1,0:T(1,128)} %bitcast.17), custom_call_target="tpu_custom_call" | custom-call | tf_op jit(solution)/shard_map/factors/pallas_call | solution.py:484
  1.7 15.4 %all_to_all.10.lr_ref = bf16[16,9,8,128]{3,2,1,0:T(8,128)(2,1)S(1)} all-to-all(bf16[16,9,8,128]{3,2,1,0:T(8,128)(2,1)S(1)} %get-tuple-element.21), channel_id=1, replica_groups=mesh['parts'=2,'row'=8,'col'=2,'sub'=1] {'row','col','sub'}, dimensions={0} | all-to-all | bytes 589824 | tf_op jit(solution)/shard_map/all_to_all | solution.py:507
  17.1 0.0 copy-start.2
  17.1 0.7 %triangle.1 = bf16[16,5,8,128]{3,2,1,0:T(8,128)(2,1)S(1)} custom-call(f32[8,128]{1,0:T(8,128)S(1)} %get-tuple-element.19.vectors_ref, bf16[16,9,8,128]{3,2,1,0:T(8,128)(2,1)S(1)} %all_to_all.10.lr_ref), custom_call_target="tpu_custom_call" | custom-call | tf_op jit(solution)/shard_map/triangle/pallas_call | solution.py:508
  17.8 10.9 %all_to_all.11.sum_ref = bf16[16,5,8,128]{3,2,1,0:T(8,128)(2,1)S(1)} all-to-all(bf16[16,5,8,128]{3,2,1,0:T(8,128)(2,1)S(1)} %triangle.1), channel_id=1, replica_groups=mesh['parts'=2,'row'=8,'col'=2,'sub'=1] {'row','col','sub'}, dimensions={0} | all-to-all | bytes 327680 | tf_op jit(solution)/shard_map/all_to_all | solution.py:515
  28.7 0.0 copy-done
  28.7 0.0 copy-done.5
  28.7 0.0 copy-done.4
  28.7 0.0 copy-done.3
  28.8 0.6 %middle.1 = (f32[576,128]{1,0:T(8,128)S(1)}, bf16[576,128]{1,0:T(8,128)(2,1)S(1)}, bf16[1,4,576]{2,1,0:T(4,128)(2,1)S(1)}) custom-call(f32[576,128]{1,0:T(8,128)S(1)} %bitcast.9, bf16[576,128]{1,0:T(8,128)(2,1)S(1)} %get-tuple-element.20.normed_ref, bf16[16,5,8,128]{3,2,1,0:T(8,128)(2,1)S(1)} %all_to_all.11.sum_ref, ...), custom_call_target="tpu_custom_call" | custom-call | tf_op jit(solution)/shard_map/middle/pallas_call | solution.py:518
  29.4 0.1 collective-permute-start
  29.5 1.1 %collective-permute-done = bf16[1,4,576]{2,1,0:T(4,128)(2,1)S(1)} collective-permute-done((bf16[1,4,576]{2,1,0:T(4,128)(2,1)S(1)}, bf16[1,4,576]{2,1,0:T(4,128)(2,1)S(1)}, u32[]{:S(2)}, u32[]{:S(2)}) %collective-permute-start) | collective-permute-done | bytes 4640 | tf_op jit(solution)/shard_map/ppermute | solution.py:544
  30.6 2.6 %collective-permute-start.1 = (bf16[2,4,576]{2,1,0:T(4,128)(2,1)S(1)}, bf16[2,4,576]{2,1,0:T(4,128)(2,1)S(1)}, u32[]{:S(2)}, u32[]{:S(2)}) collective-permute-start(bf16[2,4,576]{2,1,0:T(4,128)(2,1)S(1)} %constant_dynamic-update-slice_fusion), channel_id=1, source_target_pairs={{2,4},{0,12},{6,0},{4,8},{3,10},{1,14},{7,2},{5,6},{8,9},{10,15},{... | collective-permute-start | bytes 27656 | tf_op jit(solution)/shard_map/ppermute | solution.py:551
  33.2 0.8 %collective-permute-start.3 = (bf16[12,48,128]{2,1,0:T(8,128)(2,1)S(1)}, bf16[12,48,128]{2,1,0:T(8,128)(2,1)S(1)}, u32[]{:S(2)}, u32[]{:S(2)}) collective-permute-start(bf16[12,48,128]{2,1,0:T(8,128)(2,1)S(1)} %bitcast.11), channel_id=1, source_target_pairs={{0,1},{1,0},{2,3},{3,2},{4,5},{5,4},{6,7},{7,6},{8,9},{9,8},{10,11... | collective-permute-start | bytes 442376 | tf_op jit(solution)/shard_map/ppermute | solution.py:552
  34.0 2.1 %collective-permute-start.2 = (bf16[2,4,576]{2,1,0:T(4,128)(2,1)S(1)}, bf16[2,4,576]{2,1,0:T(4,128)(2,1)S(1)}, u32[]{:S(2)}, u32[]{:S(2)}) collective-permute-start(bf16[2,4,576]{2,1,0:T(4,128)(2,1)S(1)} %constant_dynamic-update-slice_fusion), channel_id=1, source_target_pairs={{0,0},{2,8},{4,4},{6,12},{3,2},{1,6},{5,10},{7,14},{10,3},{8,7},{1... | collective-permute-start | bytes 27656 | tf_op jit(solution)/shard_map/ppermute | solution.py:551
  36.1 0.0 collective-permute-done.1
  36.1 3.7 %collective-permute-done.2 = bf16[2,4,576]{2,1,0:T(4,128)(2,1)S(1)} collective-permute-done((bf16[2,4,576]{2,1,0:T(4,128)(2,1)S(1)}, bf16[2,4,576]{2,1,0:T(4,128)(2,1)S(1)}, u32[]{:S(2)}, u32[]{:S(2)}) %collective-permute-start.2) | collective-permute-done | bytes 9248 | tf_op jit(solution)/shard_map/ppermute | solution.py:551
  39.9 0.1 collective-permute-start.4
  39.9 0.0 copy-done.1
  40.0 0.3 own.1
  40.3 0.0 collective-permute-done.3.far_ref
  40.3 0.5 %scores.1 = (f32[12,192,96]{2,1,0:T(8,128)S(1)}, bf16[12,96,128]{2,1,0:T(8,128)(2,1)S(1)}, f32[192,128]{1,0:T(8,128)S(1)}) custom-call(f32[8,128]{1,0:T(8,128)S(1)} %get-tuple-element.19.vectors_ref, bf16[4,4,576]{2,1,0:T(4,128)(2,1)S(1)} %constant_dynamic-update-slice_fusion.2.fetched_ref, bf16[12,48,128]{2,1,0:T(8,128)(2,1)S(1)} %get-tuple-element.24.q_ref, ...), custom_call_target="tpu_custom_call" | custom-call | tf_op jit(solution)/shard_map/scores/pallas_call | solution.py:568
  40.8 0.3 collective-permute-done.4.swapped_ref
  41.1 0.0 copy-done.2
  41.1 1.7 %attention.1 = f32[12,48,128]{2,1,0:T(8,128)} custom-call(f32[192,128]{1,0:T(8,128)S(1)} %get-tuple-element.28.bias_ref, bf16[4,4,576]{2,1,0:T(4,128)(2,1)S(1)} %collective-permute-done.4.swapped_ref, f32[12,192,96]{2,1,0:T(8,128)S(1)} %get-tuple-element.29.scores_ref, bf16[12,96,128]{2,1,0:T(8,128)(2,1)S(1)} %get-tuple-element.30.v_all_ref, ...), custom_call_target="tpu_custom_call" | custom-call | tf_op jit(solution)/shard_map/attention/pallas_call | solution.py:579
  (4 shorter events, 0.0 us)
Async XLA Ops:
  0.0 28.7 %copy-start = (f32[12,48,128]{2,1,0:T(8,128)S(1)}, f32[12,48,128]{2,1,0:T(8,128)}, u32[]{:S(2)}) copy-start(f32[12,48,128]{2,1,0:T(8,128)} %param.11) | copy-start | bytes 884740
  0.0 28.7 %copy-start.5 = (bf16[128,4]{0,1:T(4,128)(2,1)S(1)}, bf16[128,4]{0,1:T(4,128)(2,1)}, u32[]{:S(2)}) copy-start(bf16[128,4]{0,1:T(4,128)(2,1)} %param.20) | copy-start | bytes 3076
  0.0 28.7 %copy-start.4 = (bf16[128,128]{1,0:T(8,128)(2,1)S(1)}, bf16[128,128]{1,0:T(8,128)(2,1)}, u32[]{:S(2)}) copy-start(bf16[128,128]{1,0:T(8,128)(2,1)} %gate_w_ref.1) | copy-start | bytes 98308
  0.0 28.7 %copy-start.3 = (bf16[128,128]{1,0:T(8,128)(2,1)S(1)}, bf16[128,128]{1,0:T(8,128)(2,1)}, u32[]{:S(2)}) copy-start(bf16[128,128]{1,0:T(8,128)(2,1)} %out_w_ref.2) | copy-start | bytes 98308
  0.0 39.9 %copy-start.1 = (bf16[128,4,128]{2,1,0:T(4,128)(2,1)S(1)}, bf16[128,4,128]{2,1,0:T(4,128)(2,1)}, u32[]{:S(2)}) copy-start(bf16[128,4,128]{2,1,0:T(4,128)(2,1)} %w_ref.3) | copy-start | bytes 393220
  17.1 24.0 %copy-start.2 = (bf16[128,128]{1,0:T(8,128)(2,1)S(1)}, bf16[128,128]{1,0:T(8,128)(2,1)}, u32[]{:S(2)}) copy-start(bf16[128,128]{1,0:T(8,128)(2,1)} %out_w_ref.3) | copy-start | bytes 98308
  29.4 1.2 %collective-permute-start = (bf16[1,4,576]{2,1,0:T(4,128)(2,1)S(1)}, bf16[1,4,576]{2,1,0:T(4,128)(2,1)S(1)}, u32[]{:S(2)}, u32[]{:S(2)}) collective-permute-start(bf16[1,4,576]{2,1,0:T(4,128)(2,1)S(1)} %get-tuple-element.22), channel_id=1, source_target_pairs={{0,2},{2,0},{4,6},{6,4},{8,10},{10,8},{12,14},{14,12},{1,3},{3,1},... | collective-permute-start | bytes 13832 | tf_op jit(solution)/shard_map/ppermute | solution.py:544
  30.6 5.5 %collective-permute-start.1 = (bf16[2,4,576]{2,1,0:T(4,128)(2,1)S(1)}, bf16[2,4,576]{2,1,0:T(4,128)(2,1)S(1)}, u32[]{:S(2)}, u32[]{:S(2)}) collective-permute-start(bf16[2,4,576]{2,1,0:T(4,128)(2,1)S(1)} %constant_dynamic-update-slice_fusion), channel_id=1, source_target_pairs={{2,4},{0,12},{6,0},{4,8},{3,10},{1,14},{7,2},{5,6},{8,9},{10,15},{... | collective-permute-start | bytes 27656 | tf_op jit(solution)/shard_map/ppermute | solution.py:551
  33.2 7.1 %collective-permute-start.3 = (bf16[12,48,128]{2,1,0:T(8,128)(2,1)S(1)}, bf16[12,48,128]{2,1,0:T(8,128)(2,1)S(1)}, u32[]{:S(2)}, u32[]{:S(2)}) collective-permute-start(bf16[12,48,128]{2,1,0:T(8,128)(2,1)S(1)} %bitcast.11), channel_id=1, source_target_pairs={{0,1},{1,0},{2,3},{3,2},{4,5},{5,4},{6,7},{7,6},{8,9},{9,8},{10,11... | collective-permute-start | bytes 442376 | tf_op jit(solution)/shard_map/ppermute | solution.py:552
  34.0 5.9 %collective-permute-start.2 = (bf16[2,4,576]{2,1,0:T(4,128)(2,1)S(1)}, bf16[2,4,576]{2,1,0:T(4,128)(2,1)S(1)}, u32[]{:S(2)}, u32[]{:S(2)}) collective-permute-start(bf16[2,4,576]{2,1,0:T(4,128)(2,1)S(1)} %constant_dynamic-update-slice_fusion), channel_id=1, source_target_pairs={{0,0},{2,8},{4,4},{6,12},{3,2},{1,6},{5,10},{7,14},{10,3},{8,7},{1... | collective-permute-start | bytes 27656 | tf_op jit(solution)/shard_map/ppermute | solution.py:551
  39.9 1.3 %collective-permute-start.4 = (bf16[4,4,576]{2,1,0:T(4,128)(2,1)S(1)}, bf16[4,4,576]{2,1,0:T(4,128)(2,1)S(1)}, u32[]{:S(2)}, u32[]{:S(2)}) collective-permute-start(bf16[4,4,576]{2,1,0:T(4,128)(2,1)S(1)} %constant_dynamic-update-slice_fusion.2.fetched_ref), channel_id=1, source_target_pairs={{0,2},{2,0},{4,6},{6,4},{8,10},{10,8},{12,14},{14,12},{1,3},{3,1},... | collective-permute-start | bytes 55304 | tf_op jit(solution)/shard_map/ppermute | solution.py:544

commit v7 on v6

--- a/solution.py
+++ b/solution.py
@@ -326,9 +326,9 @@
     return trips, codes
 
 
-FIRST = (((1, 3), (2, 3)), ((2, 3), (2, 3)))
-SWAPPED = ((), (0, 1, 3))
-TURNED = (((1, 0), (1, 1)), ((1, 0), (1, 0)), ((0, 1), (0, 1)), ((0, 0), (0, 1)))
+FIRST = (((0, 1), (0, 2)), ((0, 1), (1, 2)))
+SWAPPED = ((1,), (0, 1, 2, 3))
+TURNED = (((1, 0), (1, 0)), ((0, 1), (1, 1)), ((1, 0), (0, 0)), ((0, 1), (0, 0)))
 
 
 def fetch_code(codes, row, col):

time: 43.4 us -> 41.8 us (0.963)
  the two profiles are of different devices: /device:TPU:6 before, /device:TPU:0 now
where the time goes in v7:
time: 41.8 us; the launch traced here: 41.6 us
  blocking collectives  28.7 us (69%)
  Pallas kernels  5.5 us (13%)
  waiting for transfers between devices  3.97 us (9%)
  starting transfers between devices  3.24 us (8%)
    all_to_all x1, blocking collectives, body_channels(): lr = lax.all_to_all(lr, group, 0, 0, tiled=True)  17.8 us
    all_to_all x1, blocking collectives, body_channels(): sums = lax.all_to_all(sums, group, 0, 0, tiled=True)  10.9 us
    ppermute x2, waiting for transfers between devices, body_channels(): fetched.append(lax.ppermute(bias, group, trips[p]))  2.29 us
    pallas_call x1, Pallas kernels, body_channels(): pl.pallas_call(functools.partial(attention_kernel, codes), out_shape=jax....  1.69 us
    pallas_call x1, Pallas kernels, body_channels(): pl.pallas_call(functools.partial(factors_kernel, devices), out_shape=(plt...  1.69 us
    ppermute x2, starting transfers between devices, body_channels(): fetched.append(lax.ppermute(bias, group, trips[p]))  1.57 us
    ppermute x1, starting transfers between devices, body_channels(): far = lax.ppermute(att, ('col', 'sub'), [(c, c ^ 1) for c in range(cols)])  1.48 us
    ppermute x2, waiting for transfers between devices, swap(): return lax.ppermute(v, 'row', [(r, r ^ 1) for r in range(rows)])  1.05 us
  transfers between devices with their start and end apart: 5, of which 3 were waited for; matrix products, arithmetic and copies ran while one was open for 0% of the time, Pallas kernels for 2%

profile of v7, /device:TPU:0, one launch (start us, length us, event | category | flops | bytes accessed | tf_op | source)
XLA Modules:
  0.0 41.6 jit_solution(5802763245169000030)
XLA Ops:
  0.0 0.0 copy-start
  0.0 0.0 copy-start.5
  0.0 0.0 copy-start.4
  0.0 0.0 copy-start.3
  0.0 0.0 copy-start.1
  0.0 1.7 %factors.1 = (bf16[16,9,8,128]{3,2,1,0:T(8,128)(2,1)S(1)}, bf16[576,128]{1,0:T(8,128)(2,1)S(1)}, f32[8,128]{1,0:T(8,128)S(1)}) custom-call(f32[576,128]{1,0:T(8,128)} %bitcast.8, f32[1,128]{1,0:T(1,128)} %bitcast.14, bf16[128,4,128]{2,1,0:T(4,128)(2,1)} %w_ref.2, s32[1,96]{1,0:T(1,128)} %bitcast.15, f32[1,128]{1,0:T(1,128)} %bitcast.16, f32[1,128]{1,0:T(1,128)} %bitcast.17), custom_call_target="tpu_custom_call" | custom-call | tf_op jit(solution)/shard_map/factors/pallas_call | solution.py:484
  1.7 17.8 %all_to_all.10.lr_ref = bf16[16,9,8,128]{3,2,1,0:T(8,128)(2,1)S(1)} all-to-all(bf16[16,9,8,128]{3,2,1,0:T(8,128)(2,1)S(1)} %get-tuple-element.21), channel_id=1, replica_groups=mesh['parts'=2,'row'=8,'col'=2,'sub'=1] {'row','col','sub'}, dimensions={0} | all-to-all | bytes 589824 | tf_op jit(solution)/shard_map/all_to_all | solution.py:507
  19.5 0.0 copy-start.2
  19.5 0.7 %triangle.1 = bf16[16,5,8,128]{3,2,1,0:T(8,128)(2,1)S(1)} custom-call(f32[8,128]{1,0:T(8,128)S(1)} %get-tuple-element.19.vectors_ref, bf16[16,9,8,128]{3,2,1,0:T(8,128)(2,1)S(1)} %all_to_all.10.lr_ref), custom_call_target="tpu_custom_call" | custom-call | tf_op jit(solution)/shard_map/triangle/pallas_call | solution.py:508
  20.2 10.9 %all_to_all.11.sum_ref = bf16[16,5,8,128]{3,2,1,0:T(8,128)(2,1)S(1)} all-to-all(bf16[16,5,8,128]{3,2,1,0:T(8,128)(2,1)S(1)} %triangle.1), channel_id=1, replica_groups=mesh['parts'=2,'row'=8,'col'=2,'sub'=1] {'row','col','sub'}, dimensions={0} | all-to-all | bytes 327680 | tf_op jit(solution)/shard_map/all_to_all | solution.py:515
  31.1 0.0 copy-done
  31.1 0.0 copy-done.5
  31.1 0.0 copy-done.4
  31.1 0.0 copy-done.3
  31.2 0.6 %middle.1 = (f32[576,128]{1,0:T(8,128)S(1)}, bf16[576,128]{1,0:T(8,128)(2,1)S(1)}, bf16[1,4,576]{2,1,0:T(4,128)(2,1)S(1)}) custom-call(f32[576,128]{1,0:T(8,128)S(1)} %bitcast.9, bf16[576,128]{1,0:T(8,128)(2,1)S(1)} %get-tuple-element.20.normed_ref, bf16[16,5,8,128]{3,2,1,0:T(8,128)(2,1)S(1)} %all_to_all.11.sum_ref, ...), custom_call_target="tpu_custom_call" | custom-call | tf_op jit(solution)/shard_map/middle/pallas_call | solution.py:518
  31.8 0.1 collective-permute-start
  31.9 1.1 %collective-permute-done = bf16[1,4,576]{2,1,0:T(4,128)(2,1)S(1)} collective-permute-done((bf16[1,4,576]{2,1,0:T(4,128)(2,1)S(1)}, bf16[1,4,576]{2,1,0:T(4,128)(2,1)S(1)}, u32[]{:S(2)}, u32[]{:S(2)}) %collective-permute-start) | collective-permute-done | bytes 4640 | tf_op jit(solution)/shard_map/ppermute | solution.py:544
  33.0 0.8 %collective-permute-start.1 = (bf16[2,4,576]{2,1,0:T(4,128)(2,1)S(1)}, bf16[2,4,576]{2,1,0:T(4,128)(2,1)S(1)}, u32[]{:S(2)}, u32[]{:S(2)}) collective-permute-start(bf16[2,4,576]{2,1,0:T(4,128)(2,1)S(1)} %constant_dynamic-update-slice_fusion), channel_id=1, source_target_pairs={{2,0},{0,6},{4,8},{6,12},{3,2},{1,10},{7,4},{5,14},{10,3},{8,7},{1... | collective-permute-start | bytes 27656 | tf_op jit(solution)/shard_map/ppermute | solution.py:551
  33.8 1.5 %collective-permute-start.3 = (bf16[12,48,128]{2,1,0:T(8,128)(2,1)S(1)}, bf16[12,48,128]{2,1,0:T(8,128)(2,1)S(1)}, u32[]{:S(2)}, u32[]{:S(2)}) collective-permute-start(bf16[12,48,128]{2,1,0:T(8,128)(2,1)S(1)} %bitcast.11), channel_id=1, source_target_pairs={{0,1},{1,0},{2,3},{3,2},{4,5},{5,4},{6,7},{7,6},{8,9},{9,8},{10,11... | collective-permute-start | bytes 442376 | tf_op jit(solution)/shard_map/ppermute | solution.py:552
  35.3 0.8 %collective-permute-start.2 = (bf16[2,4,576]{2,1,0:T(4,128)(2,1)S(1)}, bf16[2,4,576]{2,1,0:T(4,128)(2,1)S(1)}, u32[]{:S(2)}, u32[]{:S(2)}) collective-permute-start(bf16[2,4,576]{2,1,0:T(4,128)(2,1)S(1)} %constant_dynamic-update-slice_fusion), channel_id=1, source_target_pairs={{0,8},{2,12},{6,0},{4,6},{1,4},{3,14},{7,2},{5,10},{8,11},{10,15},... | collective-permute-start | bytes 27656 | tf_op jit(solution)/shard_map/ppermute | solution.py:551
  36.0 0.0 collective-permute-done.1
  36.1 2.3 %collective-permute-done.2 = bf16[2,4,576]{2,1,0:T(4,128)(2,1)S(1)} collective-permute-done((bf16[2,4,576]{2,1,0:T(4,128)(2,1)S(1)}, bf16[2,4,576]{2,1,0:T(4,128)(2,1)S(1)}, u32[]{:S(2)}, u32[]{:S(2)}) %collective-permute-start.2) | collective-permute-done | bytes 9248 | tf_op jit(solution)/shard_map/ppermute | solution.py:551
  38.4 0.1 collective-permute-start.4
  38.4 0.0 copy-done.1
  38.4 0.3 own.1
  38.8 0.6 %collective-permute-done.3.far_ref = bf16[12,48,128]{2,1,0:T(8,128)(2,1)S(1)} collective-permute-done((bf16[12,48,128]{2,1,0:T(8,128)(2,1)S(1)}, bf16[12,48,128]{2,1,0:T(8,128)(2,1)S(1)}, u32[]{:S(2)}, u32[]{:S(2)}) %collective-permute-start.3) | collective-permute-done | bytes 147488 | tf_op jit(solution)/shard_map/ppermute | solution.py:552
  39.4 0.5 %scores.1 = (f32[12,192,96]{2,1,0:T(8,128)S(1)}, bf16[12,96,128]{2,1,0:T(8,128)(2,1)S(1)}, f32[192,128]{1,0:T(8,128)S(1)}) custom-call(f32[8,128]{1,0:T(8,128)S(1)} %get-tuple-element.19.vectors_ref, bf16[4,4,576]{2,1,0:T(4,128)(2,1)S(1)} %constant_dynamic-update-slice_fusion.2.fetched_ref, bf16[12,48,128]{2,1,0:T(8,128)(2,1)S(1)} %get-tuple-element.24.q_ref, ...), custom_call_target="tpu_custom_call" | custom-call | tf_op jit(solution)/shard_map/scores/pallas_call | solution.py:568
  39.9 0.0 collective-permute-done.4.swapped_ref
  39.9 0.0 copy-done.2
  39.9 1.7 %attention.1 = f32[12,48,128]{2,1,0:T(8,128)} custom-call(f32[192,128]{1,0:T(8,128)S(1)} %get-tuple-element.28.bias_ref, bf16[4,4,576]{2,1,0:T(4,128)(2,1)S(1)} %collective-permute-done.4.swapped_ref, f32[12,192,96]{2,1,0:T(8,128)S(1)} %get-tuple-element.29.scores_ref, bf16[12,96,128]{2,1,0:T(8,128)(2,1)S(1)} %get-tuple-element.30.v_all_ref, ...), custom_call_target="tpu_custom_call" | custom-call | tf_op jit(solution)/shard_map/attention/pallas_call | solution.py:579
  (4 shorter events, 0.0 us)
Async XLA Ops:
  0.0 31.1 %copy-start = (f32[12,48,128]{2,1,0:T(8,128)S(1)}, f32[12,48,128]{2,1,0:T(8,128)}, u32[]{:S(2)}) copy-start(f32[12,48,128]{2,1,0:T(8,128)} %param.11) | copy-start | bytes 884740
  0.0 31.1 %copy-start.5 = (bf16[128,4]{0,1:T(4,128)(2,1)S(1)}, bf16[128,4]{0,1:T(4,128)(2,1)}, u32[]{:S(2)}) copy-start(bf16[128,4]{0,1:T(4,128)(2,1)} %param.20) | copy-start | bytes 3076
  0.0 31.1 %copy-start.4 = (bf16[128,128]{1,0:T(8,128)(2,1)S(1)}, bf16[128,128]{1,0:T(8,128)(2,1)}, u32[]{:S(2)}) copy-start(bf16[128,128]{1,0:T(8,128)(2,1)} %gate_w_ref.1) | copy-start | bytes 98308
  0.0 31.1 %copy-start.3 = (bf16[128,128]{1,0:T(8,128)(2,1)S(1)}, bf16[128,128]{1,0:T(8,128)(2,1)}, u32[]{:S(2)}) copy-start(bf16[128,128]{1,0:T(8,128)(2,1)} %out_w_ref.2) | copy-start | bytes 98308
  0.0 38.4 %copy-start.1 = (bf16[128,4,128]{2,1,0:T(4,128)(2,1)S(1)}, bf16[128,4,128]{2,1,0:T(4,128)(2,1)}, u32[]{:S(2)}) copy-start(bf16[128,4,128]{2,1,0:T(4,128)(2,1)} %w_ref.3) | copy-start | bytes 393220
  19.5 20.4 %copy-start.2 = (bf16[128,128]{1,0:T(8,128)(2,1)S(1)}, bf16[128,128]{1,0:T(8,128)(2,1)}, u32[]{:S(2)}) copy-start(bf16[128,128]{1,0:T(8,128)(2,1)} %out_w_ref.3) | copy-start | bytes 98308
  31.8 1.2 %collective-permute-start = (bf16[1,4,576]{2,1,0:T(4,128)(2,1)S(1)}, bf16[1,4,576]{2,1,0:T(4,128)(2,1)S(1)}, u32[]{:S(2)}, u32[]{:S(2)}) collective-permute-start(bf16[1,4,576]{2,1,0:T(4,128)(2,1)S(1)} %get-tuple-element.22), channel_id=1, source_target_pairs={{0,2},{2,0},{4,6},{6,4},{8,10},{10,8},{12,14},{14,12},{1,3},{3,1},... | collective-permute-start | bytes 13832 | tf_op jit(solution)/shard_map/ppermute | solution.py:544
  33.0 3.1 %collective-permute-start.1 = (bf16[2,4,576]{2,1,0:T(4,128)(2,1)S(1)}, bf16[2,4,576]{2,1,0:T(4,128)(2,1)S(1)}, u32[]{:S(2)}, u32[]{:S(2)}) collective-permute-start(bf16[2,4,576]{2,1,0:T(4,128)(2,1)S(1)} %constant_dynamic-update-slice_fusion), channel_id=1, source_target_pairs={{2,0},{0,6},{4,8},{6,12},{3,2},{1,10},{7,4},{5,14},{10,3},{8,7},{1... | collective-permute-start | bytes 27656 | tf_op jit(solution)/shard_map/ppermute | solution.py:551
  33.8 5.7 %collective-permute-start.3 = (bf16[12,48,128]{2,1,0:T(8,128)(2,1)S(1)}, bf16[12,48,128]{2,1,0:T(8,128)(2,1)S(1)}, u32[]{:S(2)}, u32[]{:S(2)}) collective-permute-start(bf16[12,48,128]{2,1,0:T(8,128)(2,1)S(1)} %bitcast.11), channel_id=1, source_target_pairs={{0,1},{1,0},{2,3},{3,2},{4,5},{5,4},{6,7},{7,6},{8,9},{9,8},{10,11... | collective-permute-start | bytes 442376 | tf_op jit(solution)/shard_map/ppermute | solution.py:552
  35.3 3.1 %collective-permute-start.2 = (bf16[2,4,576]{2,1,0:T(4,128)(2,1)S(1)}, bf16[2,4,576]{2,1,0:T(4,128)(2,1)S(1)}, u32[]{:S(2)}, u32[]{:S(2)}) collective-permute-start(bf16[2,4,576]{2,1,0:T(4,128)(2,1)S(1)} %constant_dynamic-update-slice_fusion), channel_id=1, source_target_pairs={{0,8},{2,12},{6,0},{4,6},{1,4},{3,14},{7,2},{5,10},{8,11},{10,15},... | collective-permute-start | bytes 27656 | tf_op jit(solution)/shard_map/ppermute | solution.py:551
  38.4 1.5 %collective-permute-start.4 = (bf16[4,4,576]{2,1,0:T(4,128)(2,1)S(1)}, bf16[4,4,576]{2,1,0:T(4,128)(2,1)S(1)}, u32[]{:S(2)}, u32[]{:S(2)}) collective-permute-start(bf16[4,4,576]{2,1,0:T(4,128)(2,1)S(1)} %constant_dynamic-update-slice_fusion.2.fetched_ref), channel_id=1, source_target_pairs={{0,2},{2,0},{4,6},{6,4},{8,10},{10,8},{12,14},{14,12},{1,3},{3,1},... | collective-permute-start | bytes 55304 | tf_op jit(solution)/shard_map/ppermute | solution.py:544

commit v8 on v7

--- a/solution.py
+++ b/solution.py
@@ -168,9 +168,11 @@
     lr_ref,
     normed_ref,
     rows_ref,
+    kept_ref,
     w_scratch,
 ):
     cells, _ = pair_ref.shape
+    kept_ref[...] = pair_ref[...]
     live = live_ref[...].astype(f32)
     rows_ref[0:1] = jnp.concatenate([live, jnp.zeros((1, LANES - live.shape[1]), f32)], axis=1)
     rows_ref[1:2] = out_gain_ref[...]
@@ -179,17 +181,17 @@
     own = hidden // devices
     normed = norm_last(pair_ref[...], gain_ref[...]).astype(bf16)
     normed_ref[...] = normed
-    w_t = [jnp.transpose(w).astype(bf16) for w in split_weight(w_ref, w_scratch)]
+    w = [w.astype(bf16) for w in split_weight(w_ref, w_scratch)]
     spare = (-cells) % LANES
     tiles = (cells + spare) // LANES
     if spare:
         tail = normed[:spare]
-        rhs_left = jnp.concatenate([normed, tail], axis=0)
-        rhs_right = jnp.concatenate([tail, normed], axis=0)
+        rows_left = jnp.concatenate([normed, tail], axis=0)
+        rows_right = jnp.concatenate([tail, normed], axis=0)
     else:
-        rhs_left = rhs_right = normed
-    left = sigmoid(dot_nt(w_t[0], rhs_left)) * dot_nt(w_t[1], rhs_left)
-    right = sigmoid(dot_nt(w_t[2], rhs_right)) * dot_nt(w_t[3], rhs_right)
+        rows_left = rows_right = normed
+    left = jnp.transpose(sigmoid(dot_nn(rows_left, w[0])) * dot_nn(rows_left, w[1]))
+    right = jnp.transpose(sigmoid(dot_nn(rows_right, w[2])) * dot_nn(rows_right, w[3]))
     panels = [left[:, t * LANES : (t + 1) * LANES] for t in range(tiles)]
     right_panels = [right[:, t * LANES : (t + 1) * LANES] for t in range(tiles)]
     if spare:
@@ -240,7 +242,7 @@
     keep = live_wide > 0
     for h in range(own):
         left = jnp.where(keep, left_scratch[pl.ds(h, residues, stride=own), :], 0.0).astype(bf16)
-        right = jnp.where(keep, right_scratch[pl.ds(h, residues, stride=own), :], 0.0).astype(bf16)
+        right = right_scratch[pl.ds(h, residues, stride=own), :].astype(bf16)
         right = jnp.concatenate([right, jnp.zeros((LANES - residues, LANES), bf16)], axis=0)
         sum_scratch[pl.ds(h, residues, stride=own), :] = dot_nt(left, right) * both
     tiles = sum_ref.shape[1]
@@ -481,12 +483,13 @@
     flat = pair.reshape(cells, chan)
     live = residue_mask.reshape(1, residues)
 
-    lr, normed, vectors = pl.pallas_call(
+    lr, normed, vectors, kept = pl.pallas_call(
         functools.partial(factors_kernel, devices),
         out_shape=(
             pltpu.VMEM((devices, lr_panels, own, LANES), bf16),
             pltpu.VMEM((cells, chan), bf16),
             pltpu.VMEM((8, LANES), f32),
+            pltpu.VMEM((cells, chan), f32),
         ),
         scratch_shapes=[pltpu.VMEM((chan * tri_in_weight.shape[1], hidden), f32)],
         compiler_params=kernel_params,
@@ -514,7 +517,7 @@
     )(near(vectors), near(lr))
     sums = lax.all_to_all(sums, group, 0, 0, tiled=True)
     shape = (rows_here, cols_here, chan)
-    chunks = math.gcd(rows_here, 3)
+    chunks = math.gcd(rows_here, 2)
     mid, att, bias = pl.pallas_call(
         middle_kernel,
         out_shape=(
@@ -528,7 +531,7 @@
         *map(
             near,
             (
-                flat,
+                kept,
                 normed,
                 sums,
                 vectors,

time: 41.8 us -> 41.7 us (level)
  the two profiles are of different devices: /device:TPU:0 before, /device:TPU:9 now
where the time goes in v8:
time: 41.7 us; the launch traced here: 41.5 us
  blocking collectives  26.9 us (65%)
  starting transfers between devices  7.39 us (18%)
  Pallas kernels  5.43 us (13%)
  waiting for transfers between devices  1.64 us (4%)
    all_to_all x1, blocking collectives, body_channels(): lr = lax.all_to_all(lr, group, 0, 0, tiled=True)  16 us
    all_to_all x1, blocking collectives, body_channels(): sums = lax.all_to_all(sums, group, 0, 0, tiled=True)  10.9 us
    ppermute x2, starting transfers between devices, swap(): return lax.ppermute(v, 'row', [(r, r ^ 1) for r in range(rows)])  4.13 us
    ppermute x2, starting transfers between devices, body_channels(): fetched.append(lax.ppermute(bias, group, trips[p]))  2.97 us
    pallas_call x1, Pallas kernels, body_channels(): pl.pallas_call(functools.partial(factors_kernel, devices), out_shape=(plt...  1.71 us
    pallas_call x1, Pallas kernels, body_channels(): pl.pallas_call(functools.partial(attention_kernel, codes), out_shape=jax....  1.6 us
    ppermute x2, waiting for transfers between devices, swap(): return lax.ppermute(v, 'row', [(r, r ^ 1) for r in range(rows)])  0.83 us
  transfers between devices with their start and end apart: 5, of which 2 were waited for; matrix products, arithmetic and copies ran while one was open for 0% of the time, Pallas kernels for 2%

profile of v8, /device:TPU:9, one launch (start us, length us, event | category | flops | bytes accessed | tf_op | source)
XLA Modules:
  0.0 41.5 jit_solution(17658431067076765786)
XLA Ops:
  0.0 0.0 copy-start.4
  0.0 0.0 copy-start.3
  0.0 0.0 copy-start.2
  0.0 0.0 copy-start
  0.0 1.7 %factors.1 = (bf16[16,9,8,128]{3,2,1,0:T(8,128)(2,1)S(1)}, bf16[576,128]{1,0:T(8,128)(2,1)S(1)}, f32[8,128]{1,0:T(8,128)S(1)}, f32[576,128]{1,0:T(8,128)S(1)}) custom-call(f32[576,128]{1,0:T(8,128)} %bitcast.12, f32[1,128]{1,0:T(1,128)} %bitcast.13, bf16[128,4,128]{2,1,0:T(4,128)(2,1)} %w_ref.2, s32[1,96]{1,0:T(1,128)} %bitcast.14, f32[1,128]{1,0:T(1,128)} %bitcast.15, ...), custom_call_target="tpu_custom_call" | custom-call | tf_op jit(solution)/shard_map/factors/pallas_call | solution.py:486
  1.7 16.0 %all_to_all.10.lr_ref = bf16[16,9,8,128]{3,2,1,0:T(8,128)(2,1)S(1)} all-to-all(bf16[16,9,8,128]{3,2,1,0:T(8,128)(2,1)S(1)} %get-tuple-element.23), channel_id=1, replica_groups=mesh['parts'=2,'row'=8,'col'=2,'sub'=1] {'row','col','sub'}, dimensions={0} | all-to-all | bytes 589824 | tf_op jit(solution)/shard_map/all_to_all | solution.py:510
  17.7 0.0 copy-start.1
  17.7 0.7 %triangle.1 = bf16[16,5,8,128]{3,2,1,0:T(8,128)(2,1)S(1)} custom-call(f32[8,128]{1,0:T(8,128)S(1)} %get-tuple-element.20.vectors_ref, bf16[16,9,8,128]{3,2,1,0:T(8,128)(2,1)S(1)} %all_to_all.10.lr_ref), custom_call_target="tpu_custom_call" | custom-call | tf_op jit(solution)/shard_map/triangle/pallas_call | solution.py:511
  18.4 10.9 %all_to_all.11.sum_ref = bf16[16,5,8,128]{3,2,1,0:T(8,128)(2,1)S(1)} all-to-all(bf16[16,5,8,128]{3,2,1,0:T(8,128)(2,1)S(1)} %triangle.1), channel_id=1, replica_groups=mesh['parts'=2,'row'=8,'col'=2,'sub'=1] {'row','col','sub'}, dimensions={0} | all-to-all | bytes 327680 | tf_op jit(solution)/shard_map/all_to_all | solution.py:518
  29.4 0.0 copy-done.4
  29.4 0.0 copy-done.3
  29.4 0.0 copy-done.2
  29.4 0.6 %middle.1 = (f32[576,128]{1,0:T(8,128)S(1)}, bf16[576,128]{1,0:T(8,128)(2,1)S(1)}, bf16[1,4,576]{2,1,0:T(4,128)(2,1)S(1)}) custom-call(f32[576,128]{1,0:T(8,128)S(1)} %get-tuple-element.21.pair_ref, bf16[576,128]{1,0:T(8,128)(2,1)S(1)} %get-tuple-element.22.normed_ref, bf16[16,5,8,128]{3,2,1,0:T(8,128)(2,1)S(1)} %all_to_all.11.sum_ref, ...), custom_call_target="tpu_custom_call" | custom-call | tf_op jit(solution)/shard_map/middle/pallas_call | solution.py:521
  30.0 0.4 collective-permute-start
  30.4 0.8 %collective-permute-done = bf16[1,4,576]{2,1,0:T(4,128)(2,1)S(1)} collective-permute-done((bf16[1,4,576]{2,1,0:T(4,128)(2,1)S(1)}, bf16[1,4,576]{2,1,0:T(4,128)(2,1)S(1)}, u32[]{:S(2)}, u32[]{:S(2)}) %collective-permute-start) | collective-permute-done | bytes 4640 | tf_op jit(solution)/shard_map/ppermute | solution.py:547
  31.2 1.5 %collective-permute-start.1 = (bf16[2,4,576]{2,1,0:T(4,128)(2,1)S(1)}, bf16[2,4,576]{2,1,0:T(4,128)(2,1)S(1)}, u32[]{:S(2)}, u32[]{:S(2)}) collective-permute-start(bf16[2,4,576]{2,1,0:T(4,128)(2,1)S(1)} %constant_dynamic-update-slice_fusion), channel_id=1, source_target_pairs={{2,0},{0,6},{4,8},{6,12},{3,2},{1,10},{7,4},{5,14},{10,3},{8,7},{1... | collective-permute-start | bytes 27656 | tf_op jit(solution)/shard_map/ppermute | solution.py:554
  32.7 0.3 collective-permute-start.3
  33.0 1.5 %collective-permute-start.2 = (bf16[2,4,576]{2,1,0:T(4,128)(2,1)S(1)}, bf16[2,4,576]{2,1,0:T(4,128)(2,1)S(1)}, u32[]{:S(2)}, u32[]{:S(2)}) collective-permute-start(bf16[2,4,576]{2,1,0:T(4,128)(2,1)S(1)} %constant_dynamic-update-slice_fusion), channel_id=1, source_target_pairs={{0,8},{2,12},{6,0},{4,6},{1,4},{3,14},{7,2},{5,10},{8,11},{10,15},... | collective-permute-start | bytes 27656 | tf_op jit(solution)/shard_map/ppermute | solution.py:554
  34.5 0.0 collective-permute-done.1
  34.5 0.8 %collective-permute-done.2 = bf16[2,4,576]{2,1,0:T(4,128)(2,1)S(1)} collective-permute-done((bf16[2,4,576]{2,1,0:T(4,128)(2,1)S(1)}, bf16[2,4,576]{2,1,0:T(4,128)(2,1)S(1)}, u32[]{:S(2)}, u32[]{:S(2)}) %collective-permute-start.2) | collective-permute-done | bytes 9248 | tf_op jit(solution)/shard_map/ppermute | solution.py:554
  35.3 3.7 %collective-permute-start.4 = (bf16[4,4,576]{2,1,0:T(4,128)(2,1)S(1)}, bf16[4,4,576]{2,1,0:T(4,128)(2,1)S(1)}, u32[]{:S(2)}, u32[]{:S(2)}) collective-permute-start(bf16[4,4,576]{2,1,0:T(4,128)(2,1)S(1)} %constant_dynamic-update-slice_fusion.2.fetched_ref), channel_id=1, source_target_pairs={{0,2},{2,0},{4,6},{6,4},{8,10},{10,8},{12,14},{14,12},{1,3},{3,1},... | collective-permute-start | bytes 55304 | tf_op jit(solution)/shard_map/ppermute | solution.py:547
  39.1 0.0 copy-done
  39.1 0.3 own.1
  39.4 0.0 collective-permute-done.3.far_ref
  39.4 0.5 %scores.1 = (f32[12,192,96]{2,1,0:T(8,128)S(1)}, bf16[12,96,128]{2,1,0:T(8,128)(2,1)S(1)}, f32[192,128]{1,0:T(8,128)S(1)}) custom-call(f32[8,128]{1,0:T(8,128)S(1)} %get-tuple-element.20.vectors_ref, bf16[4,4,576]{2,1,0:T(4,128)(2,1)S(1)} %constant_dynamic-update-slice_fusion.2.fetched_ref, bf16[12,48,128]{2,1,0:T(8,128)(2,1)S(1)} %get-tuple-element.26.q_ref, ...), custom_call_target="tpu_custom_call" | custom-call | tf_op jit(solution)/shard_map/scores/pallas_call | solution.py:571
  39.9 0.0 collective-permute-done.4.swapped_ref
  39.9 0.0 copy-done.1
  39.9 1.6 %attention.1 = f32[12,48,128]{2,1,0:T(8,128)} custom-call(f32[192,128]{1,0:T(8,128)S(1)} %get-tuple-element.30.bias_ref, bf16[4,4,576]{2,1,0:T(4,128)(2,1)S(1)} %collective-permute-done.4.swapped_ref, f32[12,192,96]{2,1,0:T(8,128)S(1)} %get-tuple-element.31.scores_ref, bf16[12,96,128]{2,1,0:T(8,128)(2,1)S(1)} %get-tuple-element.32.v_all_ref, ...), custom_call_target="tpu_custom_call" | custom-call | tf_op jit(solution)/shard_map/attention/pallas_call | solution.py:582
  (4 shorter events, 0.0 us)
Async XLA Ops:
  0.0 29.4 %copy-start.4 = (bf16[128,4]{0,1:T(4,128)(2,1)S(1)}, bf16[128,4]{0,1:T(4,128)(2,1)}, u32[]{:S(2)}) copy-start(bf16[128,4]{0,1:T(4,128)(2,1)} %param.20) | copy-start | bytes 3076
  0.0 29.4 %copy-start.3 = (bf16[128,128]{1,0:T(8,128)(2,1)S(1)}, bf16[128,128]{1,0:T(8,128)(2,1)}, u32[]{:S(2)}) copy-start(bf16[128,128]{1,0:T(8,128)(2,1)} %gate_w_ref.1) | copy-start | bytes 98308
  0.0 29.4 %copy-start.2 = (bf16[128,128]{1,0:T(8,128)(2,1)S(1)}, bf16[128,128]{1,0:T(8,128)(2,1)}, u32[]{:S(2)}) copy-start(bf16[128,128]{1,0:T(8,128)(2,1)} %out_w_ref.2) | copy-start | bytes 98308
  0.0 39.1 %copy-start = (bf16[128,4,128]{2,1,0:T(4,128)(2,1)S(1)}, bf16[128,4,128]{2,1,0:T(4,128)(2,1)}, u32[]{:S(2)}) copy-start(bf16[128,4,128]{2,1,0:T(4,128)(2,1)} %w_ref.3) | copy-start | bytes 393220
  17.7 22.2 %copy-start.1 = (bf16[128,128]{1,0:T(8,128)(2,1)S(1)}, bf16[128,128]{1,0:T(8,128)(2,1)}, u32[]{:S(2)}) copy-start(bf16[128,128]{1,0:T(8,128)(2,1)} %out_w_ref.3) | copy-start | bytes 98308
  30.0 1.2 %collective-permute-start = (bf16[1,4,576]{2,1,0:T(4,128)(2,1)S(1)}, bf16[1,4,576]{2,1,0:T(4,128)(2,1)S(1)}, u32[]{:S(2)}, u32[]{:S(2)}) collective-permute-start(bf16[1,4,576]{2,1,0:T(4,128)(2,1)S(1)} %get-tuple-element.24), channel_id=1, source_target_pairs={{0,2},{2,0},{4,6},{6,4},{8,10},{10,8},{12,14},{14,12},{1,3},{3,1},... | collective-permute-start | bytes 13832 | tf_op jit(solution)/shard_map/ppermute | solution.py:547
  31.2 3.3 %collective-permute-start.1 = (bf16[2,4,576]{2,1,0:T(4,128)(2,1)S(1)}, bf16[2,4,576]{2,1,0:T(4,128)(2,1)S(1)}, u32[]{:S(2)}, u32[]{:S(2)}) collective-permute-start(bf16[2,4,576]{2,1,0:T(4,128)(2,1)S(1)} %constant_dynamic-update-slice_fusion), channel_id=1, source_target_pairs={{2,0},{0,6},{4,8},{6,12},{3,2},{1,10},{7,4},{5,14},{10,3},{8,7},{1... | collective-permute-start | bytes 27656 | tf_op jit(solution)/shard_map/ppermute | solution.py:554
  32.7 6.7 %collective-permute-start.3 = (bf16[12,48,128]{2,1,0:T(8,128)(2,1)S(1)}, bf16[12,48,128]{2,1,0:T(8,128)(2,1)S(1)}, u32[]{:S(2)}, u32[]{:S(2)}) collective-permute-start(bf16[12,48,128]{2,1,0:T(8,128)(2,1)S(1)} %bitcast.9), channel_id=1, source_target_pairs={{0,1},{1,0},{2,3},{3,2},{4,5},{5,4},{6,7},{7,6},{8,9},{9,8},{10,11... | collective-permute-start | bytes 442376 | tf_op jit(solution)/shard_map/ppermute | solution.py:555
  33.0 2.3 %collective-permute-start.2 = (bf16[2,4,576]{2,1,0:T(4,128)(2,1)S(1)}, bf16[2,4,576]{2,1,0:T(4,128)(2,1)S(1)}, u32[]{:S(2)}, u32[]{:S(2)}) collective-permute-start(bf16[2,4,576]{2,1,0:T(4,128)(2,1)S(1)} %constant_dynamic-update-slice_fusion), channel_id=1, source_target_pairs={{0,8},{2,12},{6,0},{4,6},{1,4},{3,14},{7,2},{5,10},{8,11},{10,15},... | collective-permute-start | bytes 27656 | tf_op jit(solution)/shard_map/ppermute | solution.py:554
  35.3 4.6 %collective-permute-start.4 = (bf16[4,4,576]{2,1,0:T(4,128)(2,1)S(1)}, bf16[4,4,576]{2,1,0:T(4,128)(2,1)S(1)}, u32[]{:S(2)}, u32[]{:S(2)}) collective-permute-start(bf16[4,4,576]{2,1,0:T(4,128)(2,1)S(1)} %constant_dynamic-update-slice_fusion.2.fetched_ref), channel_id=1, source_target_pairs={{0,2},{2,0},{4,6},{6,4},{8,10},{10,8},{12,14},{14,12},{1,3},{3,1},... | collective-permute-start | bytes 55304 | tf_op jit(solution)/shard_map/ppermute | solution.py:547

commit v9 on v8

--- a/solution.py
+++ b/solution.py
@@ -157,26 +157,26 @@
     return [w_scratch[pl.ds(p, rows, stride=mats), :] for p in range(mats)]
 
 
+def live_lanes(live_ref):
+    live = live_ref[...].astype(f32)
+    return jnp.concatenate([live, jnp.zeros((1, LANES - live.shape[1]), f32)], axis=1)
+
+
 def factors_kernel(
     devices,
     pair_ref,
     gain_ref,
     w_ref,
     live_ref,
-    out_gain_ref,
-    att_gain_ref,
     lr_ref,
     normed_ref,
-    rows_ref,
+    lanes_ref,
     kept_ref,
     w_scratch,
 ):
     cells, _ = pair_ref.shape
     kept_ref[...] = pair_ref[...]
-    live = live_ref[...].astype(f32)
-    rows_ref[0:1] = jnp.concatenate([live, jnp.zeros((1, LANES - live.shape[1]), f32)], axis=1)
-    rows_ref[1:2] = out_gain_ref[...]
-    rows_ref[2:3] = att_gain_ref[...]
+    lanes_ref[...] = live_lanes(live_ref)
     hidden = w_ref.shape[2]
     own = hidden // devices
     normed = norm_last(pair_ref[...], gain_ref[...]).astype(bf16)
@@ -215,7 +215,7 @@
 
 
 def triangle_kernel(
-    rows_here, cols_here, vectors_ref, lr_ref, sum_ref, left_scratch, right_scratch, sum_scratch
+    rows_here, cols_here, live_ref, lr_ref, sum_ref, left_scratch, right_scratch, sum_scratch
 ):
     _, panels_in, own, _ = lr_ref.shape
     residues = left_scratch.shape[0] // own
@@ -235,7 +235,7 @@
                     moved = segment(parts[c], start, c * cols_here)
                     line = jnp.where(lane < c * cols_here, line, moved)
                 scratch[pl.ds((r * rows_here + i) * own, own), :] = line
-    live_wide = vectors_ref[0:1]
+    live_wide = live_ref[...]
     live_square = jnp.broadcast_to(live_wide, (LANES, LANES))
     both = live_square * jnp.transpose(live_square)
     both = both[:residues]
@@ -267,7 +267,8 @@
     pair_ref,
     normed_ref,
     sum_ref,
-    vectors_ref,
+    out_gain_ref,
+    att_gain_ref,
     out_w_ref,
     gate_w_ref,
     bias_w_ref,
@@ -278,7 +279,7 @@
     devices, tiles, own, _ = sum_ref.shape
     cells, _ = pair_ref.shape
     hidden = devices * own
-    gain_col = jnp.transpose(jnp.broadcast_to(vectors_ref[1:2], (LANES, hidden)))
+    gain_col = jnp.transpose(jnp.broadcast_to(out_gain_ref[...], (LANES, hidden)))
     gate = sigmoid(dot_nn(normed_ref[...], gate_w_ref[...]))
     bias_w = bias_w_ref[...]
     hidden_rows = []
@@ -292,7 +293,7 @@
     hidden_rows = jnp.concatenate(hidden_rows, axis=0)[:cells]
     mid = pair_ref[...] + gate * dot_nn(hidden_rows, out_w_ref[...])
     mid_ref[...] = mid
-    att = norm_last(mid, vectors_ref[2:3]).astype(bf16)
+    att = norm_last(mid, att_gain_ref[...]).astype(bf16)
     att_ref[...] = att
     bias_ref[0] = dot_nt(bias_w, att).astype(bf16)
 
@@ -361,7 +362,7 @@
 
 def scores_kernel(
     codes,
-    vectors_ref,
+    live_ref,
     fetched_ref,
     q_ref,
     k_ref,
@@ -396,7 +397,7 @@
         scores_ref[i] = dot_nt(q_heads, in_order(k_ref[i], k_far[i]))
         v_all_ref[i] = in_order(v_ref[i], v_far[i])
     lane_row = lax.broadcasted_iota(jnp.int32, (1, LANES), 1)
-    live = vectors_ref[0:1]
+    live = live_ref[...]
     swapped = jnp.where(
         lane_row < cols_here,
         pltpu.roll(live, LANES - cols_here, 1),
@@ -483,12 +484,12 @@
     flat = pair.reshape(cells, chan)
     live = residue_mask.reshape(1, residues)
 
-    lr, normed, vectors, kept = pl.pallas_call(
+    lr, normed, lanes, kept = pl.pallas_call(
         functools.partial(factors_kernel, devices),
         out_shape=(
             pltpu.VMEM((devices, lr_panels, own, LANES), bf16),
             pltpu.VMEM((cells, chan), bf16),
-            pltpu.VMEM((8, LANES), f32),
+            pltpu.VMEM((1, LANES), f32),
             pltpu.VMEM((cells, chan), f32),
         ),
         scratch_shapes=[pltpu.VMEM((chan * tri_in_weight.shape[1], hidden), f32)],
@@ -502,8 +503,6 @@
                 tri_norm_gain.reshape(1, chan),
                 tri_in_weight,
                 live,
-                tri_out_norm_gain.reshape(1, hidden),
-                att_norm_gain.reshape(1, chan),
             ),
         )
     )
@@ -514,7 +513,7 @@
         scratch_shapes=[pltpu.VMEM((residues * own, LANES), f32) for _ in range(3)],
         compiler_params=kernel_params,
         name="triangle",
-    )(near(vectors), near(lr))
+    )(near(lanes), near(lr))
     sums = lax.all_to_all(sums, group, 0, 0, tiled=True)
     shape = (rows_here, cols_here, chan)
     chunks = math.gcd(rows_here, 2)
@@ -534,7 +533,8 @@
                 kept,
                 normed,
                 sums,
-                vectors,
+                tri_out_norm_gain.reshape(1, hidden),
+                att_norm_gain.reshape(1, chan),
                 tri_out_weight,
                 tri_gate_weight,
                 att_bias_weight.T,
@@ -578,7 +578,7 @@
         scratch_shapes=[pltpu.VMEM((cols_here * heads, LANES), f32)],
         compiler_params=kernel_params,
         name="scores",
-    )(*map(near, (vectors, fetched, queries, keys, far, values, kv_weight)))
+    )(*map(near, (lanes, fetched, queries, keys, far, values, kv_weight)))
     return pl.pallas_call(
         functools.partial(attention_kernel, codes),
         out_shape=jax.ShapeDtypeStruct(shape, f32),

time: 41.7 us -> 41.8 us (level)
  no operation moved by 1% of the time
where the time goes in v9:
time: 41.8 us; the launch traced here: 41.6 us
  blocking collectives  26.9 us (64%)
  starting transfers between devices  7.39 us (18%)
  Pallas kernels  5.45 us (13%)
  waiting for transfers between devices  1.63 us (4%)
    all_to_all x1, blocking collectives, body_channels(): lr = lax.all_to_all(lr, group, 0, 0, tiled=True)  16 us
    all_to_all x1, blocking collectives, body_channels(): sums = lax.all_to_all(sums, group, 0, 0, tiled=True)  10.9 us
    ppermute x2, starting transfers between devices, swap(): return lax.ppermute(v, 'row', [(r, r ^ 1) for r in range(rows)])  4.13 us
    ppermute x2, starting transfers between devices, body_channels(): fetched.append(lax.ppermute(bias, group, trips[p]))  2.97 us
    pallas_call x1, Pallas kernels, body_channels(): pl.pallas_call(functools.partial(factors_kernel, devices), out_shape=(plt...  1.72 us
    pallas_call x1, Pallas kernels, body_channels(): pl.pallas_call(functools.partial(attention_kernel, codes), out_shape=jax....  1.6 us
  transfers between devices with their start and end apart: 5, of which 2 were waited for; matrix products, arithmetic and copies ran while one was open for 0% of the time, Pallas kernels for 2%

profile of v9, /device:TPU:9, one launch (start us, length us, event | category | flops | bytes accessed | tf_op | source)
XLA Modules:
  0.0 41.6 jit_solution(1301799910212889330)
XLA Ops:
  0.0 0.0 copy-start.5
  0.0 0.0 copy-start.6
  0.0 0.0 copy-start.4
  0.0 0.0 copy-start.3
  0.0 0.0 copy-start.2
  0.0 0.0 copy-start
  0.0 1.7 %factors.1 = (bf16[16,9,8,128]{3,2,1,0:T(8,128)(2,1)S(1)}, bf16[576,128]{1,0:T(8,128)(2,1)S(1)}, f32[1,128]{1,0:T(1,128)S(1)}, f32[576,128]{1,0:T(8,128)S(1)}) custom-call(f32[576,128]{1,0:T(8,128)} %bitcast.14, f32[1,128]{1,0:T(1,128)} %bitcast.15, bf16[128,4,128]{2,1,0:T(4,128)(2,1)} %w_ref.2, s32[1,96]{1,0:T(1,128)} %bitcast.16), custom_call_target="tpu_custom_call" | custom-call | tf_op jit(solution)/shard_map/factors/pallas_call | solution.py:487
  1.8 16.0 %all_to_all.10.lr_ref = bf16[16,9,8,128]{3,2,1,0:T(8,128)(2,1)S(1)} all-to-all(bf16[16,9,8,128]{3,2,1,0:T(8,128)(2,1)S(1)} %get-tuple-element.23), channel_id=1, replica_groups=mesh['parts'=2,'row'=8,'col'=2,'sub'=1] {'row','col','sub'}, dimensions={0} | all-to-all | bytes 589824 | tf_op jit(solution)/shard_map/all_to_all | solution.py:509
  17.8 0.0 copy-start.1
  17.8 0.7 %triangle.1 = bf16[16,5,8,128]{3,2,1,0:T(8,128)(2,1)S(1)} custom-call(f32[1,128]{1,0:T(1,128)S(1)} %get-tuple-element.20.live_ref, bf16[16,9,8,128]{3,2,1,0:T(8,128)(2,1)S(1)} %all_to_all.10.lr_ref), custom_call_target="tpu_custom_call" | custom-call | tf_op jit(solution)/shard_map/triangle/pallas_call | solution.py:510
  18.4 10.9 %all_to_all.11.sum_ref = bf16[16,5,8,128]{3,2,1,0:T(8,128)(2,1)S(1)} all-to-all(bf16[16,5,8,128]{3,2,1,0:T(8,128)(2,1)S(1)} %triangle.1), channel_id=1, replica_groups=mesh['parts'=2,'row'=8,'col'=2,'sub'=1] {'row','col','sub'}, dimensions={0} | all-to-all | bytes 327680 | tf_op jit(solution)/shard_map/all_to_all | solution.py:517
  29.4 0.0 copy-done.5
  29.4 0.0 copy-done.6
  29.4 0.0 copy-done.4
  29.4 0.0 copy-done.3
  29.4 0.0 copy-done.2
  29.4 0.6 %middle.1 = (f32[576,128]{1,0:T(8,128)S(1)}, bf16[576,128]{1,0:T(8,128)(2,1)S(1)}, bf16[1,4,576]{2,1,0:T(4,128)(2,1)S(1)}) custom-call(f32[576,128]{1,0:T(8,128)S(1)} %get-tuple-element.21.pair_ref, bf16[576,128]{1,0:T(8,128)(2,1)S(1)} %get-tuple-element.22.normed_ref, bf16[16,5,8,128]{3,2,1,0:T(8,128)(2,1)S(1)} %all_to_all.11.sum_ref, ...), custom_call_target="tpu_custom_call" | custom-call | tf_op jit(solution)/shard_map/middle/pallas_call | solution.py:520
  30.1 0.4 collective-permute-start
  30.5 0.8 %collective-permute-done = bf16[1,4,576]{2,1,0:T(4,128)(2,1)S(1)} collective-permute-done((bf16[1,4,576]{2,1,0:T(4,128)(2,1)S(1)}, bf16[1,4,576]{2,1,0:T(4,128)(2,1)S(1)}, u32[]{:S(2)}, u32[]{:S(2)}) %collective-permute-start) | collective-permute-done | bytes 4640 | tf_op jit(solution)/shard_map/ppermute | solution.py:547
  31.3 1.5 %collective-permute-start.1 = (bf16[2,4,576]{2,1,0:T(4,128)(2,1)S(1)}, bf16[2,4,576]{2,1,0:T(4,128)(2,1)S(1)}, u32[]{:S(2)}, u32[]{:S(2)}) collective-permute-start(bf16[2,4,576]{2,1,0:T(4,128)(2,1)S(1)} %constant_dynamic-update-slice_fusion), channel_id=1, source_target_pairs={{2,0},{0,6},{4,8},{6,12},{3,2},{1,10},{7,4},{5,14},{10,3},{8,7},{1... | collective-permute-start | bytes 27656 | tf_op jit(solution)/shard_map/ppermute | solution.py:554
  32.8 0.3 collective-permute-start.3
  33.0 1.5 %collective-permute-start.2 = (bf16[2,4,576]{2,1,0:T(4,128)(2,1)S(1)}, bf16[2,4,576]{2,1,0:T(4,128)(2,1)S(1)}, u32[]{:S(2)}, u32[]{:S(2)}) collective-permute-start(bf16[2,4,576]{2,1,0:T(4,128)(2,1)S(1)} %constant_dynamic-update-slice_fusion), channel_id=1, source_target_pairs={{0,8},{2,12},{6,0},{4,6},{1,4},{3,14},{7,2},{5,10},{8,11},{10,15},... | collective-permute-start | bytes 27656 | tf_op jit(solution)/shard_map/ppermute | solution.py:554
  34.6 0.0 collective-permute-done.1
  34.6 0.8 %collective-permute-done.2 = bf16[2,4,576]{2,1,0:T(4,128)(2,1)S(1)} collective-permute-done((bf16[2,4,576]{2,1,0:T(4,128)(2,1)S(1)}, bf16[2,4,576]{2,1,0:T(4,128)(2,1)S(1)}, u32[]{:S(2)}, u32[]{:S(2)}) %collective-permute-start.2) | collective-permute-done | bytes 9248 | tf_op jit(solution)/shard_map/ppermute | solution.py:554
  35.4 3.7 %collective-permute-start.4 = (bf16[4,4,576]{2,1,0:T(4,128)(2,1)S(1)}, bf16[4,4,576]{2,1,0:T(4,128)(2,1)S(1)}, u32[]{:S(2)}, u32[]{:S(2)}) collective-permute-start(bf16[4,4,576]{2,1,0:T(4,128)(2,1)S(1)} %constant_dynamic-update-slice_fusion.2.fetched_ref), channel_id=1, source_target_pairs={{0,2},{2,0},{4,6},{6,4},{8,10},{10,8},{12,14},{14,12},{1,3},{3,1},... | collective-permute-start | bytes 55304 | tf_op jit(solution)/shard_map/ppermute | solution.py:547
  39.1 0.0 copy-done
  39.1 0.3 own.1
  39.5 0.0 collective-permute-done.3.far_ref
  39.5 0.5 %scores.1 = (f32[12,192,96]{2,1,0:T(8,128)S(1)}, bf16[12,96,128]{2,1,0:T(8,128)(2,1)S(1)}, f32[192,128]{1,0:T(8,128)S(1)}) custom-call(f32[1,128]{1,0:T(1,128)S(1)} %get-tuple-element.20.live_ref, bf16[4,4,576]{2,1,0:T(4,128)(2,1)S(1)} %constant_dynamic-update-slice_fusion.2.fetched_ref, bf16[12,48,128]{2,1,0:T(8,128)(2,1)S(1)} %get-tuple-element.26.q_ref, ...), custom_call_target="tpu_custom_call" | custom-call | tf_op jit(solution)/shard_map/scores/pallas_call | solution.py:571
  39.9 0.0 collective-permute-done.4.swapped_ref
  40.0 0.0 copy-done.1
  40.0 1.6 %attention.1 = f32[12,48,128]{2,1,0:T(8,128)} custom-call(f32[192,128]{1,0:T(8,128)S(1)} %get-tuple-element.30.bias_ref, bf16[4,4,576]{2,1,0:T(4,128)(2,1)S(1)} %collective-permute-done.4.swapped_ref, f32[12,192,96]{2,1,0:T(8,128)S(1)} %get-tuple-element.31.scores_ref, bf16[12,96,128]{2,1,0:T(8,128)(2,1)S(1)} %get-tuple-element.32.v_all_ref, ...), custom_call_target="tpu_custom_call" | custom-call | tf_op jit(solution)/shard_map/attention/pallas_call | solution.py:582
  (4 shorter events, 0.0 us)
Async XLA Ops:
  0.0 29.4 %copy-start.5 = (f32[128]{0:T(128)S(1)}, f32[128]{0:T(128)}, u32[]{:S(2)}) copy-start(f32[128]{0:T(128)} %param.16) | copy-start | bytes 1540
  0.0 29.4 %copy-start.6 = (f32[128]{0:T(128)S(1)}, f32[128]{0:T(128)}, u32[]{:S(2)}) copy-start(f32[128]{0:T(128)} %param.18) | copy-start | bytes 1540
  0.0 29.4 %copy-start.4 = (bf16[128,4]{0,1:T(4,128)(2,1)S(1)}, bf16[128,4]{0,1:T(4,128)(2,1)}, u32[]{:S(2)}) copy-start(bf16[128,4]{0,1:T(4,128)(2,1)} %param.20) | copy-start | bytes 3076
  0.0 29.4 %copy-start.3 = (bf16[128,128]{1,0:T(8,128)(2,1)S(1)}, bf16[128,128]{1,0:T(8,128)(2,1)}, u32[]{:S(2)}) copy-start(bf16[128,128]{1,0:T(8,128)(2,1)} %gate_w_ref.1) | copy-start | bytes 98308
  0.0 29.4 %copy-start.2 = (bf16[128,128]{1,0:T(8,128)(2,1)S(1)}, bf16[128,128]{1,0:T(8,128)(2,1)}, u32[]{:S(2)}) copy-start(bf16[128,128]{1,0:T(8,128)(2,1)} %out_w_ref.2) | copy-start | bytes 98308
  0.0 39.1 %copy-start = (bf16[128,4,128]{2,1,0:T(4,128)(2,1)S(1)}, bf16[128,4,128]{2,1,0:T(4,128)(2,1)}, u32[]{:S(2)}) copy-start(bf16[128,4,128]{2,1,0:T(4,128)(2,1)} %w_ref.3) | copy-start | bytes 393220
  17.8 22.2 %copy-start.1 = (bf16[128,128]{1,0:T(8,128)(2,1)S(1)}, bf16[128,128]{1,0:T(8,128)(2,1)}, u32[]{:S(2)}) copy-start(bf16[128,128]{1,0:T(8,128)(2,1)} %out_w_ref.3) | copy-start | bytes 98308
  30.1 1.2 %collective-permute-start = (bf16[1,4,576]{2,1,0:T(4,128)(2,1)S(1)}, bf16[1,4,576]{2,1,0:T(4,128)(2,1)S(1)}, u32[]{:S(2)}, u32[]{:S(2)}) collective-permute-start(bf16[1,4,576]{2,1,0:T(4,128)(2,1)S(1)} %get-tuple-element.24), channel_id=1, source_target_pairs={{0,2},{2,0},{4,6},{6,4},{8,10},{10,8},{12,14},{14,12},{1,3},{3,1},... | collective-permute-start | bytes 13832 | tf_op jit(solution)/shard_map/ppermute | solution.py:547
  31.3 3.3 %collective-permute-start.1 = (bf16[2,4,576]{2,1,0:T(4,128)(2,1)S(1)}, bf16[2,4,576]{2,1,0:T(4,128)(2,1)S(1)}, u32[]{:S(2)}, u32[]{:S(2)}) collective-permute-start(bf16[2,4,576]{2,1,0:T(4,128)(2,1)S(1)} %constant_dynamic-update-slice_fusion), channel_id=1, source_target_pairs={{2,0},{0,6},{4,8},{6,12},{3,2},{1,10},{7,4},{5,14},{10,3},{8,7},{1... | collective-permute-start | bytes 27656 | tf_op jit(solution)/shard_map/ppermute | solution.py:554
  32.8 6.7 %collective-permute-start.3 = (bf16[12,48,128]{2,1,0:T(8,128)(2,1)S(1)}, bf16[12,48,128]{2,1,0:T(8,128)(2,1)S(1)}, u32[]{:S(2)}, u32[]{:S(2)}) collective-permute-start(bf16[12,48,128]{2,1,0:T(8,128)(2,1)S(1)} %bitcast.9), channel_id=1, source_target_pairs={{0,1},{1,0},{2,3},{3,2},{4,5},{5,4},{6,7},{7,6},{8,9},{9,8},{10,11... | collective-permute-start | bytes 442376 | tf_op jit(solution)/shard_map/ppermute | solution.py:555
  33.0 2.3 %collective-permute-start.2 = (bf16[2,4,576]{2,1,0:T(4,128)(2,1)S(1)}, bf16[2,4,576]{2,1,0:T(4,128)(2,1)S(1)}, u32[]{:S(2)}, u32[]{:S(2)}) collective-permute-start(bf16[2,4,576]{2,1,0:T(4,128)(2,1)S(1)} %constant_dynamic-update-slice_fusion), channel_id=1, source_target_pairs={{0,8},{2,12},{6,0},{4,6},{1,4},{3,14},{7,2},{5,10},{8,11},{10,15},... | collective-permute-start | bytes 27656 | tf_op jit(solution)/shard_map/ppermute | solution.py:554
  35.4 4.6 %collective-permute-start.4 = (bf16[4,4,576]{2,1,0:T(4,128)(2,1)S(1)}, bf16[4,4,576]{2,1,0:T(4,128)(2,1)S(1)}, u32[]{:S(2)}, u32[]{:S(2)}) collective-permute-start(bf16[4,4,576]{2,1,0:T(4,128)(2,1)S(1)} %constant_dynamic-update-slice_fusion.2.fetched_ref), channel_id=1, source_target_pairs={{0,2},{2,0},{4,6},{6,4},{8,10},{10,8},{12,14},{14,12},{1,3},{3,1},... | collective-permute-start | bytes 55304 | tf_op jit(solution)/shard_map/ppermute | solution.py:547
